TPU v7x, 256 devices: a 2x2x32 block of a 4x8x32 slice. The times are simulated.
256 devices in a mesh: runs: 4 (over y, x), gx: 64 (over z, core).
Axes of the slice: x: 2, y: 2, z: 32, core: 2. Of those that a mesh axis runs over, the one named last changes fastest.
The devices are a block of a 4x8x32 slice.
Arguments:
- potential: float32 [512, 512, 512], P(('runs', 'gx')), parts along dimension 0, may hold values from -3 to 3
Outputs:
- second_potential: float32 [512, 512, 512], P(('runs', 'gx')), parts along dimension 0
- norms: float32 [8], P('runs'), parts along dimension 0
There are 4 independent parts, one for each index of `runs`. A program takes and returns all parts, laid end to end along the dimension named above; each array names one. Nothing has to cross between parts.
All inputs are finite; a program needn't handle non-finite values.
Results may differ from a plain program's by a relative error of at most 0.00015.
Values sent between devices are 32-bit elements; how exact they have to be, the bound alone decides.
No kernel may reach another device: no remote copies, remote signals or barrier semaphores. Data moves between devices by JAX's collectives and lax.ppermute only.
A program may use at most 256 MiB of HBM per device.

v0:
```python
import jax
import jax.numpy as jnp
from jax import lax
from jax.sharding import PartitionSpec as P

LEVELS = 2
COARSE = 4
CYCLES = 2


RELAX = 0.8


def with_halo(cells, sides, width):
    for axis, dim in sides:
        count = lax.axis_size(axis)
        head = lax.slice_in_dim(cells, 0, width, axis=dim)
        tail = lax.slice_in_dim(cells, cells.shape[dim] - width, cells.shape[dim], axis=dim)
        cells = jnp.concatenate(
            [
                lax.ppermute(tail, axis, [(i, (i + 1) % count) for i in range(count)]),
                cells,
                lax.ppermute(head, axis, [((i + 1) % count, i) for i in range(count)]),
            ],
            axis=dim,
        )
    return cells


def from_everyone(x, axis):
    length = lax.axis_size(axis)
    return lax.all_to_all(jnp.broadcast_to(x[None], (length, *x.shape)), axis, 0, 0, tiled=True)


def taken_together(x, axis):
    return from_everyone(x, axis).sum(axis=0)


def shifted(field, offset, axis):
    return jnp.roll(field, -offset, axis)


def source_term(padded):
    center = padded[1:-1]
    upper = padded[2:]
    lower = padded[:-2]
    curve_xx = upper + lower - 2.0 * center
    curve_yy = shifted(center, 1, 1) + shifted(center, -1, 1) - 2.0 * center
    curve_zz = shifted(center, 1, 2) + shifted(center, -1, 2) - 2.0 * center
    cross_xy = (
        shifted(upper, 1, 1) - shifted(upper, -1, 1) - shifted(lower, 1, 1) + shifted(lower, -1, 1)
    ) * 0.25
    cross_xz = (
        shifted(upper, 1, 2) - shifted(upper, -1, 2) - shifted(lower, 1, 2) + shifted(lower, -1, 2)
    ) * 0.25
    plus_y = shifted(center, 1, 1)
    minus_y = shifted(center, -1, 1)
    cross_yz = (
        shifted(plus_y, 1, 2)
        - shifted(plus_y, -1, 2)
        - shifted(minus_y, 1, 2)
        + shifted(minus_y, -1, 2)
    ) * 0.25
    return (
        curve_xx * curve_yy
        - cross_xy * cross_xy
        + curve_xx * curve_zz
        - cross_xz * cross_xz
        + curve_yy * curve_zz
        - cross_yz * cross_yz
    )


def operator(padded, spacing):
    center = padded[1:-1]
    beside_all = padded[2:] + padded[:-2]
    beside_all = beside_all + shifted(center, 1, 1) + shifted(center, -1, 1)
    beside_all = beside_all + shifted(center, 1, 2) + shifted(center, -1, 2)
    return (6.0 * center - beside_all) / spacing


def relax(padded, forcing, spacing):
    return padded[1:-1] + RELAX * spacing / 6.0 * (forcing - operator(padded, spacing))


def restrict(field):
    planes, rows, cols = field.shape
    blocks = field.reshape(planes // 2, 2, rows // 2, 2, cols // 2, 2)
    return jnp.mean(blocks, axis=(1, 3, 5))


def prolong(field):
    return jnp.repeat(jnp.repeat(jnp.repeat(field, 2, 0), 2, 1), 2, 2)


def smooth(field, forcing, spacing):
    padded = with_halo(field, (("gx", 0),), 1)
    field = relax(padded, forcing, spacing)
    return field


def residual_of(field, forcing, spacing):
    padded = with_halo(field, (("gx", 0),), 1)
    return forcing - operator(padded, spacing)


def report_norm(residue, cell_count):
    squares = taken_together(jnp.sum(residue * residue), "gx")
    return jnp.sqrt(squares / cell_count)


def coarsest_solve(forcing, spacing):
    field = jnp.zeros_like(forcing)
    for sweep_index in range(COARSE):
        padded = with_halo(field, (("gx", 0),), 1)
        field = relax(padded, forcing, spacing)
    return field


def vcycle(field, forcing, level):
    spacing = float(4**level)
    if level == LEVELS - 1:
        return coarsest_solve(forcing, spacing)
    field = smooth(field, forcing, spacing)
    residue = residual_of(field, forcing, spacing)
    coarse_rhs = restrict(residue)
    correction = vcycle(jnp.zeros_like(coarse_rhs), coarse_rhs, level + 1)
    field = field + prolong(correction)
    return smooth(field, forcing, spacing)


def on_device(potential):
    devices_x = lax.axis_size("gx")
    padded = with_halo(potential, (("gx", 0),), 1)
    source = source_term(padded)
    cell_count = float(source.size * devices_x)
    total = taken_together(jnp.sum(source), "gx")
    forcing = -(source - total / cell_count)
    field = jnp.zeros_like(forcing)
    results = []
    for cycle_index in range(CYCLES):
        field = vcycle(field, forcing, 0)
        residue = residual_of(field, forcing, 1.0)
        results.append(report_norm(residue, cell_count))
    return (field, jnp.stack(results))


def solution(mesh):
    in_specs = (P(("runs", "gx"), None, None),)
    out_specs = (P(("runs", "gx"), None, None), P("runs"))
    return jax.shard_map(
        on_device, mesh=mesh, in_specs=in_specs, out_specs=out_specs, check_vma=False
    )
```

profile of v0, /device:TPU:37, one launch (start us, length us, event | category | flops | bytes accessed | tf_op | source)
XLA Modules:
  0.0 514.5 jit_solution(14504625592592836844)
XLA Ops:
  1.8 20.4 %collective-permute-start.2 = (f32[1,512,512]{2,1,0:T(8,128)}, f32[1,512,512]{2,1,0:T(8,128)}, u32[]{:S(2)}, u32[]{:S(2)}) collective-permute-start(f32[1,512,512]{2,1,0:T(8,128)} %broadcast.128), channel_id=1, source_target_pairs={{1,0},{2,1},{3,2},{4,3},{5,4},{6,5},{7,6},{8,7},{9,8},{10,9},{11,1... | collective-permute-start | bytes 3145736 | tf_op jit(solution)/shard_map/ppermute | solution.py:23
  24.0 3.6 collective-permute-start
  32.2 13.2 %collective-permute-done.1 = f32[1,512,512]{2,1,0:T(8,128)S(1)} collective-permute-done((f32[1,512,512]{2,1,0:T(8,128)S(1)}, f32[1,512,512]{2,1,0:T(8,128)S(1)}, u32[]{:S(2)}, u32[]{:S(2)}) %collective-permute-start.1) | collective-permute-done | bytes 1048608 | tf_op jit(solution)/shard_map/ppermute | solution.py:21
  58.0 10.8 %fusion.138 = (f32[]{:T(128)}, f32[2,512,512]{2,1,0:T(8,128)S(1)}) fusion(f32[2,512,511]{2,1,0:T(8,128)S(1)} %get-tuple-element.31, f32[2,512,1]{2,1,0:T(8,128)S(1)} %get-tuple-element.33, f32[2,512,1]{2,1,0:T(8,128)S(1)} %get-tuple-element.32, f32[2,512,511]{2,1,0:T(8,128)S(1)} %get-tuple-element.30, f32[2,512,511]{2,1,0:T(8,128)S(1)} %get-tuple-element.154, ...), kind=kLoop, calls=%fused_computation.189 | loop fusion | flops 24641536 | bytes 41943044 | tf_op jit(solution)/shard_map/reduce_sum | solution.py:137
  70.1 18.2 %all-to-all-start = ((f32[64,1,1]{2,1,0:T(1,128)}), f32[64,1,1]{2,1,0:T(1,128)S(1)}, u32[]{:S(2)}, u32[]{:S(2)}) async-start(f32[64,1,1]{2,1,0:T(1,128)} %broadcast_in_dim.44), calls=%async_computation | async-start | bytes 65536 | tf_op jit(solution)/shard_map/all_to_all | solution.py:32
  90.8 19.6 %all-to-all-done = f32[64,1,1]{2,1,0:T(1,128)S(1)} async-done(((f32[64,1,1]{2,1,0:T(1,128)}), f32[64,1,1]{2,1,0:T(1,128)S(1)}, u32[]{:S(2)}, u32[]{:S(2)}) %all-to-all-start) | async-done | bytes 288 | tf_op jit(solution)/shard_map/all_to_all | solution.py:32
  117.2 11.3 %collective-permute-done.4 = f32[1,512,512]{2,1,0:T(8,128)S(1)} collective-permute-done((f32[1,512,512]{2,1,0:T(8,128)S(1)}, f32[1,512,512]{2,1,0:T(8,128)S(1)}, u32[]{:S(2)}, u32[]{:S(2)}) %collective-permute-start.4) | collective-permute-done | bytes 1048608 | tf_op jit(solution)/shard_map/ppermute | solution.py:23
  131.2 68.4 %reduce_sum.89 = f32[256,2,256,2]{3,2,1,0:T(8,128)} reshape(f32[512,512]{1,0:T(8,128)S(1)} %fusion.59) | data formatting | bytes 2097152 | tf_op jit(solution)/shard_map/reduce_sum | solution.py:89
  199.6 21.0 %reduce_sum.90 = f32[256,256]{1,0:T(8,128)S(1)} reduce(f32[256,2,256,2]{3,2,1,0:T(8,128)} %reduce_sum.89, f32[]{:T(128)} %constant.41.clone.1), dimensions={1,3}, to_apply=%region_3.4 | reduce | flops 196608 | bytes 1310724 | tf_op jit(solution)/shard_map/reduce_sum | solution.py:89
  224.9 3.9 collective-permute-done.8
  235.9 3.8 collective-permute-start.12
  251.6 3.8 collective-permute-start.14
  256.9 10.0 %collective-permute-done.14 = f32[1,512,512]{2,1,0:T(8,128)S(1)} collective-permute-done((f32[1,512,512]{2,1,0:T(8,128)S(1)}, f32[1,512,512]{2,1,0:T(8,128)S(1)}, u32[]{:S(2)}, u32[]{:S(2)}) %collective-permute-start.14) | collective-permute-done | bytes 1048608 | tf_op jit(solution)/shard_map/ppermute | solution.py:23
  270.3 3.8 collective-permute-start.16
  275.6 10.0 %collective-permute-done.16 = f32[1,512,512]{2,1,0:T(8,128)S(1)} collective-permute-done((f32[1,512,512]{2,1,0:T(8,128)S(1)}, f32[1,512,512]{2,1,0:T(8,128)S(1)}, u32[]{:S(2)}, u32[]{:S(2)}) %collective-permute-start.16) | collective-permute-done | bytes 1048608 | tf_op jit(solution)/shard_map/ppermute | solution.py:23
  285.9 3.1 multiply_reduce_fusion
  291.0 3.8 collective-permute-start.18
  296.0 6.5 %all-to-all-start.1 = ((f32[64,1,1]{2,1,0:T(1,128)}), f32[64,1,1]{2,1,0:T(1,128)S(1)}, u32[]{:S(2)}, u32[]{:S(2)}) async-start(f32[64,1,1]{2,1,0:T(1,128)} %broadcast_in_dim.55), calls=%async_computation.1 | async-start | bytes 65536 | tf_op jit(solution)/shard_map/all_to_all | solution.py:32
  303.9 3.3 collective-permute-done.18
  308.2 3.9 fusion.35
  312.1 68.4 %reduce_sum.92 = f32[256,2,256,2]{3,2,1,0:T(8,128)} reshape(f32[512,512]{1,0:T(8,128)S(1)} %fusion.35) | data formatting | bytes 2097152 | tf_op jit(solution)/shard_map/reduce_sum | solution.py:89
  380.5 21.0 %reduce_sum.93 = f32[256,256]{1,0:T(8,128)S(1)} reduce(f32[256,2,256,2]{3,2,1,0:T(8,128)} %reduce_sum.92, f32[]{:T(128)} %constant.41.clone.1), dimensions={1,3}, to_apply=%region_5.6 | reduce | flops 196608 | bytes 1310724 | tf_op jit(solution)/shard_map/reduce_sum | solution.py:89
  401.7 3.4 collective-permute-start.20
  408.8 5.0 collective-permute-start.22
  417.5 3.8 collective-permute-start.24
  431.6 3.8 collective-permute-start.26
  436.8 10.0 %collective-permute-done.26 = f32[1,512,512]{2,1,0:T(8,128)S(1)} collective-permute-done((f32[1,512,512]{2,1,0:T(8,128)S(1)}, f32[1,512,512]{2,1,0:T(8,128)S(1)}, u32[]{:S(2)}, u32[]{:S(2)}) %collective-permute-start.26) | collective-permute-done | bytes 1048608 | tf_op jit(solution)/shard_map/ppermute | solution.py:23
  450.1 3.8 collective-permute-start.28
  455.4 10.0 %collective-permute-done.28 = f32[1,512,512]{2,1,0:T(8,128)S(1)} collective-permute-done((f32[1,512,512]{2,1,0:T(8,128)S(1)}, f32[1,512,512]{2,1,0:T(8,128)S(1)}, u32[]{:S(2)}, u32[]{:S(2)}) %collective-permute-start.28) | collective-permute-done | bytes 1048608 | tf_op jit(solution)/shard_map/ppermute | solution.py:23
  465.7 3.1 fusion.79
  470.1 19.8 %all-to-all-start.2 = ((f32[64,1,1]{2,1,0:T(1,128)}), f32[64,1,1]{2,1,0:T(1,128)S(1)}, u32[]{:S(2)}, u32[]{:S(2)}) async-start(f32[64,1,1]{2,1,0:T(1,128)} %broadcast_in_dim.56), calls=%async_computation.2 | async-start | bytes 65536 | tf_op jit(solution)/shard_map/all_to_all | solution.py:32
  491.2 21.1 %all-to-all-done.2 = f32[64,1,1]{2,1,0:T(1,128)S(1)} async-done(((f32[64,1,1]{2,1,0:T(1,128)}), f32[64,1,1]{2,1,0:T(1,128)S(1)}, u32[]{:S(2)}, u32[]{:S(2)}) %all-to-all-start.2) | async-done | bytes 288 | tf_op jit(solution)/shard_map/all_to_all | solution.py:32
  (170 shorter events, 95.0 us)
Async XLA Ops:
  1.8 110.0 %collective-permute-start.2 = (f32[1,512,512]{2,1,0:T(8,128)}, f32[1,512,512]{2,1,0:T(8,128)}, u32[]{:S(2)}, u32[]{:S(2)}) collective-permute-start(f32[1,512,512]{2,1,0:T(8,128)} %broadcast.128), channel_id=1, source_target_pairs={{1,0},{2,1},{3,2},{4,3},{5,4},{6,5},{7,6},{8,7},{9,8},{10,9},{11,1... | collective-permute-start | bytes 3145736 | tf_op jit(solution)/shard_map/ppermute | solution.py:23
  22.2 89.6 %collective-permute-start.3 = (f32[1,512,512]{2,1,0:T(8,128)}, f32[1,512,512]{2,1,0:T(8,128)}, u32[]{:S(2)}, u32[]{:S(2)}) collective-permute-start(f32[1,512,512]{2,1,0:T(8,128)} %broadcast.128), channel_id=1, source_target_pairs={{0,1},{1,2},{2,3},{3,4},{4,5},{5,6},{6,7},{7,8},{8,9},{9,10},{10,1... | collective-permute-start | bytes 3145736 | tf_op jit(solution)/shard_map/ppermute | solution.py:21
  23.9 21.5 %collective-permute-start.1 = (f32[1,512,512]{2,1,0:T(8,128)S(1)}, f32[1,512,512]{2,1,0:T(8,128)S(1)}, u32[]{:S(2)}, u32[]{:S(2)}) collective-permute-start(f32[1,512,512]{2,1,0:T(8,128)S(1)} %get-tuple-element.99), channel_id=1, source_target_pairs={{0,1},{1,2},{2,3},{3,4},{4,5},{5,6},{6,7},{7,8},{8,9},{9,10},{10,1... | collective-permute-start | bytes 3145736 | tf_op jit(solution)/shard_map/ppermute | solution.py:21
  24.0 22.1 %collective-permute-start = (f32[1,512,512]{2,1,0:T(8,128)S(1)}, f32[1,512,512]{2,1,0:T(8,128)S(1)}, u32[]{:S(2)}, u32[]{:S(2)}) collective-permute-start(f32[1,512,512]{2,1,0:T(8,128)S(1)} %get-tuple-element.98), channel_id=1, source_target_pairs={{1,0},{2,1},{3,2},{4,3},{5,4},{6,5},{7,6},{8,7},{9,8},{10,9},{11,1... | collective-permute-start | bytes 3145736 | tf_op jit(solution)/shard_map/ppermute | solution.py:23
  70.1 40.3 %all-to-all-start = ((f32[64,1,1]{2,1,0:T(1,128)}), f32[64,1,1]{2,1,0:T(1,128)S(1)}, u32[]{:S(2)}, u32[]{:S(2)}) async-start(f32[64,1,1]{2,1,0:T(1,128)} %broadcast_in_dim.44), calls=%async_computation | async-start | bytes 65536 | tf_op jit(solution)/shard_map/all_to_all | solution.py:32
  89.1 131.6 %collective-permute-start.6 = (f32[1,256,256]{2,1,0:T(8,128)}, f32[1,256,256]{2,1,0:T(8,128)S(1)}, u32[]{:S(2)}, u32[]{:S(2)}) collective-permute-start(f32[1,256,256]{2,1,0:T(8,128)} %broadcast.131), channel_id=1, source_target_pairs={{1,0},{2,1},{3,2},{4,3},{5,4},{6,5},{7,6},{8,7},{9,8},{10,9},{11,1... | collective-permute-start | bytes 786440 | tf_op jit(solution)/shard_map/ppermute | solution.py:23
  90.0 131.4 %collective-permute-start.7 = (f32[1,256,256]{2,1,0:T(8,128)}, f32[1,256,256]{2,1,0:T(8,128)}, u32[]{:S(2)}, u32[]{:S(2)}) collective-permute-start(f32[1,256,256]{2,1,0:T(8,128)} %broadcast.131), channel_id=1, source_target_pairs={{0,1},{1,2},{2,3},{3,4},{4,5},{5,6},{6,7},{7,8},{8,9},{9,10},{10,1... | collective-permute-start | bytes 786440 | tf_op jit(solution)/shard_map/ppermute | solution.py:21
  114.0 14.6 %collective-permute-start.4 = (f32[1,512,512]{2,1,0:T(8,128)S(1)}, f32[1,512,512]{2,1,0:T(8,128)S(1)}, u32[]{:S(2)}, u32[]{:S(2)}) collective-permute-start(f32[1,512,512]{2,1,0:T(8,128)S(1)} %get-tuple-element.92), channel_id=1, source_target_pairs={{1,0},{2,1},{3,2},{4,3},{5,4},{6,5},{7,6},{8,7},{9,8},{10,9},{11,1... | collective-permute-start | bytes 3145736 | tf_op jit(solution)/shard_map/ppermute | solution.py:23
  115.0 13.5 %collective-permute-start.5 = (f32[1,512,512]{2,1,0:T(8,128)S(1)}, f32[1,512,512]{2,1,0:T(8,128)S(1)}, u32[]{:S(2)}, u32[]{:S(2)}) collective-permute-start(f32[1,512,512]{2,1,0:T(8,128)S(1)} %get-tuple-element.93), channel_id=1, source_target_pairs={{0,1},{1,2},{2,3},{3,4},{4,5},{5,6},{6,7},{7,8},{8,9},{9,10},{10,1... | collective-permute-start | bytes 3145736 | tf_op jit(solution)/shard_map/ppermute | solution.py:21
  222.7 6.1 %collective-permute-start.8 = (f32[1,256,256]{2,1,0:T(8,128)S(1)}, f32[1,256,256]{2,1,0:T(8,128)S(1)}, u32[]{:S(2)}, u32[]{:S(2)}) collective-permute-start(f32[1,256,256]{2,1,0:T(8,128)S(1)} %get-tuple-element.4), channel_id=1, source_target_pairs={{1,0},{2,1},{3,2},{4,3},{5,4},{6,5},{7,6},{8,7},{9,8},{10,9},{11,1... | collective-permute-start | bytes 786440 | tf_op jit(solution)/shard_map/ppermute | solution.py:23
  224.7 4.1 collective-permute-start.9
  229.2 5.8 %collective-permute-start.10 = (f32[1,256,256]{2,1,0:T(8,128)S(1)}, f32[1,256,256]{2,1,0:T(8,128)S(1)}, u32[]{:S(2)}, u32[]{:S(2)}) collective-permute-start(f32[1,256,256]{2,1,0:T(8,128)S(1)} %fusion.91), channel_id=1, source_target_pairs={{1,0},{2,1},{3,2},{4,3},{5,4},{6,5},{7,6},{8,7},{9,8},{10,9},{11,1... | collective-permute-start | bytes 786440 | tf_op jit(solution)/shard_map/ppermute | solution.py:23
  232.2 3.3 collective-permute-start.11
  235.9 6.6 %collective-permute-start.12 = (f32[1,256,256]{2,1,0:T(8,128)S(1)}, f32[1,256,256]{2,1,0:T(8,128)S(1)}, u32[]{:S(2)}, u32[]{:S(2)}) collective-permute-start(f32[1,256,256]{2,1,0:T(8,128)S(1)} %fusion.99), channel_id=1, source_target_pairs={{1,0},{2,1},{3,2},{4,3},{5,4},{6,5},{7,6},{8,7},{9,8},{10,9},{11,1... | collective-permute-start | bytes 786440 | tf_op jit(solution)/shard_map/ppermute | solution.py:23
  239.7 3.3 collective-permute-start.13
  251.6 15.3 %collective-permute-start.14 = (f32[1,512,512]{2,1,0:T(8,128)S(1)}, f32[1,512,512]{2,1,0:T(8,128)S(1)}, u32[]{:S(2)}, u32[]{:S(2)}) collective-permute-start(f32[1,512,512]{2,1,0:T(8,128)S(1)} %get-tuple-element.82), channel_id=1, source_target_pairs={{1,0},{2,1},{3,2},{4,3},{5,4},{6,5},{7,6},{8,7},{9,8},{10,9},{11,1... | collective-permute-start | bytes 3145736 | tf_op jit(solution)/shard_map/ppermute | solution.py:23
  255.4 11.7 %collective-permute-start.15 = (f32[1,512,512]{2,1,0:T(8,128)S(1)}, f32[1,512,512]{2,1,0:T(8,128)S(1)}, u32[]{:S(2)}, u32[]{:S(2)}) collective-permute-start(f32[1,512,512]{2,1,0:T(8,128)S(1)} %get-tuple-element.83), channel_id=1, source_target_pairs={{0,1},{1,2},{2,3},{3,4},{4,5},{5,6},{6,7},{7,8},{8,9},{9,10},{10,1... | collective-permute-start | bytes 3145736 | tf_op jit(solution)/shard_map/ppermute | solution.py:21
  270.3 15.3 %collective-permute-start.16 = (f32[1,512,512]{2,1,0:T(8,128)S(1)}, f32[1,512,512]{2,1,0:T(8,128)S(1)}, u32[]{:S(2)}, u32[]{:S(2)}) collective-permute-start(f32[1,512,512]{2,1,0:T(8,128)S(1)} %get-tuple-element.64), channel_id=1, source_target_pairs={{1,0},{2,1},{3,2},{4,3},{5,4},{6,5},{7,6},{8,7},{9,8},{10,9},{11,1... | collective-permute-start | bytes 3145736 | tf_op jit(solution)/shard_map/ppermute | solution.py:23
  274.1 11.7 %collective-permute-start.17 = (f32[1,512,512]{2,1,0:T(8,128)S(1)}, f32[1,512,512]{2,1,0:T(8,128)S(1)}, u32[]{:S(2)}, u32[]{:S(2)}) collective-permute-start(f32[1,512,512]{2,1,0:T(8,128)S(1)} %get-tuple-element.65), channel_id=1, source_target_pairs={{0,1},{1,2},{2,3},{3,4},{4,5},{5,6},{6,7},{7,8},{8,9},{9,10},{10,1... | collective-permute-start | bytes 3145736 | tf_op jit(solution)/shard_map/ppermute | solution.py:21
  291.0 16.3 %collective-permute-start.18 = (f32[1,512,512]{2,1,0:T(8,128)}, f32[1,512,512]{2,1,0:T(8,128)S(1)}, u32[]{:S(2)}, u32[]{:S(2)}) collective-permute-start(f32[1,512,512]{2,1,0:T(8,128)} %get-tuple-element.62), channel_id=1, source_target_pairs={{1,0},{2,1},{3,2},{4,3},{5,4},{6,5},{7,6},{8,7},{9,8},{10,9},{11,1... | collective-permute-start | bytes 3145736 | tf_op jit(solution)/shard_map/ppermute | solution.py:23
  294.7 12.7 %collective-permute-start.19 = (f32[1,512,512]{2,1,0:T(8,128)}, f32[1,512,512]{2,1,0:T(8,128)}, u32[]{:S(2)}, u32[]{:S(2)}) collective-permute-start(f32[1,512,512]{2,1,0:T(8,128)} %get-tuple-element.63), channel_id=1, source_target_pairs={{0,1},{1,2},{2,3},{3,4},{4,5},{5,6},{6,7},{7,8},{8,9},{9,10},{10,1... | collective-permute-start | bytes 3145736 | tf_op jit(solution)/shard_map/ppermute | solution.py:21
  296.0 172.8 %all-to-all-start.1 = ((f32[64,1,1]{2,1,0:T(1,128)}), f32[64,1,1]{2,1,0:T(1,128)S(1)}, u32[]{:S(2)}, u32[]{:S(2)}) async-start(f32[64,1,1]{2,1,0:T(1,128)} %broadcast_in_dim.55), calls=%async_computation.1 | async-start | bytes 65536 | tf_op jit(solution)/shard_map/all_to_all | solution.py:32
  401.7 5.8 %collective-permute-start.20 = (f32[1,256,256]{2,1,0:T(8,128)S(1)}, f32[1,256,256]{2,1,0:T(8,128)S(1)}, u32[]{:S(2)}, u32[]{:S(2)}) collective-permute-start(f32[1,256,256]{2,1,0:T(8,128)S(1)} %fusion.134), channel_id=1, source_target_pairs={{1,0},{2,1},{3,2},{4,3},{5,4},{6,5},{7,6},{8,7},{9,8},{10,9},{11,1... | collective-permute-start | bytes 786440 | tf_op jit(solution)/shard_map/ppermute | solution.py:23
  405.1 3.3 collective-permute-start.21
  408.8 6.6 %collective-permute-start.22 = (f32[1,256,256]{2,1,0:T(8,128)S(1)}, f32[1,256,256]{2,1,0:T(8,128)S(1)}, u32[]{:S(2)}, u32[]{:S(2)}) collective-permute-start(f32[1,256,256]{2,1,0:T(8,128)S(1)} %fusion.116), channel_id=1, source_target_pairs={{1,0},{2,1},{3,2},{4,3},{5,4},{6,5},{7,6},{8,7},{9,8},{10,9},{11,1... | collective-permute-start | bytes 786440 | tf_op jit(solution)/shard_map/ppermute | solution.py:23
  413.8 3.3 collective-permute-start.23
  417.5 6.6 %collective-permute-start.24 = (f32[1,256,256]{2,1,0:T(8,128)S(1)}, f32[1,256,256]{2,1,0:T(8,128)S(1)}, u32[]{:S(2)}, u32[]{:S(2)}) collective-permute-start(f32[1,256,256]{2,1,0:T(8,128)S(1)} %fusion.124), channel_id=1, source_target_pairs={{1,0},{2,1},{3,2},{4,3},{5,4},{6,5},{7,6},{8,7},{9,8},{10,9},{11,1... | collective-permute-start | bytes 786440 | tf_op jit(solution)/shard_map/ppermute | solution.py:23
  431.6 15.3 %collective-permute-start.26 = (f32[1,512,512]{2,1,0:T(8,128)S(1)}, f32[1,512,512]{2,1,0:T(8,128)S(1)}, u32[]{:S(2)}, u32[]{:S(2)}) collective-permute-start(f32[1,512,512]{2,1,0:T(8,128)S(1)} %get-tuple-element.52), channel_id=1, source_target_pairs={{1,0},{2,1},{3,2},{4,3},{5,4},{6,5},{7,6},{8,7},{9,8},{10,9},{11,1... | collective-permute-start | bytes 3145736 | tf_op jit(solution)/shard_map/ppermute | solution.py:23
  435.4 11.7 %collective-permute-start.27 = (f32[1,512,512]{2,1,0:T(8,128)S(1)}, f32[1,512,512]{2,1,0:T(8,128)S(1)}, u32[]{:S(2)}, u32[]{:S(2)}) collective-permute-start(f32[1,512,512]{2,1,0:T(8,128)S(1)} %get-tuple-element.53), channel_id=1, source_target_pairs={{0,1},{1,2},{2,3},{3,4},{4,5},{5,6},{6,7},{7,8},{8,9},{9,10},{10,1... | collective-permute-start | bytes 3145736 | tf_op jit(solution)/shard_map/ppermute | solution.py:21
  450.1 15.3 %collective-permute-start.28 = (f32[1,512,512]{2,1,0:T(8,128)S(1)}, f32[1,512,512]{2,1,0:T(8,128)S(1)}, u32[]{:S(2)}, u32[]{:S(2)}) collective-permute-start(f32[1,512,512]{2,1,0:T(8,128)S(1)} %get-tuple-element.34), channel_id=1, source_target_pairs={{1,0},{2,1},{3,2},{4,3},{5,4},{6,5},{7,6},{8,7},{9,8},{10,9},{11,1... | collective-permute-start | bytes 3145736 | tf_op jit(solution)/shard_map/ppermute | solution.py:23
  453.9 11.7 %collective-permute-start.29 = (f32[1,512,512]{2,1,0:T(8,128)S(1)}, f32[1,512,512]{2,1,0:T(8,128)S(1)}, u32[]{:S(2)}, u32[]{:S(2)}) collective-permute-start(f32[1,512,512]{2,1,0:T(8,128)S(1)} %get-tuple-element.35), channel_id=1, source_target_pairs={{0,1},{1,2},{2,3},{3,4},{4,5},{5,6},{6,7},{7,8},{8,9},{9,10},{10,1... | collective-permute-start | bytes 3145736 | tf_op jit(solution)/shard_map/ppermute | solution.py:21
  470.1 42.3 %all-to-all-start.2 = ((f32[64,1,1]{2,1,0:T(1,128)}), f32[64,1,1]{2,1,0:T(1,128)S(1)}, u32[]{:S(2)}, u32[]{:S(2)}) async-start(f32[64,1,1]{2,1,0:T(1,128)} %broadcast_in_dim.56), calls=%async_computation.2 | async-start | bytes 65536 | tf_op jit(solution)/shard_map/all_to_all | solution.py:32
  (9 other events, 293.9 us)
where the time goes:
time: 522 us; the launch traced here: 515 us
  local copies, waits for them, and re-layouts  186 us (36%)
  waiting for transfers between devices  130 us (25%)
  starting transfers between devices  112 us (21%)
  other arithmetic  83.5 us (16%)
    reduce_sum x2, local copies, waits for them, and re-layouts, restrict(): return jnp.mean(blocks, axis=(1, 3, 5))  137 us
    ppermute x15, waiting for transfers between devices, with_halo(): lax.ppermute(head, axis, [((i + 1) % count, i) for i in range(count)])  70.4 us
    ppermute x15, starting transfers between devices, with_halo(): lax.ppermute(head, axis, [((i + 1) % count, i) for i in range(count)])  66.1 us
    reduce_sum x4, other arithmetic, restrict(): return jnp.mean(blocks, axis=(1, 3, 5))  48.6 us
    all_to_all x3, starting transfers between devices, from_everyone(): lax.all_to_all(jnp.broadcast_to(x[None], (length, *x.shape)), axis, 0, 0,...  44.5 us
    all_to_all x3, waiting for transfers between devices, from_everyone(): lax.all_to_all(jnp.broadcast_to(x[None], (length, *x.shape)), axis, 0, 0,...  40.7 us
    slice x62, local copies, waits for them, and re-layouts, shifted(): return jnp.roll(field, -offset, axis)  24.4 us
    ppermute x15, waiting for transfers between devices, with_halo(): lax.ppermute(tail, axis, [(i, (i + 1) % count) for i in range(count)])  18.4 us
  transfers between devices with their start and end apart: 33, of which 25 were waited for; matrix products, arithmetic and copies ran while one was open for 48% of the time, Pallas kernels for 0%

commit v1 on v0

v1 whole, which is shorter than its diff:
```python
import functools

import jax
import jax.numpy as jnp
import numpy as np
from jax import lax
from jax.experimental import pallas as pl
from jax.experimental.pallas import tpu as pltpu
from jax.sharding import PartitionSpec as P

CYCLES = 2
COARSE = 4
RELAX = 0.8
KAPPA = RELAX / 6.0
COARSE_SCALE = 4.0
CONSTANT_GAIN = KAPPA * (2.0 + COARSE * COARSE_SCALE)
LANES = 128


def rolled(x, shift, axis):
    size = x.shape[axis]
    return pltpu.roll(x, shift % size, axis)


def rolled_z(x, shift):
    rows, subs, nz = x.shape
    return rolled(x.reshape(rows * subs, nz), shift, 1).reshape(x.shape)


def fill_ends(ref, plane, nj):
    ref[plane, 0] = rolled(ref[plane, nj], 1, 0)
    ref[plane, nj + 1] = rolled(ref[plane, 1], -1, 0)


def across(ref, plane, start, rows):
    wide = ref[plane, pl.ds(start, rows + 2)]
    center = wide[1 : rows + 1]
    beside = wide[:rows] + wide[2:] + rolled_z(center, 1) + rolled_z(center, -1)
    return center, beside


def dot_exact(x, table):
    high = x.astype(jnp.bfloat16)
    rest = x - high.astype(jnp.float32)
    middle = rest.astype(jnp.bfloat16)
    low = (rest - middle.astype(jnp.float32)).astype(jnp.bfloat16)
    dot = functools.partial(jnp.dot, preferred_element_type=jnp.float32)
    return dot(high, table) + dot(middle, table) + dot(low, table)


def pair_up(sums_ref, plane, table_ref, out_ref, scale=1.0):
    nc, _, nz = sums_ref.shape[1:]
    step = min(nc, 8)

    def body(i):
        at = i * step
        block = sums_ref[plane, pl.ds(at, step)].reshape(step * 8, nz)
        out = dot_exact(block, table_ref[...]) * scale
        out_ref[pl.ds(at, step)] = out.reshape(step, 8, nz // 2)

    lax.fori_loop(0, nc // step, lambda i, c: (body(i), c)[1], 0)


def loop(count, body, unroll=2):
    lax.fori_loop(0, count, lambda i, c: (body(i), c)[1], 0, unroll=min(unroll, count))


def convert(plane, x, k, X, D, T, nj):
    tiles = T.shape[0]

    def split(i):
        rows = pl.ds(pl.multiple_of(i * 16, 16), 16)
        for t in range(tiles):
            T[t, rows, :] = plane[x, rows, pl.ds(t * LANES, LANES)]

    loop(nj // 2, split, 4)

    def body(j):
        rows = pl.ds(j, 8, stride=nj)
        row = jnp.concatenate([T[t, rows, :] for t in range(tiles)], axis=1)
        X[k, j + 1] = row
        D[k, j + 1] = rolled(row, -1, 1) - rolled(row, 1, 1)

    loop(nj, body, 16)
    fill_ends(X, k, nj)


def prepare_kernel(own, X, D, curved, rest, T):
    nj = X.shape[1] - 2
    for x in range(2):
        convert(own, x, x, X, D, T, nj)
        fill_ends(D, x, nj)

        def body(i, x=x):
            j = 2 * i
            center, beside = X[x, pl.ds(j, 4)], D[x, pl.ds(j, 4)]
            middle = center[1:3]
            double = 2.0 * middle
            curve_yy = center[2:] + center[:2] - double
            curve_zz = rolled_z(middle, 1) + rolled_z(middle, -1) - double
            cross_yz = beside[2:] - beside[:2]
            curved[x, pl.ds(j, 2)] = curve_yy + curve_zz
            rest[x, pl.ds(j, 2)] = 0.0625 * (cross_yz * cross_yz) - curve_yy * curve_zz

        loop(nj // 2, body, 8)


def source_kernel(
    X, D, curved, rest, left, right, table, f00, f01, f10, f11, s0, s1, total, XH, DH, G, T, acc
):
    nj = X.shape[1] - 2
    half = nj // 2
    outs = ((f00, f01), (f10, f11))
    convert(left, 0, 0, XH, DH, T, nj)
    convert(right, 0, 1, XH, DH, T, nj)
    lowers = ((XH, DH, 0), (X, D, 0))
    uppers = ((X, D, 1), (XH, DH, 1))
    acc[...] = jnp.zeros_like(acc)
    for x in range(2):
        for h in range(2):
            def cells(i, x=x, h=h):
                j = h * half + 2 * i
                (lower, lower_d, l), (upper, upper_d, u) = lowers[x], uppers[x]
                above, below = upper[u, pl.ds(j, 4)], lower[l, pl.ds(j, 4)]
                tilt = above - below
                curve_xx = above[1:3] + below[1:3] - 2.0 * X[x, pl.ds(j + 1, 2)]
                cross_xy = tilt[2:] - tilt[:2]
                cross_xz = upper_d[u, pl.ds(j + 1, 2)] - lower_d[l, pl.ds(j + 1, 2)]
                forcing = rest[x, pl.ds(j, 2)] + 0.0625 * (cross_xy * cross_xy + cross_xz * cross_xz)
                forcing = forcing - curve_xx * curved[x, pl.ds(j, 2)]
                outs[x][h][pl.ds(2 * i, 2)] = forcing
                pair = forcing[0] + forcing[1]
                G[x, h * (half // 2) + i] = pair
                acc[...] += pair

            loop(half // 2, cells, 4)
    folded = acc[...]
    width = folded.shape[1]
    total[...] = sum(folded[:, k : k + LANES] for k in range(0, width, LANES))
    pair_up(G, 0, table, s0)
    pair_up(G, 1, table, s1)


def load_rows(refs, V, nj):
    half = nj // 2
    for h in range(2):
        def body(i, h=h):
            V[0, h * half + i + 1] = refs[0][h][i] + refs[1][h][i]

        loop(half, body, 8)
    fill_ends(V, 0, nj)


def rhs_first_kernel(f00, f01, f10, f11, table, out, V, G):
    nj = V.shape[1] - 2
    load_rows(((f00, f01), (f10, f11)), V, nj)

    def body(i):
        center, beside = across(V, 0, 2 * i, 2)
        value = (1.0 - 5.0 * KAPPA) * center + KAPPA * beside
        G[0, i] = value[0] + value[1]

    loop(nj // 2, body, 8)
    pair_up(G, 0, table, out, 0.125)


def rhs_later_kernel(f00, f01, f10, f11, v00, v01, v10, v11, table, out, V, G):
    nj = V.shape[1] - 2
    half = nj // 2
    load_rows(((v00, v01), (v10, v11)), V, nj)
    for h in range(2):
        def body(i, h=h):
            center, beside = across(V, 0, h * half + 2 * i, 2)
            forcing = (f00, f01)[h][pl.ds(2 * i, 2)] + (f10, f11)[h][pl.ds(2 * i, 2)]
            value = forcing - (5.0 * center - beside)
            G[0, h * (half // 2) + i] = value[0] + value[1]

        loop(half // 2, body, 8)
    pair_up(G, 0, table, out, 0.125)


def correct(corrections, table, C):
    nc, _, nz = C.shape[1:]
    step = min(nc, 8)
    for k in range(3):
        def body(i, k=k):
            at = i * step
            block = corrections[k][pl.ds(at, step)].reshape(step * 8, nz // 2)
            C[k, pl.ds(at, step)] = dot_exact(block, table[...]).reshape(step, 8, nz)

        loop(nc // step, body, 1)


def smoothed(W, V, force, nj):
    half = nj // 2
    for k in range(4):
        for h in range(2):
            def body(i, k=k, h=h):
                j = h * half + 2 * i
                center, beside = across(W, k + 1, j, 2)
                beside = beside + W[k, pl.ds(j + 1, 2)] + W[k + 2, pl.ds(j + 1, 2)]
                value = (1.0 - 6.0 * KAPPA) * center + KAPPA * (force[k][h][pl.ds(2 * i, 2)] + beside)
                V[k, pl.ds(j + 1, 2)] = value

            loop(half // 2, body, 8)
        fill_ends(V, k, nj)


def residual_rows(V, x, h, i, force, half):
    j = h * half + 2 * i
    center, beside = across(V, x + 1, j, 2)
    beside = beside + V[x, pl.ds(j + 1, 2)] + V[x + 2, pl.ds(j + 1, 2)]
    return center, force[x + 1][h][pl.ds(2 * i, 2)] - (6.0 * center - beside)


def fold_row(value):
    return jnp.sum(jnp.sum(value, axis=0, keepdims=True), axis=1, keepdims=True)


def stats_row(rest, *figures):
    lane = lax.broadcasted_iota(jnp.int32, (1, LANES), 1)
    for at, figure in enumerate(figures):
        rest = jnp.where(lane == at, figure, rest)
    return rest


def halves(refs):
    return tuple((refs[2 * k], refs[2 * k + 1]) for k in range(len(refs) // 2))


def middle_kernel(*refs):
    (left, own, right), rest = tuple(halves(refs[4 * k : 4 * k + 4]) for k in range(3)), refs[12:]
    c_own, c_left, c_right, shift, table, pairs, v00, v01, v10, v11, s0, s1, stats, W, V, C, G, acc = rest
    nj = W.shape[1] - 2
    half = nj // 2
    outs = ((v00, v01), (v10, v11))
    force = left + own + right
    correct((c_left, c_own, c_right), table, C)
    for k in range(6):
        for h in range(2):
            def body(i, k=k, h=h):
                extra = C[k // 2, h * (half // 2) + i]
                value = KAPPA * force[k][h][pl.ds(2 * i, 2)]
                W[k, pl.ds(h * half + 2 * i + 1, 2)] = value + extra[None]

            loop(half // 2, body, 8)
        if 1 <= k <= 4:
            fill_ends(W, k, nj)
    smoothed(W, V, force[1:5], nj)
    acc[...] = jnp.zeros_like(acc)
    for x in range(2):
        for h in range(2):
            def body(i, x=x, h=h):
                center, residue = residual_rows(V, x, h, i, force[1:5], half)
                value = center + KAPPA * residue
                outs[x][h][pl.ds(2 * i, 2)] = value
                G[x, h * (half // 2) + i] = value[0] + value[1]
                offset = residue - shift[...][None]
                acc[0] += offset[0] + offset[1]
                acc[1] += offset[0] * offset[0] + offset[1] * offset[1]

            loop(half // 2, body, 8)
    zero = jnp.zeros((1, LANES), jnp.float32)
    stats[...] = stats_row(zero, zero, zero, zero, fold_row(acc[0]), fold_row(acc[1]))
    pair_up(G, 0, pairs, s0)
    pair_up(G, 1, pairs, s1)


def last_kernel(*refs):
    f_left, f_right = halves(refs[0:2]), halves(refs[2:4])
    f_own = halves(refs[4:8])
    v_left, v_own, v_right = (halves(refs[4 * k + 8 : 4 * k + 12]) for k in range(3))
    c_own, c_left, c_right, shift, total, first, table, out, stats, W, V, C, acc = refs[20:]
    nj = W.shape[1] - 2
    half = nj // 2
    force = f_left + f_own + f_right
    start = v_left + v_own + v_right
    correct((c_left, c_own, c_right), table, C)
    for k in range(6):
        for h in range(2):
            def body(i, k=k, h=h):
                extra = C[k // 2, h * (half // 2) + i]
                W[k, pl.ds(h * half + 2 * i + 1, 2)] = start[k][h][pl.ds(2 * i, 2)] + extra[None]

            loop(half // 2, body, 8)
        if 1 <= k <= 4:
            fill_ends(W, k, nj)
    smoothed(W, V, force, nj)
    acc[...] = jnp.zeros_like(acc)
    for x in range(2):
        for h in range(2):
            def body(i, x=x, h=h):
                center, residue = residual_rows(V, x, h, i, force, half)
                out[x, pl.ds(h * half + 2 * i, 2)] = center
                offset = residue - shift[...][None]
                acc[0] += offset[0] + offset[1]
                acc[1] += offset[0] * offset[0] + offset[1] * offset[1]

            loop(half // 2, body, 8)
    stats[...] = stats_row(first[...], fold_row(total[...]), fold_row(acc[0]), fold_row(acc[1]))


def natural_kernel(field, out, T):
    nj = field.shape[1]
    tiles = T.shape[0]
    for x in range(2):
        def body(j, x=x):
            row = field[x, j]
            for t in range(tiles):
                T[t, pl.ds(j, 8, stride=nj), :] = row[:, t * LANES : (t + 1) * LANES]

        loop(nj, body, 8)

        def join(i, x=x):
            rows = pl.ds(pl.multiple_of(i * 16, 16), 16)
            for t in range(tiles):
                out[x, rows, pl.ds(t * LANES, LANES)] = T[t, rows, :]

        loop(nj // 2, join, 4)


def finish_kernel(share, figures, field, out, norms):
    devices = figures.shape[0]
    sums = figures[:, 0:1]
    mean = -jnp.sum(sums, axis=0, keepdims=True) / (share * devices)
    off = mean + sums / share
    for c, at in enumerate((3, 1)):
        linear, square = figures[:, at : at + 1], figures[:, at + 1 : at + 2]
        squares = square + 2.0 * off * linear + share * off * off
        total = jnp.sum(squares, axis=0, keepdims=True) / (share * devices)
        norms[c] = jnp.sqrt(total)[0, 0]
    gain = mean * (CONSTANT_GAIN * CYCLES)
    for x in range(2):
        def body(i, x=x):
            rows = pl.ds(pl.multiple_of(i * 16, 16), 16)
            out[x, rows, :] = field[x, rows, :] + gain

        loop(field.shape[1] // 16, body, 4)


VMEM = pl.BlockSpec(memory_space=pltpu.VMEM)
SMEM = pl.BlockSpec(memory_space=pltpu.SMEM)


def call(kernel, args, outs, scratch, flops, out_specs=None):
    moved = 4 * (sum(a.size for a in args) + sum(int(np.prod(o)) for o in outs))
    return pl.pallas_call(
        kernel,
        out_shape=[jax.ShapeDtypeStruct(o, jnp.float32) for o in outs],
        in_specs=[VMEM] * len(args),
        out_specs=out_specs or [VMEM] * len(outs),
        scratch_shapes=[pltpu.VMEM(s, jnp.float32) for s in scratch],
        compiler_params=pltpu.CompilerParams(vmem_limit_bytes=24 * 2**20),
        cost_estimate=pl.CostEstimate(flops=flops, bytes_accessed=moved, transcendentals=0),
    )(*args)


def from_left(x):
    count = lax.axis_size("gx")
    return lax.ppermute(x, "gx", [(i, (i + 1) % count) for i in range(count)])


def from_right(x):
    count = lax.axis_size("gx")
    return lax.ppermute(x, "gx", [((i + 1) % count, i) for i in range(count)])


def gathered(row):
    count = lax.axis_size("gx")
    spread = jnp.broadcast_to(row, (count, *row.shape[1:]))
    return lax.all_to_all(spread, "gx", 0, 0, tiled=True)


def coarse_beside(field):
    first, last = field[:1], field[-1:]
    below = jnp.concatenate([jnp.roll(last, 1, 1), field[:-1]], 0)
    above = jnp.concatenate([field[1:], jnp.roll(first, -1, 1)], 0)
    return below + above + jnp.roll(field, 1, 2) + jnp.roll(field, -1, 2)


def both(to_right, to_left):
    left = from_left(to_right)
    right = from_right(to_left)
    return left, right


def coarse_part(local, s0, s1, weight, chunks):
    moved = []
    left, right = both(s1, s0)
    moved.append(both(chunks[0], chunks[0]))
    rhs = local + (weight * 0.125) * (left + right)
    step = RELAX * COARSE_SCALE / 6.0
    field = step * rhs
    for sweep in range(1, COARSE):
        left, right = both(field, field)
        moved.append(both(chunks[sweep], chunks[sweep]))
        part = (1.0 - RELAX) * field + step * rhs + KAPPA * coarse_beside(field)
        field = part + KAPPA * (left + right)
    left, right = both(field, field)
    lefts, rights = zip(*moved)
    return (field, left, right), lefts, rights


def whole(potential):
    _, ny, nz = potential.shape
    nj, nc = ny // 8, ny // 16
    width = nz // 2
    share = float(potential.size)
    columns = np.arange(nz)[:, None] // 2 == np.arange(width)[None, :]
    pairs = jnp.asarray(columns, jnp.bfloat16)
    copies = jnp.asarray(columns.T, jnp.bfloat16)
    chunk = (nj // 2, 8, nz)
    coarse = (nc, 8, width)
    tall = (nj + 2, 8, nz)

    left = from_left(potential[1:])
    right = from_right(potential[:1])
    tiles = (nz // LANES, ny, LANES)
    prepared = call(
        prepare_kernel, (potential,), [(2, *tall), (2, *tall), (2, nj, 8, nz), (2, nj, 8, nz)], [tiles], 10**8
    )
    *forcing, s0, s1, total = call(
        source_kernel, (*prepared, left, right, pairs), [chunk] * 4 + [coarse] * 2 + [(8, LANES)],
        [(2, *tall), (2, *tall), (2, nc, 8, nz), tiles, (8, nz)], 10**8,
    )
    shift = jnp.broadcast_to(jnp.sum(total) / share, (8, nz))
    (local,) = call(
        rhs_first_kernel, (*forcing, pairs), [coarse], [(1, *tall), (1, nc, 8, nz)], 3 * 10**7
    )
    correction, f_left, f_right = coarse_part(local, s0, s1, KAPPA, forcing)
    scratch = [(6, *tall), (4, *tall), (3, nc, 8, nz)]
    *field, s0, s1, first = call(
        middle_kernel, (*f_left, *forcing, *f_right, *correction, shift, copies, pairs),
        [chunk] * 4 + [coarse] * 2 + [(1, LANES)], [*scratch, (2, nc, 8, nz), (2, 8, nz)], 10**8,
    )
    (local,) = call(
        rhs_later_kernel, (*forcing, *field, pairs), [coarse], [(1, *tall), (1, nc, 8, nz)], 3 * 10**7
    )
    correction, v_left, v_right = coarse_part(local, s0, s1, 1.0, field)
    result, last = call(
        last_kernel,
        (*f_left[2:], *f_right[:2], *forcing, *v_left, *field, *v_right, *correction, shift, total, first, copies),
        [(2, nj, 8, nz), (1, LANES)], [*scratch, (2, 8, nz)], 10**8,
    )
    (result,) = call(natural_kernel, (result,), [potential.shape], [tiles], 3 * 10**7)
    result, norms = call(
        functools.partial(finish_kernel, share), (gathered(last), result),
        [potential.shape, (CYCLES,)], [], 10**7, [VMEM, SMEM],
    )
    return (result, norms)


def solution(mesh):
    in_specs = (P(("runs", "gx"), None, None),)
    out_specs = (P(("runs", "gx"), None, None), P("runs"))
    return jax.shard_map(whole, mesh=mesh, in_specs=in_specs, out_specs=out_specs, check_vma=False)
```

time: 522 us -> 225 us (0.43); the launches traced: 515 us -> 224 us
  local copies, waits for them, and re-layouts: 186 us -> 11.9 us
  other arithmetic: 83.5 us -> 2.85 us
  waiting for transfers between devices: 130 us -> 58.9 us
  Pallas kernels: 0 us -> 41 us
    reduce_sum x2 -> x0, local copies, waits for them, and re-layouts: 137 us -> none  [restrict(): return jnp.mean(blocks, axis=(1, 3, 5))]
    reduce_sum x10 -> x1, other arithmetic: 67.6 us -> 0.6 us  [whole(): shift = jnp.broadcast_to(jnp.sum(total) / share, (8, nz))]
    ppermute x30 -> x38, waiting for transfers between devices: 88.9 us -> 40.6 us  [the longest x19 26.1 us: from_left(): return lax.ppermute(x, 'gx', [(i, (i + 1) % count) for i in range(count)])]
    pallas_call x0 -> x8, Pallas kernels: none -> 41 us  [call(): pl.pallas_call(kernel, out_shape=[jax.ShapeDtypeStruct(o, jnp.float32) fo...]
    all_to_all x3 -> x1, starting transfers between devices: 44.5 us -> 17.1 us  [gathered(): return lax.all_to_all(spread, 'gx', 0, 0, tiled=True)]
    slice x69 -> x31, local copies, waits for them, and re-layouts: 28.5 us -> 3.44 us  [the longest x1 1.86 us: whole(): right = from_right(potential[:1])]
    ppermute x30 -> x38, starting transfers between devices: 67.7 us -> 90.4 us  [the longest x19 81.2 us: from_right(): return lax.ppermute(x, 'gx', [((i + 1) % count, i) for i in range(count)])]
    all_to_all x3 -> x1, waiting for transfers between devices: 40.7 us -> 18.3 us  [gathered(): return lax.all_to_all(spread, 'gx', 0, 0, tiled=True)]
  transfers between devices with their start and end apart: 33 -> 39, of which waited for: 25 -> 16; matrix products, arithmetic and copies ran while one was open for 48% -> 2% of each run, Pallas kernels for 0% -> 4%
where the time goes in v1:
time: 225 us; the launch traced here: 224 us
  starting transfers between devices  108 us (48%)
  waiting for transfers between devices  58.9 us (26%)
  Pallas kernels  41 us (18%)
  local copies, waits for them, and re-layouts  11.9 us (5%)
  other arithmetic  2.85 us (1%)
    ppermute x19, starting transfers between devices, from_right(): return lax.ppermute(x, 'gx', [((i + 1) % count, i) for i in range(count)])  81.2 us
    pallas_call x8, Pallas kernels, call(): pl.pallas_call(kernel, out_shape=[jax.ShapeDtypeStruct(o, jnp.float32) fo...  41 us
    ppermute x19, waiting for transfers between devices, from_left(): return lax.ppermute(x, 'gx', [(i, (i + 1) % count) for i in range(count)])  26.1 us
    all_to_all x1, waiting for transfers between devices, gathered(): return lax.all_to_all(spread, 'gx', 0, 0, tiled=True)  18.3 us
    all_to_all x1, starting transfers between devices, gathered(): return lax.all_to_all(spread, 'gx', 0, 0, tiled=True)  17.1 us
    ppermute x19, waiting for transfers between devices, from_right(): return lax.ppermute(x, 'gx', [((i + 1) % count, i) for i in range(count)])  14.5 us
    ppermute x19, starting transfers between devices, from_left(): return lax.ppermute(x, 'gx', [(i, (i + 1) % count) for i in range(count)])  9.21 us
    unnamed x24, local copies, waits for them, and re-layouts  7.8 us
  transfers between devices with their start and end apart: 39, of which 16 were waited for; matrix products, arithmetic and copies ran while one was open for 2% of the time, Pallas kernels for 4%

profile of v1, /device:TPU:37, one launch (start us, length us, event | category | flops | bytes accessed | tf_op | source)
XLA Modules:
  0.0 224.1 jit_solution(6025528586151347013)
XLA Ops:
  2.5 20.5 %collective-permute-start.1 = (f32[1,512,512]{2,1,0:T(8,128)S(1)}, f32[1,512,512]{2,1,0:T(8,128)S(1)}, u32[]{:S(2)}, u32[]{:S(2)}) collective-permute-start(f32[1,512,512]{2,1,0:T(8,128)S(1)} %get-tuple-element.46), channel_id=1, source_target_pairs={{1,0},{2,1},{3,2},{4,3},{5,4},{6,5},{7,6},{8,7},{9,8},{10,9},{11,1... | collective-permute-start | bytes 3145736 | tf_op jit(solution)/shard_map/ppermute | solution.py:365
  23.0 3.7 %shard_map.50 = (f32[2,66,8,512]{3,2,1,0:T(8,128)S(1)}, f32[2,66,8,512]{3,2,1,0:T(8,128)S(1)}, f32[2,64,8,512]{3,2,1,0:T(8,128)S(1)}, f32[2,64,8,512]{3,2,1,0:T(8,128)S(1)}) custom-call(f32[2,512,512]{2,1,0:T(8,128)S(1)} %copy-done), custom_call_target="tpu_custom_call" | custom-call | flops 100000000 | bytes 10616832 | tf_op jit(solution)/shard_map/pallas_call | solution.py:347
  26.7 8.0 %collective-permute-done.left = f32[1,512,512]{2,1,0:T(8,128)S(1)} collective-permute-done((f32[1,512,512]{2,1,0:T(8,128)S(1)}, f32[1,512,512]{2,1,0:T(8,128)S(1)}, u32[]{:S(2)}, u32[]{:S(2)}) %collective-permute-start) | collective-permute-done | bytes 1048608 | tf_op jit(solution)/shard_map/ppermute | solution.py:360
  34.7 5.3 %shard_map.51 = (f32[32,8,512]{2,1,0:T(8,128)S(1)}, f32[32,8,512]{2,1,0:T(8,128)S(1)}, f32[32,8,512]{2,1,0:T(8,128)S(1)}, f32[32,8,512]{2,1,0:T(8,128)S(1)}, f32...) custom-call(f32[2,66,8,512]{3,2,1,0:T(8,128)S(1)} %get-tuple-element.22.X, ...), custom_call_target="tpu_custom_call" | custom-call | flops 100000000 | bytes 13766656 | tf_op jit(solution)/shard_map/pallas_call | solution.py:347
  40.0 2.5 %collective-permute-start.10 = (f32[32,8,256]{2,1,0:T(8,128)S(1)}, f32[32,8,256]{2,1,0:T(8,128)S(1)}, u32[]{:S(2)}, u32[]{:S(2)}) collective-permute-start(f32[32,8,256]{2,1,0:T(8,128)S(1)} %get-tuple-element.30), channel_id=1, source_target_pairs={{0,1},{1,2},{2,3},{3,4},{4,5},{5,6},{6,7},{7,8},{8,9},{9,10},{10,1... | collective-permute-start | bytes 786440 | tf_op jit(solution)/shard_map/ppermute | solution.py:360
  42.5 4.8 %collective-permute-start.11 = (f32[32,8,256]{2,1,0:T(8,128)S(1)}, f32[32,8,256]{2,1,0:T(8,128)S(1)}, u32[]{:S(2)}, u32[]{:S(2)}) collective-permute-start(f32[32,8,256]{2,1,0:T(8,128)S(1)} %get-tuple-element.31), channel_id=1, source_target_pairs={{1,0},{2,1},{3,2},{4,3},{5,4},{6,5},{7,6},{8,7},{9,8},{10,9},{11,1... | collective-permute-start | bytes 786440 | tf_op jit(solution)/shard_map/ppermute | solution.py:365
  47.3 2.9 %collective-permute-start.8 = (f32[32,8,512]{2,1,0:T(8,128)S(1)}, f32[32,8,512]{2,1,0:T(8,128)S(1)}, u32[]{:S(2)}, u32[]{:S(2)}) collective-permute-start(f32[32,8,512]{2,1,0:T(8,128)S(1)} %get-tuple-element.26.f10.refs_6_), channel_id=1, source_target_pairs={{1,0},{2,1},{3,2},{4,3},{5,4},{6,5},{7,6},{8,7},{9,8},{10,9},{11,1... | collective-permute-start | bytes 1572872 | tf_op jit(solution)/shard_map/ppermute | solution.py:365
  55.8 3.4 %collective-permute-done.12 = f32[32,8,256]{2,1,0:T(8,128)S(1)} collective-permute-done((f32[32,8,256]{2,1,0:T(8,128)S(1)}, f32[32,8,256]{2,1,0:T(8,128)S(1)}, u32[]{:S(2)}, u32[]{:S(2)}) %collective-permute-start.12) | collective-permute-done | bytes 262176 | tf_op jit(solution)/shard_map/ppermute | solution.py:360
  59.2 5.2 %collective-permute-done.13 = f32[32,8,256]{2,1,0:T(8,128)S(1)} collective-permute-done((f32[32,8,256]{2,1,0:T(8,128)S(1)}, f32[32,8,256]{2,1,0:T(8,128)S(1)}, u32[]{:S(2)}, u32[]{:S(2)}) %collective-permute-start.13) | collective-permute-done | bytes 262176 | tf_op jit(solution)/shard_map/ppermute | solution.py:365
  64.8 3.8 %collective-permute-start.15 = (f32[32,8,256]{2,1,0:T(8,128)S(1)}, f32[32,8,256]{2,1,0:T(8,128)S(1)}, u32[]{:S(2)}, u32[]{:S(2)}) collective-permute-start(f32[32,8,256]{2,1,0:T(8,128)S(1)} %fusion.4), channel_id=1, source_target_pairs={{1,0},{2,1},{3,2},{4,3},{5,4},{6,5},{7,6},{8,7},{9,8},{10,9},{11,1... | collective-permute-start | bytes 786440 | tf_op jit(solution)/shard_map/ppermute | solution.py:365
  71.0 5.2 %collective-permute-start.17 = (f32[32,8,256]{2,1,0:T(8,128)S(1)}, f32[32,8,256]{2,1,0:T(8,128)S(1)}, u32[]{:S(2)}, u32[]{:S(2)}) collective-permute-start(f32[32,8,256]{2,1,0:T(8,128)S(1)} %fusion.9), channel_id=1, source_target_pairs={{1,0},{2,1},{3,2},{4,3},{5,4},{6,5},{7,6},{8,7},{9,8},{10,9},{11,1... | collective-permute-start | bytes 786440 | tf_op jit(solution)/shard_map/ppermute | solution.py:365
  76.6 3.1 %collective-permute-start.4 = (f32[32,8,512]{2,1,0:T(8,128)S(1)}, f32[32,8,512]{2,1,0:T(8,128)}, u32[]{:S(2)}, u32[]{:S(2)}) collective-permute-start(f32[32,8,512]{2,1,0:T(8,128)S(1)} %get-tuple-element.28.f00.refs_4_), channel_id=1, source_target_pairs={{1,0},{2,1},{3,2},{4,3},{5,4},{6,5},{7,6},{8,7},{9,8},{10,9},{11,1... | collective-permute-start | bytes 1572872 | tf_op jit(solution)/shard_map/ppermute | solution.py:365
  79.7 3.5 %collective-permute-start.5 = (f32[32,8,512]{2,1,0:T(8,128)S(1)}, f32[32,8,512]{2,1,0:T(8,128)}, u32[]{:S(2)}, u32[]{:S(2)}) collective-permute-start(f32[32,8,512]{2,1,0:T(8,128)S(1)} %get-tuple-element.29.f01.refs_5_), channel_id=1, source_target_pairs={{1,0},{2,1},{3,2},{4,3},{5,4},{6,5},{7,6},{8,7},{9,8},{10,9},{11,1... | collective-permute-start | bytes 1572872 | tf_op jit(solution)/shard_map/ppermute | solution.py:365
  84.1 5.2 %collective-permute-start.19 = (f32[32,8,256]{2,1,0:T(8,128)}, f32[32,8,256]{2,1,0:T(8,128)}, u32[]{:S(2)}, u32[]{:S(2)}) collective-permute-start(f32[32,8,256]{2,1,0:T(8,128)} %fusion.14.refs_12_), channel_id=1, source_target_pairs={{1,0},{2,1},{3,2},{4,3},{5,4},{6,5},{7,6},{8,7},{9,8},{10,9},{11,1... | collective-permute-start | bytes 786440 | tf_op jit(solution)/shard_map/ppermute | solution.py:365
  94.0 3.1 %collective-permute-done.18.refs_13_ = f32[32,8,256]{2,1,0:T(8,128)} collective-permute-done((f32[32,8,256]{2,1,0:T(8,128)}, f32[32,8,256]{2,1,0:T(8,128)}, u32[]{:S(2)}, u32[]{:S(2)}) %collective-permute-start.18) | collective-permute-done | bytes 262176 | tf_op jit(solution)/shard_map/ppermute | solution.py:360
  101.2 12.7 %shard_map.53 = (f32[32,8,512]{2,1,0:T(8,128)S(1)}, f32[32,8,512]{2,1,0:T(8,128)S(1)}, f32[32,8,512]{2,1,0:T(8,128)S(1)}, f32[32,8,512]{2,1,0:T(8,128)S(1)}, f32...) custom-call(f32[32,8,512]{2,1,0:T(8,128)S(1)} %copy-done.11, ...), custom_call_target="tpu_custom_call" | custom-call | flops 100000000 | bytes 10764800 | tf_op jit(solution)/shard_map/pallas_call | solution.py:347
  113.9 2.2 collective-permute-start.28
  116.1 4.3 %collective-permute-start.29 = (f32[32,8,256]{2,1,0:T(8,128)S(1)}, f32[32,8,256]{2,1,0:T(8,128)S(1)}, u32[]{:S(2)}, u32[]{:S(2)}) collective-permute-start(f32[32,8,256]{2,1,0:T(8,128)S(1)} %get-tuple-element.38), channel_id=1, source_target_pairs={{1,0},{2,1},{3,2},{4,3},{5,4},{6,5},{7,6},{8,7},{9,8},{10,9},{11,1... | collective-permute-start | bytes 786440 | tf_op jit(solution)/shard_map/ppermute | solution.py:365
  120.4 2.9 %collective-permute-start.24 = (f32[32,8,512]{2,1,0:T(8,128)S(1)}, f32[32,8,512]{2,1,0:T(8,128)S(1)}, u32[]{:S(2)}, u32[]{:S(2)}) collective-permute-start(f32[32,8,512]{2,1,0:T(8,128)S(1)} %get-tuple-element.33.v00.refs_12_), channel_id=1, source_target_pairs={{1,0},{2,1},{3,2},{4,3},{5,4},{6,5},{7,6},{8,7},{9,8},{10,9},{11,1... | collective-permute-start | bytes 1572872 | tf_op jit(solution)/shard_map/ppermute | solution.py:365
  128.8 3.4 %collective-permute-done.30 = f32[32,8,256]{2,1,0:T(8,128)S(1)} collective-permute-done((f32[32,8,256]{2,1,0:T(8,128)S(1)}, f32[32,8,256]{2,1,0:T(8,128)S(1)}, u32[]{:S(2)}, u32[]{:S(2)}) %collective-permute-start.30) | collective-permute-done | bytes 262176 | tf_op jit(solution)/shard_map/ppermute | solution.py:360
  132.2 5.2 %collective-permute-done.31 = f32[32,8,256]{2,1,0:T(8,128)S(1)} collective-permute-done((f32[32,8,256]{2,1,0:T(8,128)S(1)}, f32[32,8,256]{2,1,0:T(8,128)S(1)}, u32[]{:S(2)}, u32[]{:S(2)}) %collective-permute-start.31) | collective-permute-done | bytes 262176 | tf_op jit(solution)/shard_map/ppermute | solution.py:365
  137.8 3.8 %collective-permute-start.33 = (f32[32,8,256]{2,1,0:T(8,128)S(1)}, f32[32,8,256]{2,1,0:T(8,128)S(1)}, u32[]{:S(2)}, u32[]{:S(2)}) collective-permute-start(f32[32,8,256]{2,1,0:T(8,128)S(1)} %fusion.19), channel_id=1, source_target_pairs={{1,0},{2,1},{3,2},{4,3},{5,4},{6,5},{7,6},{8,7},{9,8},{10,9},{11,1... | collective-permute-start | bytes 786440 | tf_op jit(solution)/shard_map/ppermute | solution.py:365
  144.0 5.2 %collective-permute-start.35 = (f32[32,8,256]{2,1,0:T(8,128)S(1)}, f32[32,8,256]{2,1,0:T(8,128)S(1)}, u32[]{:S(2)}, u32[]{:S(2)}) collective-permute-start(f32[32,8,256]{2,1,0:T(8,128)S(1)} %fusion.24), channel_id=1, source_target_pairs={{1,0},{2,1},{3,2},{4,3},{5,4},{6,5},{7,6},{8,7},{9,8},{10,9},{11,1... | collective-permute-start | bytes 786440 | tf_op jit(solution)/shard_map/ppermute | solution.py:365
  149.5 3.1 %collective-permute-start.26 = (f32[32,8,512]{2,1,0:T(8,128)S(1)}, f32[32,8,512]{2,1,0:T(8,128)S(1)}, u32[]{:S(2)}, u32[]{:S(2)}) collective-permute-start(f32[32,8,512]{2,1,0:T(8,128)S(1)} %get-tuple-element.35.v10.refs_14_), channel_id=1, source_target_pairs={{1,0},{2,1},{3,2},{4,3},{5,4},{6,5},{7,6},{8,7},{9,8},{10,9},{11,1... | collective-permute-start | bytes 1572872 | tf_op jit(solution)/shard_map/ppermute | solution.py:365
  152.6 3.5 %collective-permute-start.27 = (f32[32,8,512]{2,1,0:T(8,128)S(1)}, f32[32,8,512]{2,1,0:T(8,128)S(1)}, u32[]{:S(2)}, u32[]{:S(2)}) collective-permute-start(f32[32,8,512]{2,1,0:T(8,128)S(1)} %get-tuple-element.36.v11.refs_15_), channel_id=1, source_target_pairs={{1,0},{2,1},{3,2},{4,3},{5,4},{6,5},{7,6},{8,7},{9,8},{10,9},{11,1... | collective-permute-start | bytes 1572872 | tf_op jit(solution)/shard_map/ppermute | solution.py:365
  156.4 5.9 %collective-permute-start.37 = (f32[32,8,256]{2,1,0:T(8,128)S(1)}, f32[32,8,256]{2,1,0:T(8,128)S(1)}, u32[]{:S(2)}, u32[]{:S(2)}) collective-permute-start(f32[32,8,256]{2,1,0:T(8,128)S(1)} %fusion.29.refs_20_), channel_id=1, source_target_pairs={{1,0},{2,1},{3,2},{4,3},{5,4},{6,5},{7,6},{8,7},{9,8},{10,9},{11,1... | collective-permute-start | bytes 786440 | tf_op jit(solution)/shard_map/ppermute | solution.py:365
  164.1 2.8 %collective-permute-done.23.refs_11_ = f32[32,8,512]{2,1,0:T(8,128)S(1)} collective-permute-done((f32[32,8,512]{2,1,0:T(8,128)S(1)}, f32[32,8,512]{2,1,0:T(8,128)S(1)}, u32[]{:S(2)}, u32[]{:S(2)}) %collective-permute-start.23) | collective-permute-done | bytes 524320 | tf_op jit(solution)/shard_map/ppermute | solution.py:360
  166.9 2.8 %collective-permute-done.36.refs_21_ = f32[32,8,256]{2,1,0:T(8,128)S(1)} collective-permute-done((f32[32,8,256]{2,1,0:T(8,128)S(1)}, f32[32,8,256]{2,1,0:T(8,128)S(1)}, u32[]{:S(2)}, u32[]{:S(2)}) %collective-permute-start.36) | collective-permute-done | bytes 262176 | tf_op jit(solution)/shard_map/ppermute | solution.py:360
  169.7 10.2 %shard_map.55 = (f32[2,64,8,512]{3,2,1,0:T(8,128)S(1)}, f32[1,128]{1,0:T(1,128)S(1)}) custom-call(f32[32,8,512]{2,1,0:T(8,128)S(1)} %collective-permute-done.2.refs_2_.refs_0_, f32[32,8,512]{2,1,0:T(8,128)S(1)} %collective-permute-done.3.refs_3_.refs_1_, f32[32,8,512]{2,1,0:T(8,128)} %collective-permute-done.4.refs_8_.refs_2_, ...), custom_call_target="tpu_custom_call" | custom-call | flops 100000000 | bytes 13915136 | tf_op jit(solution)/shard_map/pallas_call | solution.py:347
  181.9 17.1 %all-to-all-start = ((f32[64,1,128]{2,1,0:T(1,128)}), f32[64,1,128]{2,1,0:T(1,128)S(1)}, u32[]{:S(2)}, u32[]{:S(2)}) async-start(f32[64,1,128]{2,1,0:T(1,128)} %broadcast_in_dim.9), calls=%async_computation | async-start | bytes 65536 | tf_op jit(solution)/shard_map/all_to_all | solution.py:371
  202.8 18.3 %all-to-all-done = f32[64,1,128]{2,1,0:T(1,128)S(1)} async-done(((f32[64,1,128]{2,1,0:T(1,128)}), f32[64,1,128]{2,1,0:T(1,128)S(1)}, u32[]{:S(2)}, u32[]{:S(2)}) %all-to-all-start) | async-done | bytes 32800 | tf_op jit(solution)/shard_map/all_to_all | solution.py:371
  221.1 2.9 %shard_map.57 = (f32[2,512,512]{2,1,0:T(8,128)}, f32[2]{0:T(128)}) custom-call(f32[64,128]{1,0:T(8,128)S(1)} %bitcast.2, f32[2,512,512]{2,1,0:T(8,128)S(1)} %shard_map.56.field), custom_call_target="tpu_custom_call" | custom-call | flops 10000000 | bytes 4227080 | tf_op jit(solution)/shard_map/pallas_call | solution.py:347
  (120 shorter events, 35.8 us)
Async XLA Ops:
  2.5 24.2 %collective-permute-start.1 = (f32[1,512,512]{2,1,0:T(8,128)S(1)}, f32[1,512,512]{2,1,0:T(8,128)S(1)}, u32[]{:S(2)}, u32[]{:S(2)}) collective-permute-start(f32[1,512,512]{2,1,0:T(8,128)S(1)} %get-tuple-element.46), channel_id=1, source_target_pairs={{1,0},{2,1},{3,2},{4,3},{5,4},{6,5},{7,6},{8,7},{9,8},{10,9},{11,1... | collective-permute-start | bytes 3145736 | tf_op jit(solution)/shard_map/ppermute | solution.py:365
  23.0 11.7 %collective-permute-start = (f32[1,512,512]{2,1,0:T(8,128)S(1)}, f32[1,512,512]{2,1,0:T(8,128)S(1)}, u32[]{:S(2)}, u32[]{:S(2)}) collective-permute-start(f32[1,512,512]{2,1,0:T(8,128)S(1)} %get-tuple-element.47), channel_id=1, source_target_pairs={{0,1},{1,2},{2,3},{3,4},{4,5},{5,6},{6,7},{7,8},{8,9},{9,10},{10,1... | collective-permute-start | bytes 3145736 | tf_op jit(solution)/shard_map/ppermute | solution.py:360
  40.0 12.8 %collective-permute-start.10 = (f32[32,8,256]{2,1,0:T(8,128)S(1)}, f32[32,8,256]{2,1,0:T(8,128)S(1)}, u32[]{:S(2)}, u32[]{:S(2)}) collective-permute-start(f32[32,8,256]{2,1,0:T(8,128)S(1)} %get-tuple-element.30), channel_id=1, source_target_pairs={{0,1},{1,2},{2,3},{3,4},{4,5},{5,6},{6,7},{7,8},{8,9},{9,10},{10,1... | collective-permute-start | bytes 786440 | tf_op jit(solution)/shard_map/ppermute | solution.py:360
  42.5 10.3 %collective-permute-start.11 = (f32[32,8,256]{2,1,0:T(8,128)S(1)}, f32[32,8,256]{2,1,0:T(8,128)S(1)}, u32[]{:S(2)}, u32[]{:S(2)}) collective-permute-start(f32[32,8,256]{2,1,0:T(8,128)S(1)} %get-tuple-element.31), channel_id=1, source_target_pairs={{1,0},{2,1},{3,2},{4,3},{5,4},{6,5},{7,6},{8,7},{9,8},{10,9},{11,1... | collective-permute-start | bytes 786440 | tf_op jit(solution)/shard_map/ppermute | solution.py:365
  47.3 29.1 %collective-permute-start.8 = (f32[32,8,512]{2,1,0:T(8,128)S(1)}, f32[32,8,512]{2,1,0:T(8,128)S(1)}, u32[]{:S(2)}, u32[]{:S(2)}) collective-permute-start(f32[32,8,512]{2,1,0:T(8,128)S(1)} %get-tuple-element.26.f10.refs_6_), channel_id=1, source_target_pairs={{1,0},{2,1},{3,2},{4,3},{5,4},{6,5},{7,6},{8,7},{9,8},{10,9},{11,1... | collective-permute-start | bytes 1572872 | tf_op jit(solution)/shard_map/ppermute | solution.py:365
  50.2 26.3 %collective-permute-start.2 = (f32[32,8,512]{2,1,0:T(8,128)S(1)}, f32[32,8,512]{2,1,0:T(8,128)S(1)}, u32[]{:S(2)}, u32[]{:S(2)}) collective-permute-start(f32[32,8,512]{2,1,0:T(8,128)S(1)} %get-tuple-element.26.f10.refs_6_), channel_id=1, source_target_pairs={{0,1},{1,2},{2,3},{3,4},{4,5},{5,6},{6,7},{7,8},{8,9},{9,10},{10,1... | collective-permute-start | bytes 1572872 | tf_op jit(solution)/shard_map/ppermute | solution.py:360
  50.2 26.4 %collective-permute-start.9 = (f32[32,8,512]{2,1,0:T(8,128)S(1)}, f32[32,8,512]{2,1,0:T(8,128)S(1)}, u32[]{:S(2)}, u32[]{:S(2)}) collective-permute-start(f32[32,8,512]{2,1,0:T(8,128)S(1)} %get-tuple-element.27.f11.refs_7_), channel_id=1, source_target_pairs={{1,0},{2,1},{3,2},{4,3},{5,4},{6,5},{7,6},{8,7},{9,8},{10,9},{11,1... | collective-permute-start | bytes 1572872 | tf_op jit(solution)/shard_map/ppermute | solution.py:365
  54.2 10.1 %collective-permute-start.13 = (f32[32,8,256]{2,1,0:T(8,128)S(1)}, f32[32,8,256]{2,1,0:T(8,128)S(1)}, u32[]{:S(2)}, u32[]{:S(2)}) collective-permute-start(f32[32,8,256]{2,1,0:T(8,128)S(1)} %get-tuple-element.44), channel_id=1, source_target_pairs={{1,0},{2,1},{3,2},{4,3},{5,4},{6,5},{7,6},{8,7},{9,8},{10,9},{11,1... | collective-permute-start | bytes 786440 | tf_op jit(solution)/shard_map/ppermute | solution.py:365
  70.9 8.8 %collective-permute-start.16 = (f32[32,8,256]{2,1,0:T(8,128)S(1)}, f32[32,8,256]{2,1,0:T(8,128)S(1)}, u32[]{:S(2)}, u32[]{:S(2)}) collective-permute-start(f32[32,8,256]{2,1,0:T(8,128)S(1)} %fusion.9), channel_id=1, source_target_pairs={{0,1},{1,2},{2,3},{3,4},{4,5},{5,6},{6,7},{7,8},{8,9},{9,10},{10,1... | collective-permute-start | bytes 786440 | tf_op jit(solution)/shard_map/ppermute | solution.py:360
  71.0 8.7 %collective-permute-start.17 = (f32[32,8,256]{2,1,0:T(8,128)S(1)}, f32[32,8,256]{2,1,0:T(8,128)S(1)}, u32[]{:S(2)}, u32[]{:S(2)}) collective-permute-start(f32[32,8,256]{2,1,0:T(8,128)S(1)} %fusion.9), channel_id=1, source_target_pairs={{1,0},{2,1},{3,2},{4,3},{5,4},{6,5},{7,6},{8,7},{9,8},{10,9},{11,1... | collective-permute-start | bytes 786440 | tf_op jit(solution)/shard_map/ppermute | solution.py:365
  76.4 7.6 %collective-permute-start.3 = (f32[32,8,512]{2,1,0:T(8,128)S(1)}, f32[32,8,512]{2,1,0:T(8,128)S(1)}, u32[]{:S(2)}, u32[]{:S(2)}) collective-permute-start(f32[32,8,512]{2,1,0:T(8,128)S(1)} %get-tuple-element.27.f11.refs_7_), channel_id=1, source_target_pairs={{0,1},{1,2},{2,3},{3,4},{4,5},{5,6},{6,7},{7,8},{8,9},{9,10},{10,1... | collective-permute-start | bytes 1572872 | tf_op jit(solution)/shard_map/ppermute | solution.py:360
  76.5 12.8 %collective-permute-start.6 = (f32[32,8,512]{2,1,0:T(8,128)S(1)}, f32[32,8,512]{2,1,0:T(8,128)S(1)}, u32[]{:S(2)}, u32[]{:S(2)}) collective-permute-start(f32[32,8,512]{2,1,0:T(8,128)S(1)} %get-tuple-element.28.f00.refs_4_), channel_id=1, source_target_pairs={{0,1},{1,2},{2,3},{3,4},{4,5},{5,6},{6,7},{7,8},{8,9},{9,10},{10,1... | collective-permute-start | bytes 1572872 | tf_op jit(solution)/shard_map/ppermute | solution.py:360
  76.6 16.2 %collective-permute-start.4 = (f32[32,8,512]{2,1,0:T(8,128)S(1)}, f32[32,8,512]{2,1,0:T(8,128)}, u32[]{:S(2)}, u32[]{:S(2)}) collective-permute-start(f32[32,8,512]{2,1,0:T(8,128)S(1)} %get-tuple-element.28.f00.refs_4_), channel_id=1, source_target_pairs={{1,0},{2,1},{3,2},{4,3},{5,4},{6,5},{7,6},{8,7},{9,8},{10,9},{11,1... | collective-permute-start | bytes 1572872 | tf_op jit(solution)/shard_map/ppermute | solution.py:365
  79.7 14.2 %collective-permute-start.7 = (f32[32,8,512]{2,1,0:T(8,128)S(1)}, f32[32,8,512]{2,1,0:T(8,128)}, u32[]{:S(2)}, u32[]{:S(2)}) collective-permute-start(f32[32,8,512]{2,1,0:T(8,128)S(1)} %get-tuple-element.29.f01.refs_5_), channel_id=1, source_target_pairs={{0,1},{1,2},{2,3},{3,4},{4,5},{5,6},{6,7},{7,8},{8,9},{9,10},{10,1... | collective-permute-start | bytes 1572872 | tf_op jit(solution)/shard_map/ppermute | solution.py:360
  79.7 14.2 %collective-permute-start.5 = (f32[32,8,512]{2,1,0:T(8,128)S(1)}, f32[32,8,512]{2,1,0:T(8,128)}, u32[]{:S(2)}, u32[]{:S(2)}) collective-permute-start(f32[32,8,512]{2,1,0:T(8,128)S(1)} %get-tuple-element.29.f01.refs_5_), channel_id=1, source_target_pairs={{1,0},{2,1},{3,2},{4,3},{5,4},{6,5},{7,6},{8,7},{9,8},{10,9},{11,1... | collective-permute-start | bytes 1572872 | tf_op jit(solution)/shard_map/ppermute | solution.py:365
  84.1 9.9 %collective-permute-start.19 = (f32[32,8,256]{2,1,0:T(8,128)}, f32[32,8,256]{2,1,0:T(8,128)}, u32[]{:S(2)}, u32[]{:S(2)}) collective-permute-start(f32[32,8,256]{2,1,0:T(8,128)} %fusion.14.refs_12_), channel_id=1, source_target_pairs={{1,0},{2,1},{3,2},{4,3},{5,4},{6,5},{7,6},{8,7},{9,8},{10,9},{11,1... | collective-permute-start | bytes 786440 | tf_op jit(solution)/shard_map/ppermute | solution.py:365
  90.1 7.0 %collective-permute-start.18 = (f32[32,8,256]{2,1,0:T(8,128)}, f32[32,8,256]{2,1,0:T(8,128)}, u32[]{:S(2)}, u32[]{:S(2)}) collective-permute-start(f32[32,8,256]{2,1,0:T(8,128)} %fusion.14.refs_12_), channel_id=1, source_target_pairs={{0,1},{1,2},{2,3},{3,4},{4,5},{5,6},{6,7},{7,8},{8,9},{9,10},{10,1... | collective-permute-start | bytes 786440 | tf_op jit(solution)/shard_map/ppermute | solution.py:360
  113.9 11.9 %collective-permute-start.28 = (f32[32,8,256]{2,1,0:T(8,128)S(1)}, f32[32,8,256]{2,1,0:T(8,128)S(1)}, u32[]{:S(2)}, u32[]{:S(2)}) collective-permute-start(f32[32,8,256]{2,1,0:T(8,128)S(1)} %get-tuple-element.37), channel_id=1, source_target_pairs={{0,1},{1,2},{2,3},{3,4},{4,5},{5,6},{6,7},{7,8},{8,9},{9,10},{10,1... | collective-permute-start | bytes 786440 | tf_op jit(solution)/shard_map/ppermute | solution.py:360
  116.1 9.7 %collective-permute-start.29 = (f32[32,8,256]{2,1,0:T(8,128)S(1)}, f32[32,8,256]{2,1,0:T(8,128)S(1)}, u32[]{:S(2)}, u32[]{:S(2)}) collective-permute-start(f32[32,8,256]{2,1,0:T(8,128)S(1)} %get-tuple-element.38), channel_id=1, source_target_pairs={{1,0},{2,1},{3,2},{4,3},{5,4},{6,5},{7,6},{8,7},{9,8},{10,9},{11,1... | collective-permute-start | bytes 786440 | tf_op jit(solution)/shard_map/ppermute | solution.py:365
  120.4 29.1 %collective-permute-start.24 = (f32[32,8,512]{2,1,0:T(8,128)S(1)}, f32[32,8,512]{2,1,0:T(8,128)S(1)}, u32[]{:S(2)}, u32[]{:S(2)}) collective-permute-start(f32[32,8,512]{2,1,0:T(8,128)S(1)} %get-tuple-element.33.v00.refs_12_), channel_id=1, source_target_pairs={{1,0},{2,1},{3,2},{4,3},{5,4},{6,5},{7,6},{8,7},{9,8},{10,9},{11,1... | collective-permute-start | bytes 1572872 | tf_op jit(solution)/shard_map/ppermute | solution.py:365
  123.3 26.3 %collective-permute-start.20 = (f32[32,8,512]{2,1,0:T(8,128)S(1)}, f32[32,8,512]{2,1,0:T(8,128)S(1)}, u32[]{:S(2)}, u32[]{:S(2)}) collective-permute-start(f32[32,8,512]{2,1,0:T(8,128)S(1)} %get-tuple-element.33.v00.refs_12_), channel_id=1, source_target_pairs={{0,1},{1,2},{2,3},{3,4},{4,5},{5,6},{6,7},{7,8},{8,9},{9,10},{10,1... | collective-permute-start | bytes 1572872 | tf_op jit(solution)/shard_map/ppermute | solution.py:360
  123.3 29.3 %collective-permute-start.25 = (f32[32,8,512]{2,1,0:T(8,128)S(1)}, f32[32,8,512]{2,1,0:T(8,128)S(1)}, u32[]{:S(2)}, u32[]{:S(2)}) collective-permute-start(f32[32,8,512]{2,1,0:T(8,128)S(1)} %get-tuple-element.34.v01.refs_13_), channel_id=1, source_target_pairs={{1,0},{2,1},{3,2},{4,3},{5,4},{6,5},{7,6},{8,7},{9,8},{10,9},{11,1... | collective-permute-start | bytes 1572872 | tf_op jit(solution)/shard_map/ppermute | solution.py:365
  127.3 10.1 %collective-permute-start.31 = (f32[32,8,256]{2,1,0:T(8,128)S(1)}, f32[32,8,256]{2,1,0:T(8,128)S(1)}, u32[]{:S(2)}, u32[]{:S(2)}) collective-permute-start(f32[32,8,256]{2,1,0:T(8,128)S(1)} %get-tuple-element.42), channel_id=1, source_target_pairs={{1,0},{2,1},{3,2},{4,3},{5,4},{6,5},{7,6},{8,7},{9,8},{10,9},{11,1... | collective-permute-start | bytes 786440 | tf_op jit(solution)/shard_map/ppermute | solution.py:365
  143.9 8.7 %collective-permute-start.34 = (f32[32,8,256]{2,1,0:T(8,128)S(1)}, f32[32,8,256]{2,1,0:T(8,128)S(1)}, u32[]{:S(2)}, u32[]{:S(2)}) collective-permute-start(f32[32,8,256]{2,1,0:T(8,128)S(1)} %fusion.24), channel_id=1, source_target_pairs={{0,1},{1,2},{2,3},{3,4},{4,5},{5,6},{6,7},{7,8},{8,9},{9,10},{10,1... | collective-permute-start | bytes 786440 | tf_op jit(solution)/shard_map/ppermute | solution.py:360
  144.0 12.2 %collective-permute-start.35 = (f32[32,8,256]{2,1,0:T(8,128)S(1)}, f32[32,8,256]{2,1,0:T(8,128)S(1)}, u32[]{:S(2)}, u32[]{:S(2)}) collective-permute-start(f32[32,8,256]{2,1,0:T(8,128)S(1)} %fusion.24), channel_id=1, source_target_pairs={{1,0},{2,1},{3,2},{4,3},{5,4},{6,5},{7,6},{8,7},{9,8},{10,9},{11,1... | collective-permute-start | bytes 786440 | tf_op jit(solution)/shard_map/ppermute | solution.py:365
  149.5 12.8 %collective-permute-start.26 = (f32[32,8,512]{2,1,0:T(8,128)S(1)}, f32[32,8,512]{2,1,0:T(8,128)S(1)}, u32[]{:S(2)}, u32[]{:S(2)}) collective-permute-start(f32[32,8,512]{2,1,0:T(8,128)S(1)} %get-tuple-element.35.v10.refs_14_), channel_id=1, source_target_pairs={{1,0},{2,1},{3,2},{4,3},{5,4},{6,5},{7,6},{8,7},{9,8},{10,9},{11,1... | collective-permute-start | bytes 1572872 | tf_op jit(solution)/shard_map/ppermute | solution.py:365
  152.6 9.7 %collective-permute-start.22 = (f32[32,8,512]{2,1,0:T(8,128)S(1)}, f32[32,8,512]{2,1,0:T(8,128)S(1)}, u32[]{:S(2)}, u32[]{:S(2)}) collective-permute-start(f32[32,8,512]{2,1,0:T(8,128)S(1)} %get-tuple-element.35.v10.refs_14_), channel_id=1, source_target_pairs={{0,1},{1,2},{2,3},{3,4},{4,5},{5,6},{6,7},{7,8},{8,9},{9,10},{10,1... | collective-permute-start | bytes 1572872 | tf_op jit(solution)/shard_map/ppermute | solution.py:360
  152.6 11.5 %collective-permute-start.27 = (f32[32,8,512]{2,1,0:T(8,128)S(1)}, f32[32,8,512]{2,1,0:T(8,128)S(1)}, u32[]{:S(2)}, u32[]{:S(2)}) collective-permute-start(f32[32,8,512]{2,1,0:T(8,128)S(1)} %get-tuple-element.36.v11.refs_15_), channel_id=1, source_target_pairs={{1,0},{2,1},{3,2},{4,3},{5,4},{6,5},{7,6},{8,7},{9,8},{10,9},{11,1... | collective-permute-start | bytes 1572872 | tf_op jit(solution)/shard_map/ppermute | solution.py:365
  156.2 10.7 %collective-permute-start.23 = (f32[32,8,512]{2,1,0:T(8,128)S(1)}, f32[32,8,512]{2,1,0:T(8,128)S(1)}, u32[]{:S(2)}, u32[]{:S(2)}) collective-permute-start(f32[32,8,512]{2,1,0:T(8,128)S(1)} %get-tuple-element.36.v11.refs_15_), channel_id=1, source_target_pairs={{0,1},{1,2},{2,3},{3,4},{4,5},{5,6},{6,7},{7,8},{8,9},{9,10},{10,1... | collective-permute-start | bytes 1572872 | tf_op jit(solution)/shard_map/ppermute | solution.py:360
  156.4 10.5 %collective-permute-start.37 = (f32[32,8,256]{2,1,0:T(8,128)S(1)}, f32[32,8,256]{2,1,0:T(8,128)S(1)}, u32[]{:S(2)}, u32[]{:S(2)}) collective-permute-start(f32[32,8,256]{2,1,0:T(8,128)S(1)} %fusion.29.refs_20_), channel_id=1, source_target_pairs={{1,0},{2,1},{3,2},{4,3},{5,4},{6,5},{7,6},{8,7},{9,8},{10,9},{11,1... | collective-permute-start | bytes 786440 | tf_op jit(solution)/shard_map/ppermute | solution.py:365
  162.3 7.4 %collective-permute-start.36 = (f32[32,8,256]{2,1,0:T(8,128)S(1)}, f32[32,8,256]{2,1,0:T(8,128)S(1)}, u32[]{:S(2)}, u32[]{:S(2)}) collective-permute-start(f32[32,8,256]{2,1,0:T(8,128)S(1)} %fusion.29.refs_20_), channel_id=1, source_target_pairs={{0,1},{1,2},{2,3},{3,4},{4,5},{5,6},{6,7},{7,8},{8,9},{9,10},{10,1... | collective-permute-start | bytes 786440 | tf_op jit(solution)/shard_map/ppermute | solution.py:360
  181.9 39.2 %all-to-all-start = ((f32[64,1,128]{2,1,0:T(1,128)}), f32[64,1,128]{2,1,0:T(1,128)S(1)}, u32[]{:S(2)}, u32[]{:S(2)}) async-start(f32[64,1,128]{2,1,0:T(1,128)} %broadcast_in_dim.9), calls=%async_computation | async-start | bytes 65536 | tf_op jit(solution)/shard_map/all_to_all | solution.py:371
  (19 other events, 151.4 us)

commit v2 on v1

--- a/solution.py
+++ b/solution.py
@@ -39,18 +39,20 @@
     return center, beside
 
 
-def dot_exact(x, table):
+def dot_exact(x, table, side=0):
     high = x.astype(jnp.bfloat16)
     rest = x - high.astype(jnp.float32)
     middle = rest.astype(jnp.bfloat16)
     low = (rest - middle.astype(jnp.float32)).astype(jnp.bfloat16)
-    dot = functools.partial(jnp.dot, preferred_element_type=jnp.float32)
-    return dot(high, table) + dot(middle, table) + dot(low, table)
+    parts = jnp.concatenate([high, middle, low], 0)
+    out = lax.dot_general(parts, table, (((1,), (side,)), ((), ())), preferred_element_type=jnp.float32)
+    rows = x.shape[0]
+    return out[:rows] + out[rows : 2 * rows] + out[2 * rows :]
 
 
 def pair_up(sums_ref, plane, table_ref, out_ref, scale=1.0):
     nc, _, nz = sums_ref.shape[1:]
-    step = min(nc, 8)
+    step = min(nc, 32)
 
     def body(i):
         at = i * step
@@ -181,36 +183,52 @@
 
 def correct(corrections, table, C):
     nc, _, nz = C.shape[1:]
-    step = min(nc, 8)
+    step = min(nc, 32)
     for k in range(3):
         def body(i, k=k):
             at = i * step
             block = corrections[k][pl.ds(at, step)].reshape(step * 8, nz // 2)
-            C[k, pl.ds(at, step)] = dot_exact(block, table[...]).reshape(step, 8, nz)
+            C[k, pl.ds(at, step)] = dot_exact(block, table[...], 1).reshape(step, 8, nz)
 
         loop(nc // step, body, 1)
 
 
-def smoothed(W, V, force, nj):
+def spread_planes(start, weight, force, C, W, U, nj):
     half = nj // 2
-    for k in range(4):
+    for k in range(6):
         for h in range(2):
             def body(i, k=k, h=h):
-                j = h * half + 2 * i
-                center, beside = across(W, k + 1, j, 2)
-                beside = beside + W[k, pl.ds(j + 1, 2)] + W[k + 2, pl.ds(j + 1, 2)]
-                value = (1.0 - 6.0 * KAPPA) * center + KAPPA * (force[k][h][pl.ds(2 * i, 2)] + beside)
-                V[k, pl.ds(j + 1, 2)] = value
-
-            loop(half // 2, body, 8)
+                extra = C[k // 2, h * (half // 2) + i]
+                at = pl.ds(h * half + 2 * i + 1, 2)
+                W[k, at] = weight * start[k][h][pl.ds(2 * i, 2)] + extra[None]
+                if 1 <= k <= 4:
+                    U[k - 1, at] = KAPPA * force[k - 1][h][pl.ds(2 * i, 2)]
+
+            loop(half // 2, body, 4)
+        if 1 <= k <= 4:
+            fill_ends(W, k, nj)
+
+
+def smoothed(W, V, U, nj):
+    def plane(k):
+        def body(i):
+            j = 2 * i
+            center, beside = across(W, k + 1, j, 2)
+            at = pl.ds(j + 1, 2)
+            beside = beside + W[k, at] + W[k + 2, at]
+            V[k, at] = (1.0 - 6.0 * KAPPA) * center + U[k, at] + KAPPA * beside
+
+        loop(nj // 2, body, 8)
         fill_ends(V, k, nj)
 
-
-def residual_rows(V, x, h, i, force, half):
-    j = h * half + 2 * i
+    loop(4, plane, 1)
+
+
+def residual_rows(V, U, x, j):
     center, beside = across(V, x + 1, j, 2)
-    beside = beside + V[x, pl.ds(j + 1, 2)] + V[x + 2, pl.ds(j + 1, 2)]
-    return center, force[x + 1][h][pl.ds(2 * i, 2)] - (6.0 * center - beside)
+    at = pl.ds(j + 1, 2)
+    beside = beside + V[x, at] + V[x + 2, at]
+    return center, (1.0 / KAPPA) * U[x + 1, at] - (6.0 * center - beside)
 
 
 def fold_row(value):
@@ -228,76 +246,61 @@
     return tuple((refs[2 * k], refs[2 * k + 1]) for k in range(len(refs) // 2))
 
 
+def add_figures(acc, residue, shift):
+    offset = residue - shift[...][None]
+    acc[0] += offset[0] + offset[1]
+    acc[1] += offset[0] * offset[0] + offset[1] * offset[1]
+
+
 def middle_kernel(*refs):
     (left, own, right), rest = tuple(halves(refs[4 * k : 4 * k + 4]) for k in range(3)), refs[12:]
-    c_own, c_left, c_right, shift, table, pairs, v00, v01, v10, v11, s0, s1, stats, W, V, C, G, acc = rest
+    c_own, c_left, c_right, shift, table, v00, v01, v10, v11, s0, s1, stats, W, V, U, C, G, acc = rest
     nj = W.shape[1] - 2
     half = nj // 2
     outs = ((v00, v01), (v10, v11))
     force = left + own + right
     correct((c_left, c_own, c_right), table, C)
-    for k in range(6):
-        for h in range(2):
-            def body(i, k=k, h=h):
-                extra = C[k // 2, h * (half // 2) + i]
-                value = KAPPA * force[k][h][pl.ds(2 * i, 2)]
-                W[k, pl.ds(h * half + 2 * i + 1, 2)] = value + extra[None]
-
-            loop(half // 2, body, 8)
-        if 1 <= k <= 4:
-            fill_ends(W, k, nj)
-    smoothed(W, V, force[1:5], nj)
+    spread_planes(force, KAPPA, force[1:5], C, W, U, nj)
+    smoothed(W, V, U, nj)
     acc[...] = jnp.zeros_like(acc)
     for x in range(2):
         for h in range(2):
             def body(i, x=x, h=h):
-                center, residue = residual_rows(V, x, h, i, force[1:5], half)
+                center, residue = residual_rows(V, U, x, h * half + 2 * i)
                 value = center + KAPPA * residue
                 outs[x][h][pl.ds(2 * i, 2)] = value
                 G[x, h * (half // 2) + i] = value[0] + value[1]
-                offset = residue - shift[...][None]
-                acc[0] += offset[0] + offset[1]
-                acc[1] += offset[0] * offset[0] + offset[1] * offset[1]
-
-            loop(half // 2, body, 8)
+                add_figures(acc, residue, shift)
+
+            loop(half // 2, body, 4)
     zero = jnp.zeros((1, LANES), jnp.float32)
     stats[...] = stats_row(zero, zero, zero, zero, fold_row(acc[0]), fold_row(acc[1]))
-    pair_up(G, 0, pairs, s0)
-    pair_up(G, 1, pairs, s1)
+    pair_up(G, 0, table, s0)
+    pair_up(G, 1, table, s1)
 
 
 def last_kernel(*refs):
     f_left, f_right = halves(refs[0:2]), halves(refs[2:4])
     f_own = halves(refs[4:8])
     v_left, v_own, v_right = (halves(refs[4 * k + 8 : 4 * k + 12]) for k in range(3))
-    c_own, c_left, c_right, shift, total, first, table, out, stats, W, V, C, acc = refs[20:]
+    c_own, c_left, c_right, shift, total, first, table, out, stats, W, V, U, C, acc = refs[20:]
     nj = W.shape[1] - 2
-    half = nj // 2
-    force = f_left + f_own + f_right
-    start = v_left + v_own + v_right
     correct((c_left, c_own, c_right), table, C)
-    for k in range(6):
-        for h in range(2):
-            def body(i, k=k, h=h):
-                extra = C[k // 2, h * (half // 2) + i]
-                W[k, pl.ds(h * half + 2 * i + 1, 2)] = start[k][h][pl.ds(2 * i, 2)] + extra[None]
-
-            loop(half // 2, body, 8)
-        if 1 <= k <= 4:
-            fill_ends(W, k, nj)
-    smoothed(W, V, force, nj)
+    spread_planes(v_left + v_own + v_right, 1.0, f_left + f_own + f_right, C, W, U, nj)
+    smoothed(W, V, U, nj)
     acc[...] = jnp.zeros_like(acc)
-    for x in range(2):
-        for h in range(2):
-            def body(i, x=x, h=h):
-                center, residue = residual_rows(V, x, h, i, force, half)
-                out[x, pl.ds(h * half + 2 * i, 2)] = center
-                offset = residue - shift[...][None]
-                acc[0] += offset[0] + offset[1]
-                acc[1] += offset[0] * offset[0] + offset[1] * offset[1]
-
-            loop(half // 2, body, 8)
-    stats[...] = stats_row(first[...], fold_row(total[...]), fold_row(acc[0]), fold_row(acc[1]))
+
+    def plane(x):
+        def body(i):
+            center, residue = residual_rows(V, U, x, 2 * i)
+            out[x, pl.ds(2 * i, 2)] = center
+            add_figures(acc, residue, shift)
+
+        loop(nj // 2, body, 8)
+
+    loop(2, plane, 1)
+    row = stats_row(first[...], fold_row(total[...]), fold_row(acc[0]), fold_row(acc[1]))
+    stats[...] = jnp.broadcast_to(row[None], stats.shape)
 
 
 def natural_kernel(field, out, T):
@@ -365,10 +368,8 @@
     return lax.ppermute(x, "gx", [((i + 1) % count, i) for i in range(count)])
 
 
-def gathered(row):
-    count = lax.axis_size("gx")
-    spread = jnp.broadcast_to(row, (count, *row.shape[1:]))
-    return lax.all_to_all(spread, "gx", 0, 0, tiled=True)
+def gathered(rows):
+    return lax.all_to_all(rows, "gx", 0, 0, tiled=True)
 
 
 def coarse_beside(field):
@@ -408,12 +409,12 @@
     share = float(potential.size)
     columns = np.arange(nz)[:, None] // 2 == np.arange(width)[None, :]
     pairs = jnp.asarray(columns, jnp.bfloat16)
-    copies = jnp.asarray(columns.T, jnp.bfloat16)
     chunk = (nj // 2, 8, nz)
     coarse = (nc, 8, width)
     tall = (nj + 2, 8, nz)
 
-    left = from_left(potential[1:])
+    tail, potential = lax.optimization_barrier((potential[1:], potential))
+    left = from_left(tail)
     right = from_right(potential[:1])
     tiles = (nz // LANES, ny, LANES)
     prepared = call(
@@ -428,9 +429,9 @@
         rhs_first_kernel, (*forcing, pairs), [coarse], [(1, *tall), (1, nc, 8, nz)], 3 * 10**7
     )
     correction, f_left, f_right = coarse_part(local, s0, s1, KAPPA, forcing)
-    scratch = [(6, *tall), (4, *tall), (3, nc, 8, nz)]
+    scratch = [(6, *tall), (4, *tall), (4, *tall), (3, nc, 8, nz)]
     *field, s0, s1, first = call(
-        middle_kernel, (*f_left, *forcing, *f_right, *correction, shift, copies, pairs),
+        middle_kernel, (*f_left, *forcing, *f_right, *correction, shift, pairs),
         [chunk] * 4 + [coarse] * 2 + [(1, LANES)], [*scratch, (2, nc, 8, nz), (2, 8, nz)], 10**8,
     )
     (local,) = call(
@@ -439,12 +440,12 @@
     correction, v_left, v_right = coarse_part(local, s0, s1, 1.0, field)
     result, last = call(
         last_kernel,
-        (*f_left[2:], *f_right[:2], *forcing, *v_left, *field, *v_right, *correction, shift, total, first, copies),
-        [(2, nj, 8, nz), (1, LANES)], [*scratch, (2, 8, nz)], 10**8,
+        (*f_left[2:], *f_right[:2], *forcing, *v_left, *field, *v_right, *correction, shift, total, first, pairs),
+        [(2, nj, 8, nz), (lax.axis_size("gx"), 1, LANES)], [*scratch, (2, 8, nz)], 10**8,
     )
     (result,) = call(natural_kernel, (result,), [potential.shape], [tiles], 3 * 10**7)
     result, norms = call(
-        functools.partial(finish_kernel, share), (gathered(last), result),
+        functools.partial(finish_kernel, share), (gathered(last).reshape(-1, LANES), result),
         [potential.shape, (CYCLES,)], [], 10**7, [VMEM, SMEM],
     )
     return (result, norms)

time: 225 us -> 217 us (0.964)
  Pallas kernels: 41 us -> 33.8 us
    pallas_call x8, Pallas kernels: 41 us -> 33.8 us  [call(): pl.pallas_call(kernel, out_shape=[jax.ShapeDtypeStruct(o, jnp.float32) fo...]
    unnamed x24 -> x20, local copies, waits for them, and re-layouts: 7.8 us -> 7.29 us
where the time goes in v2:
time: 217 us; the launch traced here: 216 us
  starting transfers between devices  107 us (49%)
  waiting for transfers between devices  60.1 us (28%)
  Pallas kernels  33.8 us (16%)
  local copies, waits for them, and re-layouts  10.4 us (5%)
  other arithmetic  2.84 us (1%)
    ppermute x19, starting transfers between devices, from_right(): return lax.ppermute(x, 'gx', [((i + 1) % count, i) for i in range(count)])  81.1 us
    pallas_call x8, Pallas kernels, call(): pl.pallas_call(kernel, out_shape=[jax.ShapeDtypeStruct(o, jnp.float32) fo...  33.8 us
    ppermute x19, waiting for transfers between devices, from_left(): return lax.ppermute(x, 'gx', [(i, (i + 1) % count) for i in range(count)])  27.5 us
    all_to_all x1, waiting for transfers between devices, gathered(): return lax.all_to_all(rows, 'gx', 0, 0, tiled=True)  18.1 us
    all_to_all x1, starting transfers between devices, gathered(): return lax.all_to_all(rows, 'gx', 0, 0, tiled=True)  17.1 us
    ppermute x19, waiting for transfers between devices, from_right(): return lax.ppermute(x, 'gx', [((i + 1) % count, i) for i in range(count)])  14.5 us
    ppermute x19, starting transfers between devices, from_left(): return lax.ppermute(x, 'gx', [(i, (i + 1) % count) for i in range(count)])  9.21 us
    unnamed x20, local copies, waits for them, and re-layouts  7.29 us
  transfers between devices with their start and end apart: 39, of which 16 were waited for; matrix products, arithmetic and copies ran while one was open for 2% of the time, Pallas kernels for 4%

profile of v2, /device:TPU:37, one launch (start us, length us, event | category | flops | bytes accessed | tf_op | source)
XLA Modules:
  0.0 216.3 jit_solution(6496079068321887363)
XLA Ops:
  2.6 20.5 %collective-permute-start.1 = (f32[1,512,512]{2,1,0:T(8,128)S(1)}, f32[1,512,512]{2,1,0:T(8,128)S(1)}, u32[]{:S(2)}, u32[]{:S(2)}) collective-permute-start(f32[1,512,512]{2,1,0:T(8,128)S(1)} %slice.231), channel_id=1, source_target_pairs={{1,0},{2,1},{3,2},{4,3},{5,4},{6,5},{7,6},{8,7},{9,8},{10,9},{11,1... | collective-permute-start | bytes 3145736 | tf_op jit(solution)/shard_map/ppermute | solution.py:368
  23.1 3.7 %shard_map.41 = (f32[2,66,8,512]{3,2,1,0:T(8,128)S(1)}, f32[2,66,8,512]{3,2,1,0:T(8,128)S(1)}, f32[2,64,8,512]{3,2,1,0:T(8,128)S(1)}, f32[2,64,8,512]{3,2,1,0:T(8,128)S(1)}) custom-call(f32[2,512,512]{2,1,0:T(8,128)S(1)} %copy-done), custom_call_target="tpu_custom_call" | custom-call | flops 100000000 | bytes 10616832 | tf_op jit(solution)/shard_map/pallas_call | solution.py:350
  26.8 8.0 %collective-permute-done.left = f32[1,512,512]{2,1,0:T(8,128)S(1)} collective-permute-done((f32[1,512,512]{2,1,0:T(8,128)S(1)}, f32[1,512,512]{2,1,0:T(8,128)S(1)}, u32[]{:S(2)}, u32[]{:S(2)}) %collective-permute-start) | collective-permute-done | bytes 1048608 | tf_op jit(solution)/shard_map/ppermute | solution.py:363
  34.8 3.7 %shard_map.42 = (f32[32,8,512]{2,1,0:T(8,128)S(1)}, f32[32,8,512]{2,1,0:T(8,128)S(1)}, f32[32,8,512]{2,1,0:T(8,128)S(1)}, f32[32,8,512]{2,1,0:T(8,128)S(1)}, f32...) custom-call(f32[2,66,8,512]{3,2,1,0:T(8,128)S(1)} %get-tuple-element.25.X, ...), custom_call_target="tpu_custom_call" | custom-call | flops 100000000 | bytes 13766656 | tf_op jit(solution)/shard_map/pallas_call | solution.py:350
  38.5 2.5 %collective-permute-start.10 = (f32[32,8,256]{2,1,0:T(8,128)S(1)}, f32[32,8,256]{2,1,0:T(8,128)S(1)}, u32[]{:S(2)}, u32[]{:S(2)}) collective-permute-start(f32[32,8,256]{2,1,0:T(8,128)S(1)} %get-tuple-element.34), channel_id=1, source_target_pairs={{0,1},{1,2},{2,3},{3,4},{4,5},{5,6},{6,7},{7,8},{8,9},{9,10},{10,1... | collective-permute-start | bytes 786440 | tf_op jit(solution)/shard_map/ppermute | solution.py:363
  41.0 4.8 %collective-permute-start.11 = (f32[32,8,256]{2,1,0:T(8,128)S(1)}, f32[32,8,256]{2,1,0:T(8,128)S(1)}, u32[]{:S(2)}, u32[]{:S(2)}) collective-permute-start(f32[32,8,256]{2,1,0:T(8,128)S(1)} %get-tuple-element.35), channel_id=1, source_target_pairs={{1,0},{2,1},{3,2},{4,3},{5,4},{6,5},{7,6},{8,7},{9,8},{10,9},{11,1... | collective-permute-start | bytes 786440 | tf_op jit(solution)/shard_map/ppermute | solution.py:368
  45.9 2.9 %collective-permute-start.8 = (f32[32,8,512]{2,1,0:T(8,128)S(1)}, f32[32,8,512]{2,1,0:T(8,128)S(1)}, u32[]{:S(2)}, u32[]{:S(2)}) collective-permute-start(f32[32,8,512]{2,1,0:T(8,128)S(1)} %get-tuple-element.30.f10.refs_6_), channel_id=1, source_target_pairs={{1,0},{2,1},{3,2},{4,3},{5,4},{6,5},{7,6},{8,7},{9,8},{10,9},{11,1... | collective-permute-start | bytes 1572872 | tf_op jit(solution)/shard_map/ppermute | solution.py:368
  53.6 4.1 %collective-permute-done.12 = f32[32,8,256]{2,1,0:T(8,128)S(1)} collective-permute-done((f32[32,8,256]{2,1,0:T(8,128)S(1)}, f32[32,8,256]{2,1,0:T(8,128)S(1)}, u32[]{:S(2)}, u32[]{:S(2)}) %collective-permute-start.12) | collective-permute-done | bytes 262176 | tf_op jit(solution)/shard_map/ppermute | solution.py:363
  57.7 5.2 %collective-permute-done.13 = f32[32,8,256]{2,1,0:T(8,128)S(1)} collective-permute-done((f32[32,8,256]{2,1,0:T(8,128)S(1)}, f32[32,8,256]{2,1,0:T(8,128)S(1)}, u32[]{:S(2)}, u32[]{:S(2)}) %collective-permute-start.13) | collective-permute-done | bytes 262176 | tf_op jit(solution)/shard_map/ppermute | solution.py:368
  63.3 3.8 %collective-permute-start.15 = (f32[32,8,256]{2,1,0:T(8,128)S(1)}, f32[32,8,256]{2,1,0:T(8,128)S(1)}, u32[]{:S(2)}, u32[]{:S(2)}) collective-permute-start(f32[32,8,256]{2,1,0:T(8,128)S(1)} %fusion.4), channel_id=1, source_target_pairs={{1,0},{2,1},{3,2},{4,3},{5,4},{6,5},{7,6},{8,7},{9,8},{10,9},{11,1... | collective-permute-start | bytes 786440 | tf_op jit(solution)/shard_map/ppermute | solution.py:368
  69.5 5.2 %collective-permute-start.17 = (f32[32,8,256]{2,1,0:T(8,128)S(1)}, f32[32,8,256]{2,1,0:T(8,128)S(1)}, u32[]{:S(2)}, u32[]{:S(2)}) collective-permute-start(f32[32,8,256]{2,1,0:T(8,128)S(1)} %fusion.9), channel_id=1, source_target_pairs={{1,0},{2,1},{3,2},{4,3},{5,4},{6,5},{7,6},{8,7},{9,8},{10,9},{11,1... | collective-permute-start | bytes 786440 | tf_op jit(solution)/shard_map/ppermute | solution.py:368
  75.2 3.1 %collective-permute-start.4 = (f32[32,8,512]{2,1,0:T(8,128)S(1)}, f32[32,8,512]{2,1,0:T(8,128)}, u32[]{:S(2)}, u32[]{:S(2)}) collective-permute-start(f32[32,8,512]{2,1,0:T(8,128)S(1)} %get-tuple-element.32.f00.refs_4_), channel_id=1, source_target_pairs={{1,0},{2,1},{3,2},{4,3},{5,4},{6,5},{7,6},{8,7},{9,8},{10,9},{11,1... | collective-permute-start | bytes 1572872 | tf_op jit(solution)/shard_map/ppermute | solution.py:368
  78.2 3.5 %collective-permute-start.5 = (f32[32,8,512]{2,1,0:T(8,128)S(1)}, f32[32,8,512]{2,1,0:T(8,128)}, u32[]{:S(2)}, u32[]{:S(2)}) collective-permute-start(f32[32,8,512]{2,1,0:T(8,128)S(1)} %get-tuple-element.33.f01.refs_5_), channel_id=1, source_target_pairs={{1,0},{2,1},{3,2},{4,3},{5,4},{6,5},{7,6},{8,7},{9,8},{10,9},{11,1... | collective-permute-start | bytes 1572872 | tf_op jit(solution)/shard_map/ppermute | solution.py:368
  82.6 5.2 %collective-permute-start.19 = (f32[32,8,256]{2,1,0:T(8,128)}, f32[32,8,256]{2,1,0:T(8,128)}, u32[]{:S(2)}, u32[]{:S(2)}) collective-permute-start(f32[32,8,256]{2,1,0:T(8,128)} %fusion.14.refs_12_), channel_id=1, source_target_pairs={{1,0},{2,1},{3,2},{4,3},{5,4},{6,5},{7,6},{8,7},{9,8},{10,9},{11,1... | collective-permute-start | bytes 786440 | tf_op jit(solution)/shard_map/ppermute | solution.py:368
  92.5 3.1 %collective-permute-done.18.refs_13_ = f32[32,8,256]{2,1,0:T(8,128)} collective-permute-done((f32[32,8,256]{2,1,0:T(8,128)}, f32[32,8,256]{2,1,0:T(8,128)}, u32[]{:S(2)}, u32[]{:S(2)}) %collective-permute-start.18) | collective-permute-done | bytes 262176 | tf_op jit(solution)/shard_map/ppermute | solution.py:363
  98.8 9.8 %shard_map.44 = (f32[32,8,512]{2,1,0:T(8,128)S(1)}, f32[32,8,512]{2,1,0:T(8,128)S(1)}, f32[32,8,512]{2,1,0:T(8,128)S(1)}, f32[32,8,512]{2,1,0:T(8,128)S(1)}, f32...) custom-call(f32[32,8,512]{2,1,0:T(8,128)S(1)} %copy-done.9, ...), custom_call_target="tpu_custom_call" | custom-call | flops 100000000 | bytes 10240512 | tf_op jit(solution)/shard_map/pallas_call | solution.py:350
  108.6 2.2 %collective-permute-start.28 = (f32[32,8,256]{2,1,0:T(8,128)S(1)}, f32[32,8,256]{2,1,0:T(8,128)S(1)}, u32[]{:S(2)}, u32[]{:S(2)}) collective-permute-start(f32[32,8,256]{2,1,0:T(8,128)S(1)} %get-tuple-element.41), channel_id=1, source_target_pairs={{0,1},{1,2},{2,3},{3,4},{4,5},{5,6},{6,7},{7,8},{8,9},{9,10},{10,1... | collective-permute-start | bytes 786440 | tf_op jit(solution)/shard_map/ppermute | solution.py:363
  110.8 4.3 %collective-permute-start.29 = (f32[32,8,256]{2,1,0:T(8,128)S(1)}, f32[32,8,256]{2,1,0:T(8,128)S(1)}, u32[]{:S(2)}, u32[]{:S(2)}) collective-permute-start(f32[32,8,256]{2,1,0:T(8,128)S(1)} %get-tuple-element.42), channel_id=1, source_target_pairs={{1,0},{2,1},{3,2},{4,3},{5,4},{6,5},{7,6},{8,7},{9,8},{10,9},{11,1... | collective-permute-start | bytes 786440 | tf_op jit(solution)/shard_map/ppermute | solution.py:368
  115.1 2.9 %collective-permute-start.24 = (f32[32,8,512]{2,1,0:T(8,128)S(1)}, f32[32,8,512]{2,1,0:T(8,128)S(1)}, u32[]{:S(2)}, u32[]{:S(2)}) collective-permute-start(f32[32,8,512]{2,1,0:T(8,128)S(1)} %get-tuple-element.37.v00.refs_12_), channel_id=1, source_target_pairs={{1,0},{2,1},{3,2},{4,3},{5,4},{6,5},{7,6},{8,7},{9,8},{10,9},{11,1... | collective-permute-start | bytes 1572872 | tf_op jit(solution)/shard_map/ppermute | solution.py:368
  122.8 4.1 %collective-permute-done.30 = f32[32,8,256]{2,1,0:T(8,128)S(1)} collective-permute-done((f32[32,8,256]{2,1,0:T(8,128)S(1)}, f32[32,8,256]{2,1,0:T(8,128)S(1)}, u32[]{:S(2)}, u32[]{:S(2)}) %collective-permute-start.30) | collective-permute-done | bytes 262176 | tf_op jit(solution)/shard_map/ppermute | solution.py:363
  126.9 5.2 %collective-permute-done.31 = f32[32,8,256]{2,1,0:T(8,128)S(1)} collective-permute-done((f32[32,8,256]{2,1,0:T(8,128)S(1)}, f32[32,8,256]{2,1,0:T(8,128)S(1)}, u32[]{:S(2)}, u32[]{:S(2)}) %collective-permute-start.31) | collective-permute-done | bytes 262176 | tf_op jit(solution)/shard_map/ppermute | solution.py:368
  132.5 3.8 %collective-permute-start.33 = (f32[32,8,256]{2,1,0:T(8,128)S(1)}, f32[32,8,256]{2,1,0:T(8,128)S(1)}, u32[]{:S(2)}, u32[]{:S(2)}) collective-permute-start(f32[32,8,256]{2,1,0:T(8,128)S(1)} %fusion.19), channel_id=1, source_target_pairs={{1,0},{2,1},{3,2},{4,3},{5,4},{6,5},{7,6},{8,7},{9,8},{10,9},{11,1... | collective-permute-start | bytes 786440 | tf_op jit(solution)/shard_map/ppermute | solution.py:368
  138.6 5.2 %collective-permute-start.35 = (f32[32,8,256]{2,1,0:T(8,128)S(1)}, f32[32,8,256]{2,1,0:T(8,128)S(1)}, u32[]{:S(2)}, u32[]{:S(2)}) collective-permute-start(f32[32,8,256]{2,1,0:T(8,128)S(1)} %fusion.24), channel_id=1, source_target_pairs={{1,0},{2,1},{3,2},{4,3},{5,4},{6,5},{7,6},{8,7},{9,8},{10,9},{11,1... | collective-permute-start | bytes 786440 | tf_op jit(solution)/shard_map/ppermute | solution.py:368
  144.2 3.1 %collective-permute-start.26 = (f32[32,8,512]{2,1,0:T(8,128)S(1)}, f32[32,8,512]{2,1,0:T(8,128)S(1)}, u32[]{:S(2)}, u32[]{:S(2)}) collective-permute-start(f32[32,8,512]{2,1,0:T(8,128)S(1)} %get-tuple-element.39.v10.refs_14_), channel_id=1, source_target_pairs={{1,0},{2,1},{3,2},{4,3},{5,4},{6,5},{7,6},{8,7},{9,8},{10,9},{11,1... | collective-permute-start | bytes 1572872 | tf_op jit(solution)/shard_map/ppermute | solution.py:368
  147.2 3.5 %collective-permute-start.27 = (f32[32,8,512]{2,1,0:T(8,128)S(1)}, f32[32,8,512]{2,1,0:T(8,128)S(1)}, u32[]{:S(2)}, u32[]{:S(2)}) collective-permute-start(f32[32,8,512]{2,1,0:T(8,128)S(1)} %get-tuple-element.40.v11.refs_15_), channel_id=1, source_target_pairs={{1,0},{2,1},{3,2},{4,3},{5,4},{6,5},{7,6},{8,7},{9,8},{10,9},{11,1... | collective-permute-start | bytes 1572872 | tf_op jit(solution)/shard_map/ppermute | solution.py:368
  151.1 5.9 %collective-permute-start.37 = (f32[32,8,256]{2,1,0:T(8,128)S(1)}, f32[32,8,256]{2,1,0:T(8,128)S(1)}, u32[]{:S(2)}, u32[]{:S(2)}) collective-permute-start(f32[32,8,256]{2,1,0:T(8,128)S(1)} %fusion.29.refs_20_), channel_id=1, source_target_pairs={{1,0},{2,1},{3,2},{4,3},{5,4},{6,5},{7,6},{8,7},{9,8},{10,9},{11,1... | collective-permute-start | bytes 786440 | tf_op jit(solution)/shard_map/ppermute | solution.py:368
  158.7 2.8 %collective-permute-done.23.refs_11_ = f32[32,8,512]{2,1,0:T(8,128)S(1)} collective-permute-done((f32[32,8,512]{2,1,0:T(8,128)S(1)}, f32[32,8,512]{2,1,0:T(8,128)S(1)}, u32[]{:S(2)}, u32[]{:S(2)}) %collective-permute-start.23) | collective-permute-done | bytes 524320 | tf_op jit(solution)/shard_map/ppermute | solution.py:363
  161.5 2.8 %collective-permute-done.36.refs_21_ = f32[32,8,256]{2,1,0:T(8,128)S(1)} collective-permute-done((f32[32,8,256]{2,1,0:T(8,128)S(1)}, f32[32,8,256]{2,1,0:T(8,128)S(1)}, u32[]{:S(2)}, u32[]{:S(2)}) %collective-permute-start.36) | collective-permute-done | bytes 262176 | tf_op jit(solution)/shard_map/ppermute | solution.py:363
  164.3 8.9 %shard_map.46 = (f32[2,64,8,512]{3,2,1,0:T(8,128)S(1)}, f32[64,1,128]{2,1,0:T(1,128)}) custom-call(f32[32,8,512]{2,1,0:T(8,128)S(1)} %collective-permute-done.2.refs_2_.refs_0_, f32[32,8,512]{2,1,0:T(8,128)S(1)} %collective-permute-done.3.refs_3_.refs_1_, f32[32,8,512]{2,1,0:T(8,128)} %collective-permute-done.4.refs_8_.refs_2_, ...), custom_call_target="tpu_custom_call" | custom-call | flops 100000000 | bytes 13947392 | tf_op jit(solution)/shard_map/pallas_call | solution.py:350
  174.5 17.1 %all-to-all-start = ((f32[64,1,128]{2,1,0:T(1,128)}), f32[64,1,128]{2,1,0:T(1,128)S(1)}, u32[]{:S(2)}, u32[]{:S(2)}) async-start(f32[64,1,128]{2,1,0:T(1,128)} %get-tuple-element.44), calls=%async_computation | async-start | bytes 65536 | tf_op jit(solution)/shard_map/all_to_all | solution.py:372
  195.4 18.1 %all-to-all-done = f32[64,1,128]{2,1,0:T(1,128)S(1)} async-done(((f32[64,1,128]{2,1,0:T(1,128)}), f32[64,1,128]{2,1,0:T(1,128)S(1)}, u32[]{:S(2)}, u32[]{:S(2)}) %all-to-all-start) | async-done | bytes 32800 | tf_op jit(solution)/shard_map/all_to_all | solution.py:372
  213.5 2.9 %shard_map.48 = (f32[2,512,512]{2,1,0:T(8,128)}, f32[2]{0:T(128)}) custom-call(f32[64,128]{1,0:T(8,128)S(1)} %bitcast.1, f32[2,512,512]{2,1,0:T(8,128)S(1)} %shard_map.47.field), custom_call_target="tpu_custom_call" | custom-call | flops 10000000 | bytes 4227080 | tf_op jit(solution)/shard_map/pallas_call | solution.py:350
  (116 shorter events, 32.9 us)
Async XLA Ops:
  2.6 24.2 %collective-permute-start.1 = (f32[1,512,512]{2,1,0:T(8,128)S(1)}, f32[1,512,512]{2,1,0:T(8,128)S(1)}, u32[]{:S(2)}, u32[]{:S(2)}) collective-permute-start(f32[1,512,512]{2,1,0:T(8,128)S(1)} %slice.231), channel_id=1, source_target_pairs={{1,0},{2,1},{3,2},{4,3},{5,4},{6,5},{7,6},{8,7},{9,8},{10,9},{11,1... | collective-permute-start | bytes 3145736 | tf_op jit(solution)/shard_map/ppermute | solution.py:368
  23.1 11.7 %collective-permute-start = (f32[1,512,512]{2,1,0:T(8,128)S(1)}, f32[1,512,512]{2,1,0:T(8,128)S(1)}, u32[]{:S(2)}, u32[]{:S(2)}) collective-permute-start(f32[1,512,512]{2,1,0:T(8,128)S(1)} %slice.230), channel_id=1, source_target_pairs={{0,1},{1,2},{2,3},{3,4},{4,5},{5,6},{6,7},{7,8},{8,9},{9,10},{10,1... | collective-permute-start | bytes 3145736 | tf_op jit(solution)/shard_map/ppermute | solution.py:363
  38.5 12.1 %collective-permute-start.10 = (f32[32,8,256]{2,1,0:T(8,128)S(1)}, f32[32,8,256]{2,1,0:T(8,128)S(1)}, u32[]{:S(2)}, u32[]{:S(2)}) collective-permute-start(f32[32,8,256]{2,1,0:T(8,128)S(1)} %get-tuple-element.34), channel_id=1, source_target_pairs={{0,1},{1,2},{2,3},{3,4},{4,5},{5,6},{6,7},{7,8},{8,9},{9,10},{10,1... | collective-permute-start | bytes 786440 | tf_op jit(solution)/shard_map/ppermute | solution.py:363
  41.0 9.6 %collective-permute-start.11 = (f32[32,8,256]{2,1,0:T(8,128)S(1)}, f32[32,8,256]{2,1,0:T(8,128)S(1)}, u32[]{:S(2)}, u32[]{:S(2)}) collective-permute-start(f32[32,8,256]{2,1,0:T(8,128)S(1)} %get-tuple-element.35), channel_id=1, source_target_pairs={{1,0},{2,1},{3,2},{4,3},{5,4},{6,5},{7,6},{8,7},{9,8},{10,9},{11,1... | collective-permute-start | bytes 786440 | tf_op jit(solution)/shard_map/ppermute | solution.py:368
  45.9 29.1 %collective-permute-start.8 = (f32[32,8,512]{2,1,0:T(8,128)S(1)}, f32[32,8,512]{2,1,0:T(8,128)S(1)}, u32[]{:S(2)}, u32[]{:S(2)}) collective-permute-start(f32[32,8,512]{2,1,0:T(8,128)S(1)} %get-tuple-element.30.f10.refs_6_), channel_id=1, source_target_pairs={{1,0},{2,1},{3,2},{4,3},{5,4},{6,5},{7,6},{8,7},{9,8},{10,9},{11,1... | collective-permute-start | bytes 1572872 | tf_op jit(solution)/shard_map/ppermute | solution.py:368
  48.8 26.3 %collective-permute-start.2 = (f32[32,8,512]{2,1,0:T(8,128)S(1)}, f32[32,8,512]{2,1,0:T(8,128)S(1)}, u32[]{:S(2)}, u32[]{:S(2)}) collective-permute-start(f32[32,8,512]{2,1,0:T(8,128)S(1)} %get-tuple-element.30.f10.refs_6_), channel_id=1, source_target_pairs={{0,1},{1,2},{2,3},{3,4},{4,5},{5,6},{6,7},{7,8},{8,9},{9,10},{10,1... | collective-permute-start | bytes 1572872 | tf_op jit(solution)/shard_map/ppermute | solution.py:363
  48.8 26.4 %collective-permute-start.9 = (f32[32,8,512]{2,1,0:T(8,128)S(1)}, f32[32,8,512]{2,1,0:T(8,128)S(1)}, u32[]{:S(2)}, u32[]{:S(2)}) collective-permute-start(f32[32,8,512]{2,1,0:T(8,128)S(1)} %get-tuple-element.31.f11.refs_7_), channel_id=1, source_target_pairs={{1,0},{2,1},{3,2},{4,3},{5,4},{6,5},{7,6},{8,7},{9,8},{10,9},{11,1... | collective-permute-start | bytes 1572872 | tf_op jit(solution)/shard_map/ppermute | solution.py:368
  52.1 10.8 %collective-permute-start.13 = (f32[32,8,256]{2,1,0:T(8,128)S(1)}, f32[32,8,256]{2,1,0:T(8,128)S(1)}, u32[]{:S(2)}, u32[]{:S(2)}) collective-permute-start(f32[32,8,256]{2,1,0:T(8,128)S(1)} %get-tuple-element.48), channel_id=1, source_target_pairs={{1,0},{2,1},{3,2},{4,3},{5,4},{6,5},{7,6},{8,7},{9,8},{10,9},{11,1... | collective-permute-start | bytes 786440 | tf_op jit(solution)/shard_map/ppermute | solution.py:368
  69.4 8.8 %collective-permute-start.16 = (f32[32,8,256]{2,1,0:T(8,128)S(1)}, f32[32,8,256]{2,1,0:T(8,128)S(1)}, u32[]{:S(2)}, u32[]{:S(2)}) collective-permute-start(f32[32,8,256]{2,1,0:T(8,128)S(1)} %fusion.9), channel_id=1, source_target_pairs={{0,1},{1,2},{2,3},{3,4},{4,5},{5,6},{6,7},{7,8},{8,9},{9,10},{10,1... | collective-permute-start | bytes 786440 | tf_op jit(solution)/shard_map/ppermute | solution.py:363
  69.5 8.7 %collective-permute-start.17 = (f32[32,8,256]{2,1,0:T(8,128)S(1)}, f32[32,8,256]{2,1,0:T(8,128)S(1)}, u32[]{:S(2)}, u32[]{:S(2)}) collective-permute-start(f32[32,8,256]{2,1,0:T(8,128)S(1)} %fusion.9), channel_id=1, source_target_pairs={{1,0},{2,1},{3,2},{4,3},{5,4},{6,5},{7,6},{8,7},{9,8},{10,9},{11,1... | collective-permute-start | bytes 786440 | tf_op jit(solution)/shard_map/ppermute | solution.py:368
  75.0 7.7 %collective-permute-start.3 = (f32[32,8,512]{2,1,0:T(8,128)S(1)}, f32[32,8,512]{2,1,0:T(8,128)S(1)}, u32[]{:S(2)}, u32[]{:S(2)}) collective-permute-start(f32[32,8,512]{2,1,0:T(8,128)S(1)} %get-tuple-element.31.f11.refs_7_), channel_id=1, source_target_pairs={{0,1},{1,2},{2,3},{3,4},{4,5},{5,6},{6,7},{7,8},{8,9},{9,10},{10,1... | collective-permute-start | bytes 1572872 | tf_op jit(solution)/shard_map/ppermute | solution.py:363
  75.0 12.8 %collective-permute-start.6 = (f32[32,8,512]{2,1,0:T(8,128)S(1)}, f32[32,8,512]{2,1,0:T(8,128)S(1)}, u32[]{:S(2)}, u32[]{:S(2)}) collective-permute-start(f32[32,8,512]{2,1,0:T(8,128)S(1)} %get-tuple-element.32.f00.refs_4_), channel_id=1, source_target_pairs={{0,1},{1,2},{2,3},{3,4},{4,5},{5,6},{6,7},{7,8},{8,9},{9,10},{10,1... | collective-permute-start | bytes 1572872 | tf_op jit(solution)/shard_map/ppermute | solution.py:363
  75.2 16.2 %collective-permute-start.4 = (f32[32,8,512]{2,1,0:T(8,128)S(1)}, f32[32,8,512]{2,1,0:T(8,128)}, u32[]{:S(2)}, u32[]{:S(2)}) collective-permute-start(f32[32,8,512]{2,1,0:T(8,128)S(1)} %get-tuple-element.32.f00.refs_4_), channel_id=1, source_target_pairs={{1,0},{2,1},{3,2},{4,3},{5,4},{6,5},{7,6},{8,7},{9,8},{10,9},{11,1... | collective-permute-start | bytes 1572872 | tf_op jit(solution)/shard_map/ppermute | solution.py:368
  78.2 14.2 %collective-permute-start.7 = (f32[32,8,512]{2,1,0:T(8,128)S(1)}, f32[32,8,512]{2,1,0:T(8,128)}, u32[]{:S(2)}, u32[]{:S(2)}) collective-permute-start(f32[32,8,512]{2,1,0:T(8,128)S(1)} %get-tuple-element.33.f01.refs_5_), channel_id=1, source_target_pairs={{0,1},{1,2},{2,3},{3,4},{4,5},{5,6},{6,7},{7,8},{8,9},{9,10},{10,1... | collective-permute-start | bytes 1572872 | tf_op jit(solution)/shard_map/ppermute | solution.py:363
  78.2 14.2 %collective-permute-start.5 = (f32[32,8,512]{2,1,0:T(8,128)S(1)}, f32[32,8,512]{2,1,0:T(8,128)}, u32[]{:S(2)}, u32[]{:S(2)}) collective-permute-start(f32[32,8,512]{2,1,0:T(8,128)S(1)} %get-tuple-element.33.f01.refs_5_), channel_id=1, source_target_pairs={{1,0},{2,1},{3,2},{4,3},{5,4},{6,5},{7,6},{8,7},{9,8},{10,9},{11,1... | collective-permute-start | bytes 1572872 | tf_op jit(solution)/shard_map/ppermute | solution.py:368
  82.6 9.9 %collective-permute-start.19 = (f32[32,8,256]{2,1,0:T(8,128)}, f32[32,8,256]{2,1,0:T(8,128)}, u32[]{:S(2)}, u32[]{:S(2)}) collective-permute-start(f32[32,8,256]{2,1,0:T(8,128)} %fusion.14.refs_12_), channel_id=1, source_target_pairs={{1,0},{2,1},{3,2},{4,3},{5,4},{6,5},{7,6},{8,7},{9,8},{10,9},{11,1... | collective-permute-start | bytes 786440 | tf_op jit(solution)/shard_map/ppermute | solution.py:368
  108.6 11.2 %collective-permute-start.28 = (f32[32,8,256]{2,1,0:T(8,128)S(1)}, f32[32,8,256]{2,1,0:T(8,128)S(1)}, u32[]{:S(2)}, u32[]{:S(2)}) collective-permute-start(f32[32,8,256]{2,1,0:T(8,128)S(1)} %get-tuple-element.41), channel_id=1, source_target_pairs={{0,1},{1,2},{2,3},{3,4},{4,5},{5,6},{6,7},{7,8},{8,9},{9,10},{10,1... | collective-permute-start | bytes 786440 | tf_op jit(solution)/shard_map/ppermute | solution.py:363
  110.8 9.0 %collective-permute-start.29 = (f32[32,8,256]{2,1,0:T(8,128)S(1)}, f32[32,8,256]{2,1,0:T(8,128)S(1)}, u32[]{:S(2)}, u32[]{:S(2)}) collective-permute-start(f32[32,8,256]{2,1,0:T(8,128)S(1)} %get-tuple-element.42), channel_id=1, source_target_pairs={{1,0},{2,1},{3,2},{4,3},{5,4},{6,5},{7,6},{8,7},{9,8},{10,9},{11,1... | collective-permute-start | bytes 786440 | tf_op jit(solution)/shard_map/ppermute | solution.py:368
  115.1 29.0 %collective-permute-start.24 = (f32[32,8,512]{2,1,0:T(8,128)S(1)}, f32[32,8,512]{2,1,0:T(8,128)S(1)}, u32[]{:S(2)}, u32[]{:S(2)}) collective-permute-start(f32[32,8,512]{2,1,0:T(8,128)S(1)} %get-tuple-element.37.v00.refs_12_), channel_id=1, source_target_pairs={{1,0},{2,1},{3,2},{4,3},{5,4},{6,5},{7,6},{8,7},{9,8},{10,9},{11,1... | collective-permute-start | bytes 1572872 | tf_op jit(solution)/shard_map/ppermute | solution.py:368
  117.9 26.2 %collective-permute-start.20 = (f32[32,8,512]{2,1,0:T(8,128)S(1)}, f32[32,8,512]{2,1,0:T(8,128)S(1)}, u32[]{:S(2)}, u32[]{:S(2)}) collective-permute-start(f32[32,8,512]{2,1,0:T(8,128)S(1)} %get-tuple-element.37.v00.refs_12_), channel_id=1, source_target_pairs={{0,1},{1,2},{2,3},{3,4},{4,5},{5,6},{6,7},{7,8},{8,9},{9,10},{10,1... | collective-permute-start | bytes 1572872 | tf_op jit(solution)/shard_map/ppermute | solution.py:363
  117.9 29.3 %collective-permute-start.25 = (f32[32,8,512]{2,1,0:T(8,128)S(1)}, f32[32,8,512]{2,1,0:T(8,128)S(1)}, u32[]{:S(2)}, u32[]{:S(2)}) collective-permute-start(f32[32,8,512]{2,1,0:T(8,128)S(1)} %get-tuple-element.38.v01.refs_13_), channel_id=1, source_target_pairs={{1,0},{2,1},{3,2},{4,3},{5,4},{6,5},{7,6},{8,7},{9,8},{10,9},{11,1... | collective-permute-start | bytes 1572872 | tf_op jit(solution)/shard_map/ppermute | solution.py:368
  121.3 10.8 %collective-permute-start.31 = (f32[32,8,256]{2,1,0:T(8,128)S(1)}, f32[32,8,256]{2,1,0:T(8,128)S(1)}, u32[]{:S(2)}, u32[]{:S(2)}) collective-permute-start(f32[32,8,256]{2,1,0:T(8,128)S(1)} %get-tuple-element.46), channel_id=1, source_target_pairs={{1,0},{2,1},{3,2},{4,3},{5,4},{6,5},{7,6},{8,7},{9,8},{10,9},{11,1... | collective-permute-start | bytes 786440 | tf_op jit(solution)/shard_map/ppermute | solution.py:368
  138.6 8.7 %collective-permute-start.34 = (f32[32,8,256]{2,1,0:T(8,128)S(1)}, f32[32,8,256]{2,1,0:T(8,128)S(1)}, u32[]{:S(2)}, u32[]{:S(2)}) collective-permute-start(f32[32,8,256]{2,1,0:T(8,128)S(1)} %fusion.24), channel_id=1, source_target_pairs={{0,1},{1,2},{2,3},{3,4},{4,5},{5,6},{6,7},{7,8},{8,9},{9,10},{10,1... | collective-permute-start | bytes 786440 | tf_op jit(solution)/shard_map/ppermute | solution.py:363
  138.6 12.2 %collective-permute-start.35 = (f32[32,8,256]{2,1,0:T(8,128)S(1)}, f32[32,8,256]{2,1,0:T(8,128)S(1)}, u32[]{:S(2)}, u32[]{:S(2)}) collective-permute-start(f32[32,8,256]{2,1,0:T(8,128)S(1)} %fusion.24), channel_id=1, source_target_pairs={{1,0},{2,1},{3,2},{4,3},{5,4},{6,5},{7,6},{8,7},{9,8},{10,9},{11,1... | collective-permute-start | bytes 786440 | tf_op jit(solution)/shard_map/ppermute | solution.py:368
  144.1 7.0 %collective-permute-start.21 = (f32[32,8,512]{2,1,0:T(8,128)S(1)}, f32[32,8,512]{2,1,0:T(8,128)S(1)}, u32[]{:S(2)}, u32[]{:S(2)}) collective-permute-start(f32[32,8,512]{2,1,0:T(8,128)S(1)} %get-tuple-element.38.v01.refs_13_), channel_id=1, source_target_pairs={{0,1},{1,2},{2,3},{3,4},{4,5},{5,6},{6,7},{7,8},{8,9},{9,10},{10,1... | collective-permute-start | bytes 1572872 | tf_op jit(solution)/shard_map/ppermute | solution.py:363
  144.2 12.8 %collective-permute-start.26 = (f32[32,8,512]{2,1,0:T(8,128)S(1)}, f32[32,8,512]{2,1,0:T(8,128)S(1)}, u32[]{:S(2)}, u32[]{:S(2)}) collective-permute-start(f32[32,8,512]{2,1,0:T(8,128)S(1)} %get-tuple-element.39.v10.refs_14_), channel_id=1, source_target_pairs={{1,0},{2,1},{3,2},{4,3},{5,4},{6,5},{7,6},{8,7},{9,8},{10,9},{11,1... | collective-permute-start | bytes 1572872 | tf_op jit(solution)/shard_map/ppermute | solution.py:368
  147.2 9.7 %collective-permute-start.22 = (f32[32,8,512]{2,1,0:T(8,128)S(1)}, f32[32,8,512]{2,1,0:T(8,128)S(1)}, u32[]{:S(2)}, u32[]{:S(2)}) collective-permute-start(f32[32,8,512]{2,1,0:T(8,128)S(1)} %get-tuple-element.39.v10.refs_14_), channel_id=1, source_target_pairs={{0,1},{1,2},{2,3},{3,4},{4,5},{5,6},{6,7},{7,8},{8,9},{9,10},{10,1... | collective-permute-start | bytes 1572872 | tf_op jit(solution)/shard_map/ppermute | solution.py:363
  147.2 11.5 %collective-permute-start.27 = (f32[32,8,512]{2,1,0:T(8,128)S(1)}, f32[32,8,512]{2,1,0:T(8,128)S(1)}, u32[]{:S(2)}, u32[]{:S(2)}) collective-permute-start(f32[32,8,512]{2,1,0:T(8,128)S(1)} %get-tuple-element.40.v11.refs_15_), channel_id=1, source_target_pairs={{1,0},{2,1},{3,2},{4,3},{5,4},{6,5},{7,6},{8,7},{9,8},{10,9},{11,1... | collective-permute-start | bytes 1572872 | tf_op jit(solution)/shard_map/ppermute | solution.py:368
  150.8 10.7 %collective-permute-start.23 = (f32[32,8,512]{2,1,0:T(8,128)S(1)}, f32[32,8,512]{2,1,0:T(8,128)S(1)}, u32[]{:S(2)}, u32[]{:S(2)}) collective-permute-start(f32[32,8,512]{2,1,0:T(8,128)S(1)} %get-tuple-element.40.v11.refs_15_), channel_id=1, source_target_pairs={{0,1},{1,2},{2,3},{3,4},{4,5},{5,6},{6,7},{7,8},{8,9},{9,10},{10,1... | collective-permute-start | bytes 1572872 | tf_op jit(solution)/shard_map/ppermute | solution.py:363
  151.1 10.5 %collective-permute-start.37 = (f32[32,8,256]{2,1,0:T(8,128)S(1)}, f32[32,8,256]{2,1,0:T(8,128)S(1)}, u32[]{:S(2)}, u32[]{:S(2)}) collective-permute-start(f32[32,8,256]{2,1,0:T(8,128)S(1)} %fusion.29.refs_20_), channel_id=1, source_target_pairs={{1,0},{2,1},{3,2},{4,3},{5,4},{6,5},{7,6},{8,7},{9,8},{10,9},{11,1... | collective-permute-start | bytes 786440 | tf_op jit(solution)/shard_map/ppermute | solution.py:368
  156.9 7.4 %collective-permute-start.36 = (f32[32,8,256]{2,1,0:T(8,128)S(1)}, f32[32,8,256]{2,1,0:T(8,128)S(1)}, u32[]{:S(2)}, u32[]{:S(2)}) collective-permute-start(f32[32,8,256]{2,1,0:T(8,128)S(1)} %fusion.29.refs_20_), channel_id=1, source_target_pairs={{0,1},{1,2},{2,3},{3,4},{4,5},{5,6},{6,7},{7,8},{8,9},{9,10},{10,1... | collective-permute-start | bytes 786440 | tf_op jit(solution)/shard_map/ppermute | solution.py:363
  174.5 39.0 %all-to-all-start = ((f32[64,1,128]{2,1,0:T(1,128)}), f32[64,1,128]{2,1,0:T(1,128)S(1)}, u32[]{:S(2)}, u32[]{:S(2)}) async-start(f32[64,1,128]{2,1,0:T(1,128)} %get-tuple-element.44), calls=%async_computation | async-start | bytes 65536 | tf_op jit(solution)/shard_map/all_to_all | solution.py:372
  (17 other events, 111.0 us)

commit v3 on v2

--- a/solution.py
+++ b/solution.py
@@ -182,53 +182,69 @@
 
 
 def correct(corrections, table, C):
-    nc, _, nz = C.shape[1:]
-    step = min(nc, 32)
+    nc, nz = C.shape[1] - 2, C.shape[3]
     for k in range(3):
-        def body(i, k=k):
-            at = i * step
-            block = corrections[k][pl.ds(at, step)].reshape(step * 8, nz // 2)
-            C[k, pl.ds(at, step)] = dot_exact(block, table[...], 1).reshape(step, 8, nz)
-
-        loop(nc // step, body, 1)
-
-
-def spread_planes(start, weight, force, C, W, U, nj):
-    half = nj // 2
+        block = corrections[k][...].reshape(nc * 8, nz // 2)
+        C[k, pl.ds(1, nc)] = dot_exact(block, table[...], 1).reshape(nc, 8, nz)
+        fill_ends(C, k, nc)
+
+
+def sweep_kernel(first, *refs):
+    nj = refs[-1].shape[1] - 2
+    half = nj // 2
+    W, part = refs[-1], refs[-2]
+    start = halves(refs[:12])
+    force = None if first else halves(refs[12:20])
+    own, beside_weight = (1.0 - 6.0 * KAPPA, KAPPA)
+    if first:
+        own, beside_weight = own * KAPPA + KAPPA, KAPPA * KAPPA
     for k in range(6):
         for h in range(2):
-            def body(i, k=k, h=h):
-                extra = C[k // 2, h * (half // 2) + i]
-                at = pl.ds(h * half + 2 * i + 1, 2)
-                W[k, at] = weight * start[k][h][pl.ds(2 * i, 2)] + extra[None]
-                if 1 <= k <= 4:
-                    U[k - 1, at] = KAPPA * force[k - 1][h][pl.ds(2 * i, 2)]
-
-            loop(half // 2, body, 4)
+            def fill(i, k=k, h=h):
+                W[k, h * half + i + 1] = start[k][h][i]
+
+            loop(half, fill, 8)
         if 1 <= k <= 4:
             fill_ends(W, k, nj)
-
-
-def smoothed(W, V, U, nj):
-    def plane(k):
-        def body(i):
-            j = 2 * i
-            center, beside = across(W, k + 1, j, 2)
-            at = pl.ds(j + 1, 2)
-            beside = beside + W[k, at] + W[k + 2, at]
-            V[k, at] = (1.0 - 6.0 * KAPPA) * center + U[k, at] + KAPPA * beside
-
-        loop(nj // 2, body, 8)
+    for k in range(4):
+        for h in range(2):
+            def body(i, k=k, h=h):
+                j = h * half + 2 * i
+                center, beside = across(W, k + 1, j, 2)
+                at = pl.ds(j + 1, 2)
+                value = own * center + beside_weight * (beside + W[k, at] + W[k + 2, at])
+                if not first:
+                    value = value + KAPPA * force[k][h][pl.ds(2 * i, 2)]
+                part[k, pl.ds(j, 2)] = value
+
+            loop(half // 2, body, 8)
+
+
+def add_correction(part, C, V, nj):
+    def body(i):
+        planes = [C[a, pl.ds(i, 3)] for a in range(3)]
+        centers = [plane[1] for plane in planes]
+        sides = [KAPPA * (centers[a] + centers[a + 1]) for a in range(2)]
+        bases = [
+            (1.0 - 5.0 * KAPPA) * center + KAPPA * (rolled(center, 1, 1) + rolled(center, -1, 1)) for center in centers
+        ]
+        for k in range(4):
+            a = (k + 1) // 2
+            base = bases[a] + sides[k // 2]
+            for row in range(2):
+                V[k, 2 * i + row + 1] = part[k, 2 * i + row] + (base + KAPPA * planes[a][2 * row])
+
+    loop(nj // 2, body, 4)
+    for k in range(4):
         fill_ends(V, k, nj)
 
-    loop(4, plane, 1)
-
-
-def residual_rows(V, U, x, j):
+
+def residual_rows(V, force, x, h, i, half):
+    j = h * half + 2 * i
     center, beside = across(V, x + 1, j, 2)
     at = pl.ds(j + 1, 2)
     beside = beside + V[x, at] + V[x + 2, at]
-    return center, (1.0 / KAPPA) * U[x + 1, at] - (6.0 * center - beside)
+    return center, force[x][h][pl.ds(2 * i, 2)] - (6.0 * center - beside)
 
 
 def fold_row(value):
@@ -252,21 +268,20 @@
     acc[1] += offset[0] * offset[0] + offset[1] * offset[1]
 
 
-def middle_kernel(*refs):
-    (left, own, right), rest = tuple(halves(refs[4 * k : 4 * k + 4]) for k in range(3)), refs[12:]
-    c_own, c_left, c_right, shift, table, v00, v01, v10, v11, s0, s1, stats, W, V, U, C, G, acc = rest
-    nj = W.shape[1] - 2
-    half = nj // 2
+def middle_kernel(
+    f00, f01, f10, f11, part, c_own, c_left, c_right, shift, table, v00, v01, v10, v11, s0, s1, stats, V, C, G, acc
+):
+    nj = V.shape[1] - 2
+    half = nj // 2
+    force = ((f00, f01), (f10, f11))
     outs = ((v00, v01), (v10, v11))
-    force = left + own + right
     correct((c_left, c_own, c_right), table, C)
-    spread_planes(force, KAPPA, force[1:5], C, W, U, nj)
-    smoothed(W, V, U, nj)
+    add_correction(part, C, V, nj)
     acc[...] = jnp.zeros_like(acc)
     for x in range(2):
         for h in range(2):
             def body(i, x=x, h=h):
-                center, residue = residual_rows(V, U, x, h * half + 2 * i)
+                center, residue = residual_rows(V, force, x, h, i, half)
                 value = center + KAPPA * residue
                 outs[x][h][pl.ds(2 * i, 2)] = value
                 G[x, h * (half // 2) + i] = value[0] + value[1]
@@ -279,26 +294,23 @@
     pair_up(G, 1, table, s1)
 
 
-def last_kernel(*refs):
-    f_left, f_right = halves(refs[0:2]), halves(refs[2:4])
-    f_own = halves(refs[4:8])
-    v_left, v_own, v_right = (halves(refs[4 * k + 8 : 4 * k + 12]) for k in range(3))
-    c_own, c_left, c_right, shift, total, first, table, out, stats, W, V, U, C, acc = refs[20:]
-    nj = W.shape[1] - 2
+def last_kernel(
+    f00, f01, f10, f11, part, c_own, c_left, c_right, shift, total, first, table, out, stats, V, C, acc
+):
+    nj = V.shape[1] - 2
+    half = nj // 2
+    force = ((f00, f01), (f10, f11))
     correct((c_left, c_own, c_right), table, C)
-    spread_planes(v_left + v_own + v_right, 1.0, f_left + f_own + f_right, C, W, U, nj)
-    smoothed(W, V, U, nj)
+    add_correction(part, C, V, nj)
     acc[...] = jnp.zeros_like(acc)
-
-    def plane(x):
-        def body(i):
-            center, residue = residual_rows(V, U, x, 2 * i)
-            out[x, pl.ds(2 * i, 2)] = center
-            add_figures(acc, residue, shift)
-
-        loop(nj // 2, body, 8)
-
-    loop(2, plane, 1)
+    for x in range(2):
+        for h in range(2):
+            def body(i, x=x, h=h):
+                center, residue = residual_rows(V, force, x, h, i, half)
+                out[x, pl.ds(h * half + 2 * i, 2)] = center
+                add_figures(acc, residue, shift)
+
+            loop(half // 2, body, 4)
     row = stats_row(first[...], fold_row(total[...]), fold_row(acc[0]), fold_row(acc[1]))
     stats[...] = jnp.broadcast_to(row[None], stats.shape)
 
@@ -429,18 +441,25 @@
         rhs_first_kernel, (*forcing, pairs), [coarse], [(1, *tall), (1, nc, 8, nz)], 3 * 10**7
     )
     correction, f_left, f_right = coarse_part(local, s0, s1, KAPPA, forcing)
-    scratch = [(6, *tall), (4, *tall), (4, *tall), (3, nc, 8, nz)]
+    planes = (4, nj, 8, nz)
+    scratch = [(4, *tall), (3, nc + 2, 8, nz)]
+    (part,) = call(
+        functools.partial(sweep_kernel, True), (*f_left, *forcing, *f_right), [planes], [(6, *tall)], 10**8
+    )
     *field, s0, s1, first = call(
-        middle_kernel, (*f_left, *forcing, *f_right, *correction, shift, pairs),
+        middle_kernel, (*forcing, part, *correction, shift, pairs),
         [chunk] * 4 + [coarse] * 2 + [(1, LANES)], [*scratch, (2, nc, 8, nz), (2, 8, nz)], 10**8,
     )
     (local,) = call(
         rhs_later_kernel, (*forcing, *field, pairs), [coarse], [(1, *tall), (1, nc, 8, nz)], 3 * 10**7
     )
     correction, v_left, v_right = coarse_part(local, s0, s1, 1.0, field)
+    (part,) = call(
+        functools.partial(sweep_kernel, False),
+        (*v_left, *field, *v_right, *f_left[2:], *forcing, *f_right[:2]), [planes], [(6, *tall)], 10**8,
+    )
     result, last = call(
-        last_kernel,
-        (*f_left[2:], *f_right[:2], *forcing, *v_left, *field, *v_right, *correction, shift, total, first, pairs),
+        last_kernel, (*forcing, part, *correction, shift, total, first, pairs),
         [(2, nj, 8, nz), (lax.axis_size("gx"), 1, LANES)], [*scratch, (2, 8, nz)], 10**8,
     )
     (result,) = call(natural_kernel, (result,), [potential.shape], [tiles], 3 * 10**7)

time: 217 us -> 240 us (1.11)
  waiting for transfers between devices: 60.1 us -> 69.3 us
  starting transfers between devices: 107 us -> 115 us
  Pallas kernels: 33.8 us -> 37.2 us
  local copies, waits for them, and re-layouts: 10.4 us -> 12.8 us
    ppermute x19, waiting for transfers between devices: 14.5 us -> 25.1 us  [from_right(): return lax.ppermute(x, 'gx', [((i + 1) % count, i) for i in range(count)])]
    ppermute x19, starting transfers between devices: 81.1 us -> 85.5 us  [from_right(): return lax.ppermute(x, 'gx', [((i + 1) % count, i) for i in range(count)])]
    pallas_call x8 -> x10, Pallas kernels: 33.8 us -> 37.2 us  [call(): pl.pallas_call(kernel, out_shape=[jax.ShapeDtypeStruct(o, jnp.float32) fo...]
    ppermute x19, starting transfers between devices: 9.21 us -> 12.3 us  [from_left(): return lax.ppermute(x, 'gx', [(i, (i + 1) % count) for i in range(count)])]
    unnamed x20 -> x26, local copies, waits for them, and re-layouts: 7.29 us -> 9.75 us
  transfers between devices with their start and end apart: 39 -> 39, of which waited for: 16 -> 14; matrix products, arithmetic and copies ran while one was open for 2% -> 2% of each run, Pallas kernels for 4% -> 8%
where the time goes in v3:
time: 240 us; the launch traced here: 239 us
  starting transfers between devices  115 us (48%)
  waiting for transfers between devices  69.3 us (29%)
  Pallas kernels  37.2 us (16%)
  local copies, waits for them, and re-layouts  12.8 us (5%)
  other arithmetic  2.82 us (1%)
    ppermute x19, starting transfers between devices, from_right(): return lax.ppermute(x, 'gx', [((i + 1) % count, i) for i in range(count)])  85.5 us
    pallas_call x10, Pallas kernels, call(): pl.pallas_call(kernel, out_shape=[jax.ShapeDtypeStruct(o, jnp.float32) fo...  37.2 us
    ppermute x19, waiting for transfers between devices, from_left(): return lax.ppermute(x, 'gx', [(i, (i + 1) % count) for i in range(count)])  26.8 us
    ppermute x19, waiting for transfers between devices, from_right(): return lax.ppermute(x, 'gx', [((i + 1) % count, i) for i in range(count)])  25.1 us
    all_to_all x1, waiting for transfers between devices, gathered(): return lax.all_to_all(rows, 'gx', 0, 0, tiled=True)  17.4 us
    all_to_all x1, starting transfers between devices, gathered(): return lax.all_to_all(rows, 'gx', 0, 0, tiled=True)  17.3 us
    ppermute x19, starting transfers between devices, from_left(): return lax.ppermute(x, 'gx', [(i, (i + 1) % count) for i in range(count)])  12.3 us
    unnamed x26, local copies, waits for them, and re-layouts  9.75 us
  transfers between devices with their start and end apart: 39, of which 14 were waited for; matrix products, arithmetic and copies ran while one was open for 2% of the time, Pallas kernels for 8%

profile of v3, /device:TPU:37, one launch (start us, length us, event | category | flops | bytes accessed | tf_op | source)
XLA Modules:
  0.0 239.3 jit_solution(16001220784146851113)
XLA Ops:
  2.1 3.2 %collective-permute-start = (f32[1,512,512]{2,1,0:T(8,128)S(1)}, f32[1,512,512]{2,1,0:T(8,128)S(1)}, u32[]{:S(2)}, u32[]{:S(2)}) collective-permute-start(f32[1,512,512]{2,1,0:T(8,128)S(1)} %slice.230), channel_id=1, source_target_pairs={{0,1},{1,2},{2,3},{3,4},{4,5},{5,6},{6,7},{7,8},{8,9},{9,10},{10,1... | collective-permute-start | bytes 3145736 | tf_op jit(solution)/shard_map/ppermute | solution.py:375
  5.4 17.7 %collective-permute-start.1 = (f32[1,512,512]{2,1,0:T(8,128)S(1)}, f32[1,512,512]{2,1,0:T(8,128)S(1)}, u32[]{:S(2)}, u32[]{:S(2)}) collective-permute-start(f32[1,512,512]{2,1,0:T(8,128)S(1)} %slice.231), channel_id=1, source_target_pairs={{1,0},{2,1},{3,2},{4,3},{5,4},{6,5},{7,6},{8,7},{9,8},{10,9},{11,1... | collective-permute-start | bytes 3145736 | tf_op jit(solution)/shard_map/ppermute | solution.py:380
  23.1 3.7 %shard_map.41 = (f32[2,66,8,512]{3,2,1,0:T(8,128)S(1)}, f32[2,66,8,512]{3,2,1,0:T(8,128)S(1)}, f32[2,64,8,512]{3,2,1,0:T(8,128)S(1)}, f32[2,64,8,512]{3,2,1,0:T(8,128)S(1)}) custom-call(f32[2,512,512]{2,1,0:T(8,128)S(1)} %copy-done), custom_call_target="tpu_custom_call" | custom-call | flops 100000000 | bytes 10616832 | tf_op jit(solution)/shard_map/pallas_call | solution.py:362
  26.8 3.7 %shard_map.42 = (f32[32,8,512]{2,1,0:T(8,128)S(1)}, f32[32,8,512]{2,1,0:T(8,128)S(1)}, f32[32,8,512]{2,1,0:T(8,128)S(1)}, f32[32,8,512]{2,1,0:T(8,128)S(1)}, f32...) custom-call(f32[2,66,8,512]{3,2,1,0:T(8,128)S(1)} %get-tuple-element.25.X, ...), custom_call_target="tpu_custom_call" | custom-call | flops 100000000 | bytes 13766656 | tf_op jit(solution)/shard_map/pallas_call | solution.py:362
  30.6 12.1 %collective-permute-start.11 = (f32[32,8,256]{2,1,0:T(8,128)S(1)}, f32[32,8,256]{2,1,0:T(8,128)S(1)}, u32[]{:S(2)}, u32[]{:S(2)}) collective-permute-start(f32[32,8,256]{2,1,0:T(8,128)S(1)} %get-tuple-element.35), channel_id=1, source_target_pairs={{1,0},{2,1},{3,2},{4,3},{5,4},{6,5},{7,6},{8,7},{9,8},{10,9},{11,1... | collective-permute-start | bytes 786440 | tf_op jit(solution)/shard_map/ppermute | solution.py:380
  44.5 5.8 %collective-permute-start.13 = (f32[32,8,256]{2,1,0:T(8,128)S(1)}, f32[32,8,256]{2,1,0:T(8,128)S(1)}, u32[]{:S(2)}, u32[]{:S(2)}) collective-permute-start(f32[32,8,256]{2,1,0:T(8,128)S(1)} %get-tuple-element.48), channel_id=1, source_target_pairs={{1,0},{2,1},{3,2},{4,3},{5,4},{6,5},{7,6},{8,7},{9,8},{10,9},{11,1... | collective-permute-start | bytes 786440 | tf_op jit(solution)/shard_map/ppermute | solution.py:380
  50.4 12.6 %collective-permute-done.12 = f32[32,8,256]{2,1,0:T(8,128)S(1)} collective-permute-done((f32[32,8,256]{2,1,0:T(8,128)S(1)}, f32[32,8,256]{2,1,0:T(8,128)S(1)}, u32[]{:S(2)}, u32[]{:S(2)}) %collective-permute-start.12) | collective-permute-done | bytes 262176 | tf_op jit(solution)/shard_map/ppermute | solution.py:375
  63.3 2.5 %collective-permute-start.14 = (f32[32,8,256]{2,1,0:T(8,128)S(1)}, f32[32,8,256]{2,1,0:T(8,128)S(1)}, u32[]{:S(2)}, u32[]{:S(2)}) collective-permute-start(f32[32,8,256]{2,1,0:T(8,128)S(1)} %fusion.4), channel_id=1, source_target_pairs={{0,1},{1,2},{2,3},{3,4},{4,5},{5,6},{6,7},{7,8},{8,9},{9,10},{10,1... | collective-permute-start | bytes 786440 | tf_op jit(solution)/shard_map/ppermute | solution.py:375
  65.9 4.4 %collective-permute-start.15 = (f32[32,8,256]{2,1,0:T(8,128)S(1)}, f32[32,8,256]{2,1,0:T(8,128)S(1)}, u32[]{:S(2)}, u32[]{:S(2)}) collective-permute-start(f32[32,8,256]{2,1,0:T(8,128)S(1)} %fusion.4), channel_id=1, source_target_pairs={{1,0},{2,1},{3,2},{4,3},{5,4},{6,5},{7,6},{8,7},{9,8},{10,9},{11,1... | collective-permute-start | bytes 786440 | tf_op jit(solution)/shard_map/ppermute | solution.py:380
  72.2 5.6 %collective-permute-start.17 = (f32[32,8,256]{2,1,0:T(8,128)S(1)}, f32[32,8,256]{2,1,0:T(8,128)S(1)}, u32[]{:S(2)}, u32[]{:S(2)}) collective-permute-start(f32[32,8,256]{2,1,0:T(8,128)S(1)} %fusion.9), channel_id=1, source_target_pairs={{1,0},{2,1},{3,2},{4,3},{5,4},{6,5},{7,6},{8,7},{9,8},{10,9},{11,1... | collective-permute-start | bytes 786440 | tf_op jit(solution)/shard_map/ppermute | solution.py:380
  78.0 3.0 %collective-permute-start.6 = (f32[32,8,512]{2,1,0:T(8,128)S(1)}, f32[32,8,512]{2,1,0:T(8,128)S(1)}, u32[]{:S(2)}, u32[]{:S(2)}) collective-permute-start(f32[32,8,512]{2,1,0:T(8,128)S(1)} %get-tuple-element.30.refs_4_.f00.refs_14_), channel_id=1, source_target_pairs={{1,0},{2,1},{3,2},{4,3},{5,4},{6,5},{7,6},{8,7},{9,8},{10,9},{11,1... | collective-permute-start | bytes 1572872 | tf_op jit(solution)/shard_map/ppermute | solution.py:380
  81.0 2.9 %collective-permute-start.7 = (f32[32,8,512]{2,1,0:T(8,128)S(1)}, f32[32,8,512]{2,1,0:T(8,128)}, u32[]{:S(2)}, u32[]{:S(2)}) collective-permute-start(f32[32,8,512]{2,1,0:T(8,128)S(1)} %get-tuple-element.31.refs_5_.f01.refs_15_), channel_id=1, source_target_pairs={{1,0},{2,1},{3,2},{4,3},{5,4},{6,5},{7,6},{8,7},{9,8},{10,9},{11,1... | collective-permute-start | bytes 1572872 | tf_op jit(solution)/shard_map/ppermute | solution.py:380
  88.2 3.3 %collective-permute-start.19 = (f32[32,8,256]{2,1,0:T(8,128)}, f32[32,8,256]{2,1,0:T(8,128)}, u32[]{:S(2)}, u32[]{:S(2)}) collective-permute-start(f32[32,8,256]{2,1,0:T(8,128)} %fusion.14.c_own), channel_id=1, source_target_pairs={{1,0},{2,1},{3,2},{4,3},{5,4},{6,5},{7,6},{8,7},{9,8},{10,9},{11,1... | collective-permute-start | bytes 786440 | tf_op jit(solution)/shard_map/ppermute | solution.py:380
  92.8 5.2 %collective-permute-done.8.refs_10_ = f32[32,8,512]{2,1,0:T(8,128)} collective-permute-done((f32[32,8,512]{2,1,0:T(8,128)S(1)}, f32[32,8,512]{2,1,0:T(8,128)}, u32[]{:S(2)}, u32[]{:S(2)}) %collective-permute-start.8) | collective-permute-done | bytes 524320 | tf_op jit(solution)/shard_map/ppermute | solution.py:380
  98.0 5.6 %collective-permute-done.9.refs_11_ = f32[32,8,512]{2,1,0:T(8,128)} collective-permute-done((f32[32,8,512]{2,1,0:T(8,128)S(1)}, f32[32,8,512]{2,1,0:T(8,128)}, u32[]{:S(2)}, u32[]{:S(2)}) %collective-permute-start.9) | collective-permute-done | bytes 524320 | tf_op jit(solution)/shard_map/ppermute | solution.py:380
  106.7 5.2 %shard_map.43.part = f32[4,64,8,512]{3,2,1,0:T(8,128)S(1)} custom-call(f32[32,8,512]{2,1,0:T(8,128)S(1)} %copy-done.10, f32[32,8,512]{2,1,0:T(8,128)S(1)} %copy-done.12, f32[32,8,512]{2,1,0:T(8,128)S(1)} %collective-permute-done.4.refs_2_.refs_12_, f32[32,8,512]{2,1,0:T(8,128)S(1)} %collective-permute-done.5.refs_3_.refs_13_, ...), custom_call_target="tpu_custom_call" | custom-call | flops 100000000 | bytes 10485760 | tf_op jit(solution)/shard_map/pallas_call | solution.py:362
  112.0 6.4 %shard_map.45 = (f32[32,8,512]{2,1,0:T(8,128)S(1)}, f32[32,8,512]{2,1,0:T(8,128)S(1)}, f32[32,8,512]{2,1,0:T(8,128)S(1)}, f32[32,8,512]{2,1,0:T(8,128)S(1)}, f32...) custom-call(f32[32,8,512]{2,1,0:T(8,128)S(1)} %get-tuple-element.30.refs_4_.f00.refs_14_, ...), custom_call_target="tpu_custom_call" | custom-call | flops 100000000 | bytes 10240512 | tf_op jit(solution)/shard_map/pallas_call | solution.py:362
  118.4 3.9 %collective-permute-start.29 = (f32[32,8,256]{2,1,0:T(8,128)S(1)}, f32[32,8,256]{2,1,0:T(8,128)S(1)}, u32[]{:S(2)}, u32[]{:S(2)}) collective-permute-start(f32[32,8,256]{2,1,0:T(8,128)S(1)} %get-tuple-element.42), channel_id=1, source_target_pairs={{1,0},{2,1},{3,2},{4,3},{5,4},{6,5},{7,6},{8,7},{9,8},{10,9},{11,1... | collective-permute-start | bytes 786440 | tf_op jit(solution)/shard_map/ppermute | solution.py:380
  124.5 5.3 %collective-permute-start.31 = (f32[32,8,256]{2,1,0:T(8,128)S(1)}, f32[32,8,256]{2,1,0:T(8,128)S(1)}, u32[]{:S(2)}, u32[]{:S(2)}) collective-permute-start(f32[32,8,256]{2,1,0:T(8,128)S(1)} %get-tuple-element.46), channel_id=1, source_target_pairs={{1,0},{2,1},{3,2},{4,3},{5,4},{6,5},{7,6},{8,7},{9,8},{10,9},{11,1... | collective-permute-start | bytes 786440 | tf_op jit(solution)/shard_map/ppermute | solution.py:380
  130.0 12.5 %collective-permute-done.30 = f32[32,8,256]{2,1,0:T(8,128)S(1)} collective-permute-done((f32[32,8,256]{2,1,0:T(8,128)S(1)}, f32[32,8,256]{2,1,0:T(8,128)S(1)}, u32[]{:S(2)}, u32[]{:S(2)}) %collective-permute-start.30) | collective-permute-done | bytes 262176 | tf_op jit(solution)/shard_map/ppermute | solution.py:375
  145.4 4.5 %collective-permute-start.33 = (f32[32,8,256]{2,1,0:T(8,128)S(1)}, f32[32,8,256]{2,1,0:T(8,128)S(1)}, u32[]{:S(2)}, u32[]{:S(2)}) collective-permute-start(f32[32,8,256]{2,1,0:T(8,128)S(1)} %fusion.19), channel_id=1, source_target_pairs={{1,0},{2,1},{3,2},{4,3},{5,4},{6,5},{7,6},{8,7},{9,8},{10,9},{11,1... | collective-permute-start | bytes 786440 | tf_op jit(solution)/shard_map/ppermute | solution.py:380
  151.6 5.7 %collective-permute-start.35 = (f32[32,8,256]{2,1,0:T(8,128)S(1)}, f32[32,8,256]{2,1,0:T(8,128)S(1)}, u32[]{:S(2)}, u32[]{:S(2)}) collective-permute-start(f32[32,8,256]{2,1,0:T(8,128)S(1)} %fusion.24), channel_id=1, source_target_pairs={{1,0},{2,1},{3,2},{4,3},{5,4},{6,5},{7,6},{8,7},{9,8},{10,9},{11,1... | collective-permute-start | bytes 786440 | tf_op jit(solution)/shard_map/ppermute | solution.py:380
  157.5 3.0 %collective-permute-start.24 = (f32[32,8,512]{2,1,0:T(8,128)S(1)}, f32[32,8,512]{2,1,0:T(8,128)S(1)}, u32[]{:S(2)}, u32[]{:S(2)}) collective-permute-start(f32[32,8,512]{2,1,0:T(8,128)S(1)} %get-tuple-element.37.refs_4_.v00), channel_id=1, source_target_pairs={{1,0},{2,1},{3,2},{4,3},{5,4},{6,5},{7,6},{8,7},{9,8},{10,9},{11,1... | collective-permute-start | bytes 1572872 | tf_op jit(solution)/shard_map/ppermute | solution.py:380
  160.5 2.9 %collective-permute-start.25 = (f32[32,8,512]{2,1,0:T(8,128)S(1)}, f32[32,8,512]{2,1,0:T(8,128)S(1)}, u32[]{:S(2)}, u32[]{:S(2)}) collective-permute-start(f32[32,8,512]{2,1,0:T(8,128)S(1)} %get-tuple-element.38.refs_5_.v01), channel_id=1, source_target_pairs={{1,0},{2,1},{3,2},{4,3},{5,4},{6,5},{7,6},{8,7},{9,8},{10,9},{11,1... | collective-permute-start | bytes 1572872 | tf_op jit(solution)/shard_map/ppermute | solution.py:380
  166.5 3.8 %collective-permute-start.37 = (f32[32,8,256]{2,1,0:T(8,128)S(1)}, f32[32,8,256]{2,1,0:T(8,128)S(1)}, u32[]{:S(2)}, u32[]{:S(2)}) collective-permute-start(f32[32,8,256]{2,1,0:T(8,128)S(1)} %fusion.29.c_own), channel_id=1, source_target_pairs={{1,0},{2,1},{3,2},{4,3},{5,4},{6,5},{7,6},{8,7},{9,8},{10,9},{11,1... | collective-permute-start | bytes 786440 | tf_op jit(solution)/shard_map/ppermute | solution.py:380
  171.8 5.6 %collective-permute-done.26.refs_10_ = f32[32,8,512]{2,1,0:T(8,128)S(1)} collective-permute-done((f32[32,8,512]{2,1,0:T(8,128)S(1)}, f32[32,8,512]{2,1,0:T(8,128)S(1)}, u32[]{:S(2)}, u32[]{:S(2)}) %collective-permute-start.26) | collective-permute-done | bytes 524320 | tf_op jit(solution)/shard_map/ppermute | solution.py:380
  177.4 5.6 %collective-permute-done.27.refs_11_ = f32[32,8,512]{2,1,0:T(8,128)S(1)} collective-permute-done((f32[32,8,512]{2,1,0:T(8,128)S(1)}, f32[32,8,512]{2,1,0:T(8,128)S(1)}, u32[]{:S(2)}, u32[]{:S(2)}) %collective-permute-start.27) | collective-permute-done | bytes 524320 | tf_op jit(solution)/shard_map/ppermute | solution.py:380
  183.0 5.2 %shard_map.46.part = f32[4,64,8,512]{3,2,1,0:T(8,128)S(1)} custom-call(f32[32,8,512]{2,1,0:T(8,128)S(1)} %collective-permute-done.20.refs_0_, f32[32,8,512]{2,1,0:T(8,128)S(1)} %collective-permute-done.21.refs_1_, f32[32,8,512]{2,1,0:T(8,128)S(1)} %collective-permute-done.22.refs_2_, f32[32,8,512]{2,1,0:T(8,128)S(1)} %collective-permute-done.23.refs_3_, ...), custom_call_target="tpu_custom_call" | custom-call | flops 100000000 | bytes 14680064 | tf_op jit(solution)/shard_map/pallas_call | solution.py:362
  188.2 5.4 %shard_map.48 = (f32[2,64,8,512]{3,2,1,0:T(8,128)S(1)}, f32[64,1,128]{2,1,0:T(1,128)}) custom-call(f32[32,8,512]{2,1,0:T(8,128)S(1)} %get-tuple-element.30.refs_4_.f00.refs_14_, f32[32,8,512]{2,1,0:T(8,128)S(1)} %get-tuple-element.31.refs_5_.f01.refs_15_, f32[32,8,512]{2,1,0:T(8,128)S(1)} %get-tuple-element.32.refs_6_.f10.refs_16_, ...), custom_call_target="tpu_custom_call" | custom-call | flops 100000000 | bytes 9753088 | tf_op jit(solution)/shard_map/pallas_call | solution.py:362
  194.9 17.3 %all-to-all-start = ((f32[64,1,128]{2,1,0:T(1,128)}), f32[64,1,128]{2,1,0:T(1,128)S(1)}, u32[]{:S(2)}, u32[]{:S(2)}) async-start(f32[64,1,128]{2,1,0:T(1,128)} %get-tuple-element.44), calls=%async_computation | async-start | bytes 65536 | tf_op jit(solution)/shard_map/all_to_all | solution.py:384
  217.3 17.4 %all-to-all-done = f32[64,1,128]{2,1,0:T(1,128)S(1)} async-done(((f32[64,1,128]{2,1,0:T(1,128)}), f32[64,1,128]{2,1,0:T(1,128)S(1)}, u32[]{:S(2)}, u32[]{:S(2)}) %all-to-all-start) | async-done | bytes 32800 | tf_op jit(solution)/shard_map/all_to_all | solution.py:384
  236.3 2.9 %shard_map.50 = (f32[2,512,512]{2,1,0:T(8,128)}, f32[2]{0:T(128)}) custom-call(f32[64,128]{1,0:T(8,128)S(1)} %bitcast.1, f32[2,512,512]{2,1,0:T(8,128)S(1)} %copy-done.2), custom_call_target="tpu_custom_call" | custom-call | flops 10000000 | bytes 4227080 | tf_op jit(solution)/shard_map/pallas_call | solution.py:362
  (124 shorter events, 33.6 us)
Async XLA Ops:
  2.1 24.7 %collective-permute-start = (f32[1,512,512]{2,1,0:T(8,128)S(1)}, f32[1,512,512]{2,1,0:T(8,128)S(1)}, u32[]{:S(2)}, u32[]{:S(2)}) collective-permute-start(f32[1,512,512]{2,1,0:T(8,128)S(1)} %slice.230), channel_id=1, source_target_pairs={{0,1},{1,2},{2,3},{3,4},{4,5},{5,6},{6,7},{7,8},{8,9},{9,10},{10,1... | collective-permute-start | bytes 3145736 | tf_op jit(solution)/shard_map/ppermute | solution.py:375
  5.4 21.4 %collective-permute-start.1 = (f32[1,512,512]{2,1,0:T(8,128)S(1)}, f32[1,512,512]{2,1,0:T(8,128)S(1)}, u32[]{:S(2)}, u32[]{:S(2)}) collective-permute-start(f32[1,512,512]{2,1,0:T(8,128)S(1)} %slice.231), channel_id=1, source_target_pairs={{1,0},{2,1},{3,2},{4,3},{5,4},{6,5},{7,6},{8,7},{9,8},{10,9},{11,1... | collective-permute-start | bytes 3145736 | tf_op jit(solution)/shard_map/ppermute | solution.py:380
  30.5 13.6 %collective-permute-start.10 = (f32[32,8,256]{2,1,0:T(8,128)S(1)}, f32[32,8,256]{2,1,0:T(8,128)S(1)}, u32[]{:S(2)}, u32[]{:S(2)}) collective-permute-start(f32[32,8,256]{2,1,0:T(8,128)S(1)} %get-tuple-element.34), channel_id=1, source_target_pairs={{0,1},{1,2},{2,3},{3,4},{4,5},{5,6},{6,7},{7,8},{8,9},{9,10},{10,1... | collective-permute-start | bytes 786440 | tf_op jit(solution)/shard_map/ppermute | solution.py:375
  30.6 13.5 %collective-permute-start.11 = (f32[32,8,256]{2,1,0:T(8,128)S(1)}, f32[32,8,256]{2,1,0:T(8,128)S(1)}, u32[]{:S(2)}, u32[]{:S(2)}) collective-permute-start(f32[32,8,256]{2,1,0:T(8,128)S(1)} %get-tuple-element.35), channel_id=1, source_target_pairs={{1,0},{2,1},{3,2},{4,3},{5,4},{6,5},{7,6},{8,7},{9,8},{10,9},{11,1... | collective-permute-start | bytes 786440 | tf_op jit(solution)/shard_map/ppermute | solution.py:380
  42.8 35.1 %collective-permute-start.2 = (f32[32,8,512]{2,1,0:T(8,128)S(1)}, f32[32,8,512]{2,1,0:T(8,128)S(1)}, u32[]{:S(2)}, u32[]{:S(2)}) collective-permute-start(f32[32,8,512]{2,1,0:T(8,128)S(1)} %get-tuple-element.30.refs_4_.f00.refs_14_), channel_id=1, source_target_pairs={{0,1},{1,2},{2,3},{3,4},{4,5},{5,6},{6,7},{7,8},{8,9},{9,10},{10,1... | collective-permute-start | bytes 1572872 | tf_op jit(solution)/shard_map/ppermute | solution.py:375
  42.8 35.2 %collective-permute-start.3 = (f32[32,8,512]{2,1,0:T(8,128)S(1)}, f32[32,8,512]{2,1,0:T(8,128)S(1)}, u32[]{:S(2)}, u32[]{:S(2)}) collective-permute-start(f32[32,8,512]{2,1,0:T(8,128)S(1)} %get-tuple-element.31.refs_5_.f01.refs_15_), channel_id=1, source_target_pairs={{0,1},{1,2},{2,3},{3,4},{4,5},{5,6},{6,7},{7,8},{8,9},{9,10},{10,1... | collective-permute-start | bytes 1572872 | tf_op jit(solution)/shard_map/ppermute | solution.py:375
  42.8 38.2 %collective-permute-start.4 = (f32[32,8,512]{2,1,0:T(8,128)S(1)}, f32[32,8,512]{2,1,0:T(8,128)S(1)}, u32[]{:S(2)}, u32[]{:S(2)}) collective-permute-start(f32[32,8,512]{2,1,0:T(8,128)S(1)} %get-tuple-element.32.refs_6_.f10.refs_16_), channel_id=1, source_target_pairs={{0,1},{1,2},{2,3},{3,4},{4,5},{5,6},{6,7},{7,8},{8,9},{9,10},{10,1... | collective-permute-start | bytes 1572872 | tf_op jit(solution)/shard_map/ppermute | solution.py:375
  44.4 18.6 %collective-permute-start.12 = (f32[32,8,256]{2,1,0:T(8,128)S(1)}, f32[32,8,256]{2,1,0:T(8,128)S(1)}, u32[]{:S(2)}, u32[]{:S(2)}) collective-permute-start(f32[32,8,256]{2,1,0:T(8,128)S(1)} %get-tuple-element.48), channel_id=1, source_target_pairs={{0,1},{1,2},{2,3},{3,4},{4,5},{5,6},{6,7},{7,8},{8,9},{9,10},{10,1... | collective-permute-start | bytes 786440 | tf_op jit(solution)/shard_map/ppermute | solution.py:375
  44.5 18.5 %collective-permute-start.13 = (f32[32,8,256]{2,1,0:T(8,128)S(1)}, f32[32,8,256]{2,1,0:T(8,128)S(1)}, u32[]{:S(2)}, u32[]{:S(2)}) collective-permute-start(f32[32,8,256]{2,1,0:T(8,128)S(1)} %get-tuple-element.48), channel_id=1, source_target_pairs={{1,0},{2,1},{3,2},{4,3},{5,4},{6,5},{7,6},{8,7},{9,8},{10,9},{11,1... | collective-permute-start | bytes 786440 | tf_op jit(solution)/shard_map/ppermute | solution.py:380
  72.1 11.8 %collective-permute-start.16 = (f32[32,8,256]{2,1,0:T(8,128)S(1)}, f32[32,8,256]{2,1,0:T(8,128)S(1)}, u32[]{:S(2)}, u32[]{:S(2)}) collective-permute-start(f32[32,8,256]{2,1,0:T(8,128)S(1)} %fusion.9), channel_id=1, source_target_pairs={{0,1},{1,2},{2,3},{3,4},{4,5},{5,6},{6,7},{7,8},{8,9},{9,10},{10,1... | collective-permute-start | bytes 786440 | tf_op jit(solution)/shard_map/ppermute | solution.py:375
  72.2 12.5 %collective-permute-start.17 = (f32[32,8,256]{2,1,0:T(8,128)S(1)}, f32[32,8,256]{2,1,0:T(8,128)S(1)}, u32[]{:S(2)}, u32[]{:S(2)}) collective-permute-start(f32[32,8,256]{2,1,0:T(8,128)S(1)} %fusion.9), channel_id=1, source_target_pairs={{1,0},{2,1},{3,2},{4,3},{5,4},{6,5},{7,6},{8,7},{9,8},{10,9},{11,1... | collective-permute-start | bytes 786440 | tf_op jit(solution)/shard_map/ppermute | solution.py:380
  78.0 9.4 %collective-permute-start.6 = (f32[32,8,512]{2,1,0:T(8,128)S(1)}, f32[32,8,512]{2,1,0:T(8,128)S(1)}, u32[]{:S(2)}, u32[]{:S(2)}) collective-permute-start(f32[32,8,512]{2,1,0:T(8,128)S(1)} %get-tuple-element.30.refs_4_.f00.refs_14_), channel_id=1, source_target_pairs={{1,0},{2,1},{3,2},{4,3},{5,4},{6,5},{7,6},{8,7},{9,8},{10,9},{11,1... | collective-permute-start | bytes 1572872 | tf_op jit(solution)/shard_map/ppermute | solution.py:380
  81.0 11.8 %collective-permute-start.7 = (f32[32,8,512]{2,1,0:T(8,128)S(1)}, f32[32,8,512]{2,1,0:T(8,128)}, u32[]{:S(2)}, u32[]{:S(2)}) collective-permute-start(f32[32,8,512]{2,1,0:T(8,128)S(1)} %get-tuple-element.31.refs_5_.f01.refs_15_), channel_id=1, source_target_pairs={{1,0},{2,1},{3,2},{4,3},{5,4},{6,5},{7,6},{8,7},{9,8},{10,9},{11,1... | collective-permute-start | bytes 1572872 | tf_op jit(solution)/shard_map/ppermute | solution.py:380
  83.9 14.1 %collective-permute-start.8 = (f32[32,8,512]{2,1,0:T(8,128)S(1)}, f32[32,8,512]{2,1,0:T(8,128)}, u32[]{:S(2)}, u32[]{:S(2)}) collective-permute-start(f32[32,8,512]{2,1,0:T(8,128)S(1)} %get-tuple-element.32.refs_6_.f10.refs_16_), channel_id=1, source_target_pairs={{1,0},{2,1},{3,2},{4,3},{5,4},{6,5},{7,6},{8,7},{9,8},{10,9},{11,1... | collective-permute-start | bytes 1572872 | tf_op jit(solution)/shard_map/ppermute | solution.py:380
  84.7 18.9 %collective-permute-start.9 = (f32[32,8,512]{2,1,0:T(8,128)S(1)}, f32[32,8,512]{2,1,0:T(8,128)}, u32[]{:S(2)}, u32[]{:S(2)}) collective-permute-start(f32[32,8,512]{2,1,0:T(8,128)S(1)} %get-tuple-element.33.refs_7_.f11.refs_17_), channel_id=1, source_target_pairs={{1,0},{2,1},{3,2},{4,3},{5,4},{6,5},{7,6},{8,7},{9,8},{10,9},{11,1... | collective-permute-start | bytes 1572872 | tf_op jit(solution)/shard_map/ppermute | solution.py:380
  85.7 26.3 %collective-permute-start.18 = (f32[32,8,256]{2,1,0:T(8,128)}, f32[32,8,256]{2,1,0:T(8,128)}, u32[]{:S(2)}, u32[]{:S(2)}) collective-permute-start(f32[32,8,256]{2,1,0:T(8,128)} %fusion.14.c_own), channel_id=1, source_target_pairs={{0,1},{1,2},{2,3},{3,4},{4,5},{5,6},{6,7},{7,8},{8,9},{9,10},{10,1... | collective-permute-start | bytes 786440 | tf_op jit(solution)/shard_map/ppermute | solution.py:375
  88.2 23.8 %collective-permute-start.19 = (f32[32,8,256]{2,1,0:T(8,128)}, f32[32,8,256]{2,1,0:T(8,128)}, u32[]{:S(2)}, u32[]{:S(2)}) collective-permute-start(f32[32,8,256]{2,1,0:T(8,128)} %fusion.14.c_own), channel_id=1, source_target_pairs={{1,0},{2,1},{3,2},{4,3},{5,4},{6,5},{7,6},{8,7},{9,8},{10,9},{11,1... | collective-permute-start | bytes 786440 | tf_op jit(solution)/shard_map/ppermute | solution.py:380
  122.3 35.2 %collective-permute-start.20 = (f32[32,8,512]{2,1,0:T(8,128)S(1)}, f32[32,8,512]{2,1,0:T(8,128)S(1)}, u32[]{:S(2)}, u32[]{:S(2)}) collective-permute-start(f32[32,8,512]{2,1,0:T(8,128)S(1)} %get-tuple-element.37.refs_4_.v00), channel_id=1, source_target_pairs={{0,1},{1,2},{2,3},{3,4},{4,5},{5,6},{6,7},{7,8},{8,9},{9,10},{10,1... | collective-permute-start | bytes 1572872 | tf_op jit(solution)/shard_map/ppermute | solution.py:375
  122.3 35.3 %collective-permute-start.21 = (f32[32,8,512]{2,1,0:T(8,128)S(1)}, f32[32,8,512]{2,1,0:T(8,128)S(1)}, u32[]{:S(2)}, u32[]{:S(2)}) collective-permute-start(f32[32,8,512]{2,1,0:T(8,128)S(1)} %get-tuple-element.38.refs_5_.v01), channel_id=1, source_target_pairs={{0,1},{1,2},{2,3},{3,4},{4,5},{5,6},{6,7},{7,8},{8,9},{9,10},{10,1... | collective-permute-start | bytes 1572872 | tf_op jit(solution)/shard_map/ppermute | solution.py:375
  122.3 38.3 %collective-permute-start.22 = (f32[32,8,512]{2,1,0:T(8,128)S(1)}, f32[32,8,512]{2,1,0:T(8,128)S(1)}, u32[]{:S(2)}, u32[]{:S(2)}) collective-permute-start(f32[32,8,512]{2,1,0:T(8,128)S(1)} %get-tuple-element.39.refs_6_.v10), channel_id=1, source_target_pairs={{0,1},{1,2},{2,3},{3,4},{4,5},{5,6},{6,7},{7,8},{8,9},{9,10},{10,1... | collective-permute-start | bytes 1572872 | tf_op jit(solution)/shard_map/ppermute | solution.py:375
  124.5 18.0 %collective-permute-start.30 = (f32[32,8,256]{2,1,0:T(8,128)S(1)}, f32[32,8,256]{2,1,0:T(8,128)S(1)}, u32[]{:S(2)}, u32[]{:S(2)}) collective-permute-start(f32[32,8,256]{2,1,0:T(8,128)S(1)} %get-tuple-element.46), channel_id=1, source_target_pairs={{0,1},{1,2},{2,3},{3,4},{4,5},{5,6},{6,7},{7,8},{8,9},{9,10},{10,1... | collective-permute-start | bytes 786440 | tf_op jit(solution)/shard_map/ppermute | solution.py:375
  124.5 17.9 %collective-permute-start.31 = (f32[32,8,256]{2,1,0:T(8,128)S(1)}, f32[32,8,256]{2,1,0:T(8,128)S(1)}, u32[]{:S(2)}, u32[]{:S(2)}) collective-permute-start(f32[32,8,256]{2,1,0:T(8,128)S(1)} %get-tuple-element.46), channel_id=1, source_target_pairs={{1,0},{2,1},{3,2},{4,3},{5,4},{6,5},{7,6},{8,7},{9,8},{10,9},{11,1... | collective-permute-start | bytes 786440 | tf_op jit(solution)/shard_map/ppermute | solution.py:380
  142.8 8.0 %collective-permute-start.32 = (f32[32,8,256]{2,1,0:T(8,128)S(1)}, f32[32,8,256]{2,1,0:T(8,128)S(1)}, u32[]{:S(2)}, u32[]{:S(2)}) collective-permute-start(f32[32,8,256]{2,1,0:T(8,128)S(1)} %fusion.19), channel_id=1, source_target_pairs={{0,1},{1,2},{2,3},{3,4},{4,5},{5,6},{6,7},{7,8},{8,9},{9,10},{10,1... | collective-permute-start | bytes 786440 | tf_op jit(solution)/shard_map/ppermute | solution.py:375
  151.6 11.9 %collective-permute-start.34 = (f32[32,8,256]{2,1,0:T(8,128)S(1)}, f32[32,8,256]{2,1,0:T(8,128)S(1)}, u32[]{:S(2)}, u32[]{:S(2)}) collective-permute-start(f32[32,8,256]{2,1,0:T(8,128)S(1)} %fusion.24), channel_id=1, source_target_pairs={{0,1},{1,2},{2,3},{3,4},{4,5},{5,6},{6,7},{7,8},{8,9},{9,10},{10,1... | collective-permute-start | bytes 786440 | tf_op jit(solution)/shard_map/ppermute | solution.py:375
  151.6 12.7 %collective-permute-start.35 = (f32[32,8,256]{2,1,0:T(8,128)S(1)}, f32[32,8,256]{2,1,0:T(8,128)S(1)}, u32[]{:S(2)}, u32[]{:S(2)}) collective-permute-start(f32[32,8,256]{2,1,0:T(8,128)S(1)} %fusion.24), channel_id=1, source_target_pairs={{1,0},{2,1},{3,2},{4,3},{5,4},{6,5},{7,6},{8,7},{9,8},{10,9},{11,1... | collective-permute-start | bytes 786440 | tf_op jit(solution)/shard_map/ppermute | solution.py:380
  157.5 8.9 %collective-permute-start.24 = (f32[32,8,512]{2,1,0:T(8,128)S(1)}, f32[32,8,512]{2,1,0:T(8,128)S(1)}, u32[]{:S(2)}, u32[]{:S(2)}) collective-permute-start(f32[32,8,512]{2,1,0:T(8,128)S(1)} %get-tuple-element.37.refs_4_.v00), channel_id=1, source_target_pairs={{1,0},{2,1},{3,2},{4,3},{5,4},{6,5},{7,6},{8,7},{9,8},{10,9},{11,1... | collective-permute-start | bytes 1572872 | tf_op jit(solution)/shard_map/ppermute | solution.py:380
  160.5 11.3 %collective-permute-start.25 = (f32[32,8,512]{2,1,0:T(8,128)S(1)}, f32[32,8,512]{2,1,0:T(8,128)S(1)}, u32[]{:S(2)}, u32[]{:S(2)}) collective-permute-start(f32[32,8,512]{2,1,0:T(8,128)S(1)} %get-tuple-element.38.refs_5_.v01), channel_id=1, source_target_pairs={{1,0},{2,1},{3,2},{4,3},{5,4},{6,5},{7,6},{8,7},{9,8},{10,9},{11,1... | collective-permute-start | bytes 1572872 | tf_op jit(solution)/shard_map/ppermute | solution.py:380
  163.4 14.0 %collective-permute-start.26 = (f32[32,8,512]{2,1,0:T(8,128)S(1)}, f32[32,8,512]{2,1,0:T(8,128)S(1)}, u32[]{:S(2)}, u32[]{:S(2)}) collective-permute-start(f32[32,8,512]{2,1,0:T(8,128)S(1)} %get-tuple-element.39.refs_6_.v10), channel_id=1, source_target_pairs={{1,0},{2,1},{3,2},{4,3},{5,4},{6,5},{7,6},{8,7},{9,8},{10,9},{11,1... | collective-permute-start | bytes 1572872 | tf_op jit(solution)/shard_map/ppermute | solution.py:380
  164.3 18.7 %collective-permute-start.27 = (f32[32,8,512]{2,1,0:T(8,128)S(1)}, f32[32,8,512]{2,1,0:T(8,128)S(1)}, u32[]{:S(2)}, u32[]{:S(2)}) collective-permute-start(f32[32,8,512]{2,1,0:T(8,128)S(1)} %get-tuple-element.40.refs_7_.v11), channel_id=1, source_target_pairs={{1,0},{2,1},{3,2},{4,3},{5,4},{6,5},{7,6},{8,7},{9,8},{10,9},{11,1... | collective-permute-start | bytes 1572872 | tf_op jit(solution)/shard_map/ppermute | solution.py:380
  164.6 23.7 %collective-permute-start.36 = (f32[32,8,256]{2,1,0:T(8,128)S(1)}, f32[32,8,256]{2,1,0:T(8,128)S(1)}, u32[]{:S(2)}, u32[]{:S(2)}) collective-permute-start(f32[32,8,256]{2,1,0:T(8,128)S(1)} %fusion.29.c_own), channel_id=1, source_target_pairs={{0,1},{1,2},{2,3},{3,4},{4,5},{5,6},{6,7},{7,8},{8,9},{9,10},{10,1... | collective-permute-start | bytes 786440 | tf_op jit(solution)/shard_map/ppermute | solution.py:375
  166.5 21.8 %collective-permute-start.37 = (f32[32,8,256]{2,1,0:T(8,128)S(1)}, f32[32,8,256]{2,1,0:T(8,128)S(1)}, u32[]{:S(2)}, u32[]{:S(2)}) collective-permute-start(f32[32,8,256]{2,1,0:T(8,128)S(1)} %fusion.29.c_own), channel_id=1, source_target_pairs={{1,0},{2,1},{3,2},{4,3},{5,4},{6,5},{7,6},{8,7},{9,8},{10,9},{11,1... | collective-permute-start | bytes 786440 | tf_op jit(solution)/shard_map/ppermute | solution.py:380
  194.9 39.8 %all-to-all-start = ((f32[64,1,128]{2,1,0:T(1,128)}), f32[64,1,128]{2,1,0:T(1,128)S(1)}, u32[]{:S(2)}, u32[]{:S(2)}) async-start(f32[64,1,128]{2,1,0:T(1,128)} %get-tuple-element.44), calls=%async_computation | async-start | bytes 65536 | tf_op jit(solution)/shard_map/all_to_all | solution.py:384
  (20 other events, 139.3 us)

commit v4 on v3

--- a/solution.py
+++ b/solution.py
@@ -189,35 +189,70 @@
         fill_ends(C, k, nc)
 
 
+def sweep_weights(first):
+    own, beside = 1.0 - 6.0 * KAPPA, KAPPA
+    return ((own + 1.0) * KAPPA, KAPPA * KAPPA) if first else (own, beside)
+
+
+def fill_planes(start, W, nj):
+    half = nj // 2
+    for k, plane in enumerate(start):
+        for h in range(2):
+            def fill(i, k=k, h=h, plane=plane):
+                W[k, h * half + i + 1] = plane[h][i]
+
+            loop(half, fill, 8)
+        fill_ends(W, k, nj)
+
+
+def own_sweep_kernel(first, *refs):
+    out, W = refs[-2:]
+    nj = W.shape[1] - 2
+    half = nj // 2
+    start = halves(refs[:4])
+    force = None if first else halves(refs[4:8])
+    own, weight = sweep_weights(first)
+    fill_planes(start, W, nj)
+    for x in range(2):
+        for h in range(2):
+            def body(i, x=x, h=h):
+                j = h * half + 2 * i
+                center, beside = across(W, x, j, 2)
+                value = own * center + weight * (beside + W[1 - x, pl.ds(j + 1, 2)])
+                if not first:
+                    value = value + KAPPA * force[x][h][pl.ds(2 * i, 2)]
+                out[x, pl.ds(j, 2)] = value
+
+            loop(half // 2, body, 8)
+
+
 def sweep_kernel(first, *refs):
-    nj = refs[-1].shape[1] - 2
-    half = nj // 2
-    W, part = refs[-1], refs[-2]
+    inner, part, W = refs[-3:]
+    nj = W.shape[1] - 2
+    half = nj // 2
     start = halves(refs[:12])
-    force = None if first else halves(refs[12:20])
-    own, beside_weight = (1.0 - 6.0 * KAPPA, KAPPA)
-    if first:
-        own, beside_weight = own * KAPPA + KAPPA, KAPPA * KAPPA
-    for k in range(6):
-        for h in range(2):
-            def fill(i, k=k, h=h):
-                W[k, h * half + i + 1] = start[k][h][i]
-
-            loop(half, fill, 8)
-        if 1 <= k <= 4:
-            fill_ends(W, k, nj)
-    for k in range(4):
-        for h in range(2):
-            def body(i, k=k, h=h):
+    force = None if first else halves(refs[12:16])
+    own, weight = sweep_weights(first)
+    fill_planes((start[1], start[4]), W, nj)
+    for side, (k, below, above) in enumerate(((0, 0, 2), (3, 3, 5))):
+        for h in range(2):
+            def outer(i, side=side, k=k, below=below, above=above, h=h):
                 j = h * half + 2 * i
-                center, beside = across(W, k + 1, j, 2)
-                at = pl.ds(j + 1, 2)
-                value = own * center + beside_weight * (beside + W[k, at] + W[k + 2, at])
+                at = pl.ds(2 * i, 2)
+                center, beside = across(W, side, j, 2)
+                value = own * center + weight * (beside + start[below][h][at] + start[above][h][at])
                 if not first:
-                    value = value + KAPPA * force[k][h][pl.ds(2 * i, 2)]
+                    value = value + KAPPA * force[side][h][at]
                 part[k, pl.ds(j, 2)] = value
 
-            loop(half // 2, body, 8)
+            loop(half // 2, outer, 8)
+    for x, k in enumerate((1, 4)):
+        for h in range(2):
+            def border(i, x=x, k=k, h=h):
+                j = h * half + 2 * i
+                part[x + 1, pl.ds(j, 2)] = inner[x, pl.ds(j, 2)] + weight * start[k][h][pl.ds(2 * i, 2)]
+
+            loop(half // 2, border, 8)
 
 
 def add_correction(part, C, V, nj):
@@ -307,7 +342,10 @@
         for h in range(2):
             def body(i, x=x, h=h):
                 center, residue = residual_rows(V, force, x, h, i, half)
-                out[x, pl.ds(h * half + 2 * i, 2)] = center
+                for row in range(2):
+                    for t in range(out.shape[1]):
+                        cells = center[row, :, t * LANES : (t + 1) * LANES]
+                        out[x, t, pl.ds(h * half + 2 * i + row, 8, stride=nj), :] = cells
                 add_figures(acc, residue, shift)
 
             loop(half // 2, body, 4)
@@ -315,42 +353,29 @@
     stats[...] = jnp.broadcast_to(row[None], stats.shape)
 
 
-def natural_kernel(field, out, T):
-    nj = field.shape[1]
-    tiles = T.shape[0]
-    for x in range(2):
-        def body(j, x=x):
-            row = field[x, j]
-            for t in range(tiles):
-                T[t, pl.ds(j, 8, stride=nj), :] = row[:, t * LANES : (t + 1) * LANES]
-
-        loop(nj, body, 8)
-
-        def join(i, x=x):
-            rows = pl.ds(pl.multiple_of(i * 16, 16), 16)
-            for t in range(tiles):
-                out[x, rows, pl.ds(t * LANES, LANES)] = T[t, rows, :]
-
-        loop(nj // 2, join, 4)
-
-
-def finish_kernel(share, figures, field, out, norms):
+def finish_kernel(share, figures, field, out, norms, gain_ref):
     devices = figures.shape[0]
-    sums = figures[:, 0:1]
-    mean = -jnp.sum(sums, axis=0, keepdims=True) / (share * devices)
-    off = mean + sums / share
-    for c, at in enumerate((3, 1)):
-        linear, square = figures[:, at : at + 1], figures[:, at + 1 : at + 2]
-        squares = square + 2.0 * off * linear + share * off * off
-        total = jnp.sum(squares, axis=0, keepdims=True) / (share * devices)
-        norms[c] = jnp.sqrt(total)[0, 0]
-    gain = mean * (CONSTANT_GAIN * CYCLES)
+
+    @pl.when(pl.program_id(0) == 0)
+    def _():
+        sums = figures[:, 0:1]
+        mean = -jnp.sum(sums, axis=0, keepdims=True) / (share * devices)
+        off = mean + sums / share
+        for c, at in enumerate((3, 1)):
+            linear, square = figures[:, at : at + 1], figures[:, at + 1 : at + 2]
+            squares = square + 2.0 * off * linear + share * off * off
+            total = jnp.sum(squares, axis=0, keepdims=True) / (share * devices)
+            norms[c] = jnp.sqrt(total)[0, 0]
+        gain_ref[...] = jnp.broadcast_to(mean * (CONSTANT_GAIN * CYCLES), gain_ref.shape)
+
+    gain = gain_ref[...]
     for x in range(2):
         def body(i, x=x):
             rows = pl.ds(pl.multiple_of(i * 16, 16), 16)
-            out[x, rows, :] = field[x, rows, :] + gain
-
-        loop(field.shape[1] // 16, body, 4)
+            for t in range(field.shape[1]):
+                out[x, rows, pl.ds(t * LANES, LANES)] = field[x, t, rows, :] + gain[:1]
+
+        loop(field.shape[2] // 16, body, 4)
 
 
 VMEM = pl.BlockSpec(memory_space=pltpu.VMEM)
@@ -397,7 +422,7 @@
     return left, right
 
 
-def coarse_part(local, s0, s1, weight, chunks):
+def coarse_part(local, s0, s1, weight, chunks, force, shape):
     moved = []
     left, right = both(s1, s0)
     moved.append(both(chunks[0], chunks[0]))
@@ -411,7 +436,11 @@
         field = part + KAPPA * (left + right)
     left, right = both(field, field)
     lefts, rights = zip(*moved)
-    return (field, left, right), lefts, rights
+    (inner,) = call(
+        functools.partial(own_sweep_kernel, not force), (*chunks, *force), [(2, *shape)],
+        [(2, shape[0] + 2, *shape[1:])], 10**8,
+    )
+    return (field, left, right), lefts, rights, inner
 
 
 def whole(potential):
@@ -440,11 +469,12 @@
     (local,) = call(
         rhs_first_kernel, (*forcing, pairs), [coarse], [(1, *tall), (1, nc, 8, nz)], 3 * 10**7
     )
-    correction, f_left, f_right = coarse_part(local, s0, s1, KAPPA, forcing)
+    rows = (nj, 8, nz)
+    correction, f_left, f_right, inner = coarse_part(local, s0, s1, KAPPA, forcing, (), rows)
     planes = (4, nj, 8, nz)
     scratch = [(4, *tall), (3, nc + 2, 8, nz)]
     (part,) = call(
-        functools.partial(sweep_kernel, True), (*f_left, *forcing, *f_right), [planes], [(6, *tall)], 10**8
+        functools.partial(sweep_kernel, True), (*f_left, *forcing, *f_right, inner), [planes], [(2, *tall)], 10**8
     )
     *field, s0, s1, first = call(
         middle_kernel, (*forcing, part, *correction, shift, pairs),
@@ -453,20 +483,31 @@
     (local,) = call(
         rhs_later_kernel, (*forcing, *field, pairs), [coarse], [(1, *tall), (1, nc, 8, nz)], 3 * 10**7
     )
-    correction, v_left, v_right = coarse_part(local, s0, s1, 1.0, field)
+    correction, v_left, v_right, inner = coarse_part(local, s0, s1, 1.0, field, forcing, rows)
     (part,) = call(
         functools.partial(sweep_kernel, False),
-        (*v_left, *field, *v_right, *f_left[2:], *forcing, *f_right[:2]), [planes], [(6, *tall)], 10**8,
+        (*v_left, *field, *v_right, *f_left[2:], *f_right[:2], inner), [planes], [(2, *tall)], 10**8,
     )
     result, last = call(
         last_kernel, (*forcing, part, *correction, shift, total, first, pairs),
-        [(2, nj, 8, nz), (lax.axis_size("gx"), 1, LANES)], [*scratch, (2, 8, nz)], 10**8,
-    )
-    (result,) = call(natural_kernel, (result,), [potential.shape], [tiles], 3 * 10**7)
-    result, norms = call(
-        functools.partial(finish_kernel, share), (gathered(last).reshape(-1, LANES), result),
-        [potential.shape, (CYCLES,)], [], 10**7, [VMEM, SMEM],
-    )
+        [(2, *tiles), (lax.axis_size("gx"), 1, LANES)], [*scratch, (2, 8, nz)], 10**8,
+    )
+    figures = gathered(last).reshape(-1, LANES)
+    blocks = 2
+    count = nz // LANES
+    result, norms = pl.pallas_call(
+        functools.partial(finish_kernel, share),
+        grid=(blocks,),
+        out_shape=[jax.ShapeDtypeStruct(potential.shape, jnp.float32), jax.ShapeDtypeStruct((CYCLES,), jnp.float32)],
+        in_specs=[
+            pl.BlockSpec(figures.shape, lambda i: (0, 0)),
+            pl.BlockSpec((2, count, ny // blocks, LANES), lambda i: (0, 0, i, 0)),
+        ],
+        out_specs=[pl.BlockSpec((2, ny // blocks, nz), lambda i: (0, i, 0)), SMEM],
+        scratch_shapes=[pltpu.VMEM((8, LANES), jnp.float32)],
+        compiler_params=pltpu.CompilerParams(vmem_limit_bytes=16 * 2**20),
+        cost_estimate=pl.CostEstimate(flops=10**7, bytes_accessed=8 * result.size, transcendentals=0),
+    )(figures, result)
     return (result, norms)
 
 

time: 240 us -> 228 us (0.950)
  blocking collectives: 0 us -> 39 us
  waiting for transfers between devices: 69.3 us -> 48.1 us
  starting transfers between devices: 115 us -> 97.8 us
  local copies, waits for them, and re-layouts: 12.8 us -> 3.93 us
  Pallas kernels: 37.2 us -> 34.1 us
    all_to_all x0 -> x1, blocking collectives: none -> 39 us  [gathered(): return lax.all_to_all(rows, 'gx', 0, 0, tiled=True)]
    all_to_all x1 -> x0, waiting for transfers between devices: 17.4 us -> none  [gathered(): return lax.all_to_all(rows, 'gx', 0, 0, tiled=True)]
    all_to_all x1 -> x0, starting transfers between devices: 17.3 us -> none  [gathered(): return lax.all_to_all(rows, 'gx', 0, 0, tiled=True)]
    unnamed x26 -> x16, local copies, waits for them, and re-layouts: 9.75 us -> 0.84 us
    pallas_call x10, Pallas kernels: 37.2 us -> 32.3 us  [call(): pl.pallas_call(kernel, out_shape=[jax.ShapeDtypeStruct(o, jnp.float32) fo...]
    ppermute x19, waiting for transfers between devices: 25.1 us -> 21.3 us  [from_right(): return lax.ppermute(x, 'gx', [((i + 1) % count, i) for i in range(count)])]
  transfers between devices with their start and end apart: 39 -> 38, of which waited for: 14 -> 12; matrix products, arithmetic and copies ran while one was open for 2% -> 2% of each run, Pallas kernels for 8% -> 7%
where the time goes in v4:
time: 228 us
  starting transfers between devices  97.8 us (43%)
  waiting for transfers between devices  48.1 us (21%)
  blocking collectives  39 us (17%)
  Pallas kernels  34.1 us (15%)
  local copies, waits for them, and re-layouts  3.93 us (2%)
  other arithmetic  2.84 us (1%)
    ppermute x19, starting transfers between devices, from_right(): return lax.ppermute(x, 'gx', [((i + 1) % count, i) for i in range(count)])  85.5 us
    all_to_all x1, blocking collectives, gathered(): return lax.all_to_all(rows, 'gx', 0, 0, tiled=True)  39 us
    pallas_call x10, Pallas kernels, call(): pl.pallas_call(kernel, out_shape=[jax.ShapeDtypeStruct(o, jnp.float32) fo...  32.3 us
    ppermute x19, waiting for transfers between devices, from_left(): return lax.ppermute(x, 'gx', [(i, (i + 1) % count) for i in range(count)])  26.8 us
    ppermute x19, waiting for transfers between devices, from_right(): return lax.ppermute(x, 'gx', [((i + 1) % count, i) for i in range(count)])  21.3 us
    ppermute x19, starting transfers between devices, from_left(): return lax.ppermute(x, 'gx', [(i, (i + 1) % count) for i in range(count)])  12.3 us
  transfers between devices with their start and end apart: 38, of which 12 were waited for; matrix products, arithmetic and copies ran while one was open for 2% of the time, Pallas kernels for 7%

profile of v4, /device:TPU:37, one launch (start us, length us, event | category | flops | bytes accessed | tf_op | source)
XLA Modules:
  0.0 227.7 jit_solution(348725081112923263)
XLA Ops:
  2.1 3.2 %collective-permute-start = (f32[1,512,512]{2,1,0:T(8,128)S(1)}, f32[1,512,512]{2,1,0:T(8,128)S(1)}, u32[]{:S(2)}, u32[]{:S(2)}) collective-permute-start(f32[1,512,512]{2,1,0:T(8,128)S(1)} %slice.230), channel_id=1, source_target_pairs={{0,1},{1,2},{2,3},{3,4},{4,5},{5,6},{6,7},{7,8},{8,9},{9,10},{10,1... | collective-permute-start | bytes 3145736 | tf_op jit(solution)/shard_map/ppermute | solution.py:400
  5.4 17.7 %collective-permute-start.1 = (f32[1,512,512]{2,1,0:T(8,128)S(1)}, f32[1,512,512]{2,1,0:T(8,128)S(1)}, u32[]{:S(2)}, u32[]{:S(2)}) collective-permute-start(f32[1,512,512]{2,1,0:T(8,128)S(1)} %slice.231), channel_id=1, source_target_pairs={{1,0},{2,1},{3,2},{4,3},{5,4},{6,5},{7,6},{8,7},{9,8},{10,9},{11,1... | collective-permute-start | bytes 3145736 | tf_op jit(solution)/shard_map/ppermute | solution.py:405
  23.1 3.7 %shard_map.41 = (f32[2,66,8,512]{3,2,1,0:T(8,128)S(1)}, f32[2,66,8,512]{3,2,1,0:T(8,128)S(1)}, f32[2,64,8,512]{3,2,1,0:T(8,128)S(1)}, f32[2,64,8,512]{3,2,1,0:T(8,128)S(1)}) custom-call(f32[2,512,512]{2,1,0:T(8,128)S(1)} %copy-done), custom_call_target="tpu_custom_call" | custom-call | flops 100000000 | bytes 10616832 | tf_op jit(solution)/shard_map/pallas_call | solution.py:387
  26.8 3.7 %shard_map.42 = (f32[32,8,512]{2,1,0:T(8,128)S(1)}, f32[32,8,512]{2,1,0:T(8,128)S(1)}, f32[32,8,512]{2,1,0:T(8,128)S(1)}, f32[32,8,512]{2,1,0:T(8,128)S(1)}, f32...) custom-call(f32[2,66,8,512]{3,2,1,0:T(8,128)S(1)} %get-tuple-element.25.X, ...), custom_call_target="tpu_custom_call" | custom-call | flops 100000000 | bytes 13766656 | tf_op jit(solution)/shard_map/pallas_call | solution.py:387
  30.6 12.1 %collective-permute-start.11 = (f32[32,8,256]{2,1,0:T(8,128)S(1)}, f32[32,8,256]{2,1,0:T(8,128)S(1)}, u32[]{:S(2)}, u32[]{:S(2)}) collective-permute-start(f32[32,8,256]{2,1,0:T(8,128)S(1)} %get-tuple-element.35), channel_id=1, source_target_pairs={{1,0},{2,1},{3,2},{4,3},{5,4},{6,5},{7,6},{8,7},{9,8},{10,9},{11,1... | collective-permute-start | bytes 786440 | tf_op jit(solution)/shard_map/ppermute | solution.py:405
  44.5 5.8 %collective-permute-start.13 = (f32[32,8,256]{2,1,0:T(8,128)S(1)}, f32[32,8,256]{2,1,0:T(8,128)S(1)}, u32[]{:S(2)}, u32[]{:S(2)}) collective-permute-start(f32[32,8,256]{2,1,0:T(8,128)S(1)} %get-tuple-element.48), channel_id=1, source_target_pairs={{1,0},{2,1},{3,2},{4,3},{5,4},{6,5},{7,6},{8,7},{9,8},{10,9},{11,1... | collective-permute-start | bytes 786440 | tf_op jit(solution)/shard_map/ppermute | solution.py:405
  50.4 12.6 %collective-permute-done.12 = f32[32,8,256]{2,1,0:T(8,128)S(1)} collective-permute-done((f32[32,8,256]{2,1,0:T(8,128)S(1)}, f32[32,8,256]{2,1,0:T(8,128)S(1)}, u32[]{:S(2)}, u32[]{:S(2)}) %collective-permute-start.12) | collective-permute-done | bytes 262176 | tf_op jit(solution)/shard_map/ppermute | solution.py:400
  63.3 2.5 %collective-permute-start.14 = (f32[32,8,256]{2,1,0:T(8,128)S(1)}, f32[32,8,256]{2,1,0:T(8,128)S(1)}, u32[]{:S(2)}, u32[]{:S(2)}) collective-permute-start(f32[32,8,256]{2,1,0:T(8,128)S(1)} %fusion.4), channel_id=1, source_target_pairs={{0,1},{1,2},{2,3},{3,4},{4,5},{5,6},{6,7},{7,8},{8,9},{9,10},{10,1... | collective-permute-start | bytes 786440 | tf_op jit(solution)/shard_map/ppermute | solution.py:400
  65.9 4.4 %collective-permute-start.15 = (f32[32,8,256]{2,1,0:T(8,128)S(1)}, f32[32,8,256]{2,1,0:T(8,128)S(1)}, u32[]{:S(2)}, u32[]{:S(2)}) collective-permute-start(f32[32,8,256]{2,1,0:T(8,128)S(1)} %fusion.4), channel_id=1, source_target_pairs={{1,0},{2,1},{3,2},{4,3},{5,4},{6,5},{7,6},{8,7},{9,8},{10,9},{11,1... | collective-permute-start | bytes 786440 | tf_op jit(solution)/shard_map/ppermute | solution.py:405
  72.2 5.6 %collective-permute-start.17 = (f32[32,8,256]{2,1,0:T(8,128)S(1)}, f32[32,8,256]{2,1,0:T(8,128)S(1)}, u32[]{:S(2)}, u32[]{:S(2)}) collective-permute-start(f32[32,8,256]{2,1,0:T(8,128)S(1)} %fusion.9), channel_id=1, source_target_pairs={{1,0},{2,1},{3,2},{4,3},{5,4},{6,5},{7,6},{8,7},{9,8},{10,9},{11,1... | collective-permute-start | bytes 786440 | tf_op jit(solution)/shard_map/ppermute | solution.py:405
  78.0 3.0 %collective-permute-start.6 = (f32[32,8,512]{2,1,0:T(8,128)S(1)}, f32[32,8,512]{2,1,0:T(8,128)S(1)}, u32[]{:S(2)}, u32[]{:S(2)}) collective-permute-start(f32[32,8,512]{2,1,0:T(8,128)S(1)} %get-tuple-element.30.refs_0_.refs_4_.f00), channel_id=1, source_target_pairs={{1,0},{2,1},{3,2},{4,3},{5,4},{6,5},{7,6},{8,7},{9,8},{10,9},{11,1... | collective-permute-start | bytes 1572872 | tf_op jit(solution)/shard_map/ppermute | solution.py:405
  81.0 2.9 %collective-permute-start.7 = (f32[32,8,512]{2,1,0:T(8,128)S(1)}, f32[32,8,512]{2,1,0:T(8,128)}, u32[]{:S(2)}, u32[]{:S(2)}) collective-permute-start(f32[32,8,512]{2,1,0:T(8,128)S(1)} %get-tuple-element.31.refs_1_.refs_5_.f01), channel_id=1, source_target_pairs={{1,0},{2,1},{3,2},{4,3},{5,4},{6,5},{7,6},{8,7},{9,8},{10,9},{11,1... | collective-permute-start | bytes 1572872 | tf_op jit(solution)/shard_map/ppermute | solution.py:405
  88.2 3.3 %collective-permute-start.19 = (f32[32,8,256]{2,1,0:T(8,128)}, f32[32,8,256]{2,1,0:T(8,128)}, u32[]{:S(2)}, u32[]{:S(2)}) collective-permute-start(f32[32,8,256]{2,1,0:T(8,128)} %fusion.14.c_own), channel_id=1, source_target_pairs={{1,0},{2,1},{3,2},{4,3},{5,4},{6,5},{7,6},{8,7},{9,8},{10,9},{11,1... | collective-permute-start | bytes 786440 | tf_op jit(solution)/shard_map/ppermute | solution.py:405
  94.7 3.3 %collective-permute-done.8.refs_10_ = f32[32,8,512]{2,1,0:T(8,128)} collective-permute-done((f32[32,8,512]{2,1,0:T(8,128)S(1)}, f32[32,8,512]{2,1,0:T(8,128)}, u32[]{:S(2)}, u32[]{:S(2)}) %collective-permute-start.8) | collective-permute-done | bytes 524320 | tf_op jit(solution)/shard_map/ppermute | solution.py:405
  98.0 5.6 %collective-permute-done.9.refs_11_ = f32[32,8,512]{2,1,0:T(8,128)} collective-permute-done((f32[32,8,512]{2,1,0:T(8,128)S(1)}, f32[32,8,512]{2,1,0:T(8,128)}, u32[]{:S(2)}, u32[]{:S(2)}) %collective-permute-start.9) | collective-permute-done | bytes 524320 | tf_op jit(solution)/shard_map/ppermute | solution.py:405
  103.6 3.5 %shard_map.44.part = f32[4,64,8,512]{3,2,1,0:T(8,128)S(1)} custom-call(f32[32,8,512]{2,1,0:T(8,128)S(1)} %copy-done.5, f32[32,8,512]{2,1,0:T(8,128)S(1)} %copy-done.7, f32[32,8,512]{2,1,0:T(8,128)S(1)} %collective-permute-done.4.refs_2_.refs_12_, f32[32,8,512]{2,1,0:T(8,128)S(1)} %collective-permute-done.5.refs_3_.refs_13_, ...), custom_call_target="tpu_custom_call" | custom-call | flops 100000000 | bytes 12582912 | tf_op jit(solution)/shard_map/pallas_call | solution.py:387
  107.1 6.4 %shard_map.46 = (f32[32,8,512]{2,1,0:T(8,128)S(1)}, f32[32,8,512]{2,1,0:T(8,128)S(1)}, f32[32,8,512]{2,1,0:T(8,128)S(1)}, f32[32,8,512]{2,1,0:T(8,128)S(1)}, f32...) custom-call(f32[32,8,512]{2,1,0:T(8,128)S(1)} %get-tuple-element.30.refs_0_.refs_4_.f00, ...), custom_call_target="tpu_custom_call" | custom-call | flops 100000000 | bytes 10240512 | tf_op jit(solution)/shard_map/pallas_call | solution.py:387
  113.6 3.9 %collective-permute-start.29 = (f32[32,8,256]{2,1,0:T(8,128)S(1)}, f32[32,8,256]{2,1,0:T(8,128)S(1)}, u32[]{:S(2)}, u32[]{:S(2)}) collective-permute-start(f32[32,8,256]{2,1,0:T(8,128)S(1)} %get-tuple-element.42), channel_id=1, source_target_pairs={{1,0},{2,1},{3,2},{4,3},{5,4},{6,5},{7,6},{8,7},{9,8},{10,9},{11,1... | collective-permute-start | bytes 786440 | tf_op jit(solution)/shard_map/ppermute | solution.py:405
  119.7 5.3 %collective-permute-start.31 = (f32[32,8,256]{2,1,0:T(8,128)S(1)}, f32[32,8,256]{2,1,0:T(8,128)S(1)}, u32[]{:S(2)}, u32[]{:S(2)}) collective-permute-start(f32[32,8,256]{2,1,0:T(8,128)S(1)} %get-tuple-element.46), channel_id=1, source_target_pairs={{1,0},{2,1},{3,2},{4,3},{5,4},{6,5},{7,6},{8,7},{9,8},{10,9},{11,1... | collective-permute-start | bytes 786440 | tf_op jit(solution)/shard_map/ppermute | solution.py:405
  125.1 12.5 %collective-permute-done.30 = f32[32,8,256]{2,1,0:T(8,128)S(1)} collective-permute-done((f32[32,8,256]{2,1,0:T(8,128)S(1)}, f32[32,8,256]{2,1,0:T(8,128)S(1)}, u32[]{:S(2)}, u32[]{:S(2)}) %collective-permute-start.30) | collective-permute-done | bytes 262176 | tf_op jit(solution)/shard_map/ppermute | solution.py:400
  138.0 2.5 %collective-permute-start.32 = (f32[32,8,256]{2,1,0:T(8,128)S(1)}, f32[32,8,256]{2,1,0:T(8,128)S(1)}, u32[]{:S(2)}, u32[]{:S(2)}) collective-permute-start(f32[32,8,256]{2,1,0:T(8,128)S(1)} %fusion.19), channel_id=1, source_target_pairs={{0,1},{1,2},{2,3},{3,4},{4,5},{5,6},{6,7},{7,8},{8,9},{9,10},{10,1... | collective-permute-start | bytes 786440 | tf_op jit(solution)/shard_map/ppermute | solution.py:400
  140.5 4.5 %collective-permute-start.33 = (f32[32,8,256]{2,1,0:T(8,128)S(1)}, f32[32,8,256]{2,1,0:T(8,128)S(1)}, u32[]{:S(2)}, u32[]{:S(2)}) collective-permute-start(f32[32,8,256]{2,1,0:T(8,128)S(1)} %fusion.19), channel_id=1, source_target_pairs={{1,0},{2,1},{3,2},{4,3},{5,4},{6,5},{7,6},{8,7},{9,8},{10,9},{11,1... | collective-permute-start | bytes 786440 | tf_op jit(solution)/shard_map/ppermute | solution.py:405
  146.8 5.7 %collective-permute-start.35 = (f32[32,8,256]{2,1,0:T(8,128)S(1)}, f32[32,8,256]{2,1,0:T(8,128)S(1)}, u32[]{:S(2)}, u32[]{:S(2)}) collective-permute-start(f32[32,8,256]{2,1,0:T(8,128)S(1)} %fusion.24), channel_id=1, source_target_pairs={{1,0},{2,1},{3,2},{4,3},{5,4},{6,5},{7,6},{8,7},{9,8},{10,9},{11,1... | collective-permute-start | bytes 786440 | tf_op jit(solution)/shard_map/ppermute | solution.py:405
  152.7 3.0 %collective-permute-start.24 = (f32[32,8,512]{2,1,0:T(8,128)S(1)}, f32[32,8,512]{2,1,0:T(8,128)S(1)}, u32[]{:S(2)}, u32[]{:S(2)}) collective-permute-start(f32[32,8,512]{2,1,0:T(8,128)S(1)} %get-tuple-element.37.refs_0_.refs_4_.v00), channel_id=1, source_target_pairs={{1,0},{2,1},{3,2},{4,3},{5,4},{6,5},{7,6},{8,7},{9,8},{10,9},{11,1... | collective-permute-start | bytes 1572872 | tf_op jit(solution)/shard_map/ppermute | solution.py:405
  155.7 2.9 %collective-permute-start.25 = (f32[32,8,512]{2,1,0:T(8,128)S(1)}, f32[32,8,512]{2,1,0:T(8,128)S(1)}, u32[]{:S(2)}, u32[]{:S(2)}) collective-permute-start(f32[32,8,512]{2,1,0:T(8,128)S(1)} %get-tuple-element.38.refs_1_.refs_5_.v01), channel_id=1, source_target_pairs={{1,0},{2,1},{3,2},{4,3},{5,4},{6,5},{7,6},{8,7},{9,8},{10,9},{11,1... | collective-permute-start | bytes 1572872 | tf_op jit(solution)/shard_map/ppermute | solution.py:405
  161.6 3.8 %collective-permute-start.37 = (f32[32,8,256]{2,1,0:T(8,128)S(1)}, f32[32,8,256]{2,1,0:T(8,128)S(1)}, u32[]{:S(2)}, u32[]{:S(2)}) collective-permute-start(f32[32,8,256]{2,1,0:T(8,128)S(1)} %fusion.29.c_own), channel_id=1, source_target_pairs={{1,0},{2,1},{3,2},{4,3},{5,4},{6,5},{7,6},{8,7},{9,8},{10,9},{11,1... | collective-permute-start | bytes 786440 | tf_op jit(solution)/shard_map/ppermute | solution.py:405
  165.4 1.9 shard_map.47.refs_16_
  167.3 5.3 %collective-permute-done.26.refs_10_ = f32[32,8,512]{2,1,0:T(8,128)S(1)} collective-permute-done((f32[32,8,512]{2,1,0:T(8,128)S(1)}, f32[32,8,512]{2,1,0:T(8,128)S(1)}, u32[]{:S(2)}, u32[]{:S(2)}) %collective-permute-start.26) | collective-permute-done | bytes 524320 | tf_op jit(solution)/shard_map/ppermute | solution.py:405
  172.6 5.6 %collective-permute-done.27.refs_11_ = f32[32,8,512]{2,1,0:T(8,128)S(1)} collective-permute-done((f32[32,8,512]{2,1,0:T(8,128)S(1)}, f32[32,8,512]{2,1,0:T(8,128)S(1)}, u32[]{:S(2)}, u32[]{:S(2)}) %collective-permute-start.27) | collective-permute-done | bytes 524320 | tf_op jit(solution)/shard_map/ppermute | solution.py:405
  178.2 3.4 %shard_map.48.part = f32[4,64,8,512]{3,2,1,0:T(8,128)S(1)} custom-call(f32[32,8,512]{2,1,0:T(8,128)S(1)} %collective-permute-done.20.refs_0_, f32[32,8,512]{2,1,0:T(8,128)S(1)} %collective-permute-done.21.refs_1_, f32[32,8,512]{2,1,0:T(8,128)S(1)} %collective-permute-done.22.refs_2_, f32[32,8,512]{2,1,0:T(8,128)S(1)} %collective-permute-done.23.refs_3_, ...), custom_call_target="tpu_custom_call" | custom-call | flops 100000000 | bytes 14680064 | tf_op jit(solution)/shard_map/pallas_call | solution.py:387
  181.6 5.2 %shard_map.50 = (f32[2,4,512,128]{3,2,1,0:T(8,128)S(1)}, f32[64,1,128]{2,1,0:T(1,128)S(1)}) custom-call(f32[32,8,512]{2,1,0:T(8,128)S(1)} %get-tuple-element.30.refs_0_.refs_4_.f00, f32[32,8,512]{2,1,0:T(8,128)S(1)} %get-tuple-element.31.refs_1_.refs_5_.f01, f32[32,8,512]{2,1,0:T(8,128)S(1)} %get-tuple-element.32.refs_2_.refs_6_.f10, ...), custom_call_target="tpu_custom_call" | custom-call | flops 100000000 | bytes 9753088 | tf_op jit(solution)/shard_map/pallas_call | solution.py:387
  186.8 39.0 %all_to_all.5 = f32[64,1,128]{2,1,0:T(1,128)S(1)} all-to-all(f32[64,1,128]{2,1,0:T(1,128)S(1)} %get-tuple-element.44), channel_id=1, replica_groups=mesh['runs'=4,'gx'=64] {'gx'}, dimensions={0} | all-to-all | bytes 65536 | tf_op jit(solution)/shard_map/all_to_all | solution.py:409
  (114 shorter events, 22.2 us)
Async XLA Ops:
  2.1 24.7 %collective-permute-start = (f32[1,512,512]{2,1,0:T(8,128)S(1)}, f32[1,512,512]{2,1,0:T(8,128)S(1)}, u32[]{:S(2)}, u32[]{:S(2)}) collective-permute-start(f32[1,512,512]{2,1,0:T(8,128)S(1)} %slice.230), channel_id=1, source_target_pairs={{0,1},{1,2},{2,3},{3,4},{4,5},{5,6},{6,7},{7,8},{8,9},{9,10},{10,1... | collective-permute-start | bytes 3145736 | tf_op jit(solution)/shard_map/ppermute | solution.py:400
  5.4 21.4 %collective-permute-start.1 = (f32[1,512,512]{2,1,0:T(8,128)S(1)}, f32[1,512,512]{2,1,0:T(8,128)S(1)}, u32[]{:S(2)}, u32[]{:S(2)}) collective-permute-start(f32[1,512,512]{2,1,0:T(8,128)S(1)} %slice.231), channel_id=1, source_target_pairs={{1,0},{2,1},{3,2},{4,3},{5,4},{6,5},{7,6},{8,7},{9,8},{10,9},{11,1... | collective-permute-start | bytes 3145736 | tf_op jit(solution)/shard_map/ppermute | solution.py:405
  30.5 13.6 %collective-permute-start.10 = (f32[32,8,256]{2,1,0:T(8,128)S(1)}, f32[32,8,256]{2,1,0:T(8,128)S(1)}, u32[]{:S(2)}, u32[]{:S(2)}) collective-permute-start(f32[32,8,256]{2,1,0:T(8,128)S(1)} %get-tuple-element.34), channel_id=1, source_target_pairs={{0,1},{1,2},{2,3},{3,4},{4,5},{5,6},{6,7},{7,8},{8,9},{9,10},{10,1... | collective-permute-start | bytes 786440 | tf_op jit(solution)/shard_map/ppermute | solution.py:400
  30.6 13.5 %collective-permute-start.11 = (f32[32,8,256]{2,1,0:T(8,128)S(1)}, f32[32,8,256]{2,1,0:T(8,128)S(1)}, u32[]{:S(2)}, u32[]{:S(2)}) collective-permute-start(f32[32,8,256]{2,1,0:T(8,128)S(1)} %get-tuple-element.35), channel_id=1, source_target_pairs={{1,0},{2,1},{3,2},{4,3},{5,4},{6,5},{7,6},{8,7},{9,8},{10,9},{11,1... | collective-permute-start | bytes 786440 | tf_op jit(solution)/shard_map/ppermute | solution.py:405
  42.8 35.1 %collective-permute-start.2 = (f32[32,8,512]{2,1,0:T(8,128)S(1)}, f32[32,8,512]{2,1,0:T(8,128)S(1)}, u32[]{:S(2)}, u32[]{:S(2)}) collective-permute-start(f32[32,8,512]{2,1,0:T(8,128)S(1)} %get-tuple-element.30.refs_0_.refs_4_.f00), channel_id=1, source_target_pairs={{0,1},{1,2},{2,3},{3,4},{4,5},{5,6},{6,7},{7,8},{8,9},{9,10},{10,1... | collective-permute-start | bytes 1572872 | tf_op jit(solution)/shard_map/ppermute | solution.py:400
  42.8 35.2 %collective-permute-start.3 = (f32[32,8,512]{2,1,0:T(8,128)S(1)}, f32[32,8,512]{2,1,0:T(8,128)S(1)}, u32[]{:S(2)}, u32[]{:S(2)}) collective-permute-start(f32[32,8,512]{2,1,0:T(8,128)S(1)} %get-tuple-element.31.refs_1_.refs_5_.f01), channel_id=1, source_target_pairs={{0,1},{1,2},{2,3},{3,4},{4,5},{5,6},{6,7},{7,8},{8,9},{9,10},{10,1... | collective-permute-start | bytes 1572872 | tf_op jit(solution)/shard_map/ppermute | solution.py:400
  42.8 38.2 %collective-permute-start.4 = (f32[32,8,512]{2,1,0:T(8,128)S(1)}, f32[32,8,512]{2,1,0:T(8,128)S(1)}, u32[]{:S(2)}, u32[]{:S(2)}) collective-permute-start(f32[32,8,512]{2,1,0:T(8,128)S(1)} %get-tuple-element.32.refs_2_.refs_6_.f10), channel_id=1, source_target_pairs={{0,1},{1,2},{2,3},{3,4},{4,5},{5,6},{6,7},{7,8},{8,9},{9,10},{10,1... | collective-permute-start | bytes 1572872 | tf_op jit(solution)/shard_map/ppermute | solution.py:400
  44.4 18.6 %collective-permute-start.12 = (f32[32,8,256]{2,1,0:T(8,128)S(1)}, f32[32,8,256]{2,1,0:T(8,128)S(1)}, u32[]{:S(2)}, u32[]{:S(2)}) collective-permute-start(f32[32,8,256]{2,1,0:T(8,128)S(1)} %get-tuple-element.48), channel_id=1, source_target_pairs={{0,1},{1,2},{2,3},{3,4},{4,5},{5,6},{6,7},{7,8},{8,9},{9,10},{10,1... | collective-permute-start | bytes 786440 | tf_op jit(solution)/shard_map/ppermute | solution.py:400
  44.5 18.5 %collective-permute-start.13 = (f32[32,8,256]{2,1,0:T(8,128)S(1)}, f32[32,8,256]{2,1,0:T(8,128)S(1)}, u32[]{:S(2)}, u32[]{:S(2)}) collective-permute-start(f32[32,8,256]{2,1,0:T(8,128)S(1)} %get-tuple-element.48), channel_id=1, source_target_pairs={{1,0},{2,1},{3,2},{4,3},{5,4},{6,5},{7,6},{8,7},{9,8},{10,9},{11,1... | collective-permute-start | bytes 786440 | tf_op jit(solution)/shard_map/ppermute | solution.py:405
  63.3 7.9 %collective-permute-start.14 = (f32[32,8,256]{2,1,0:T(8,128)S(1)}, f32[32,8,256]{2,1,0:T(8,128)S(1)}, u32[]{:S(2)}, u32[]{:S(2)}) collective-permute-start(f32[32,8,256]{2,1,0:T(8,128)S(1)} %fusion.4), channel_id=1, source_target_pairs={{0,1},{1,2},{2,3},{3,4},{4,5},{5,6},{6,7},{7,8},{8,9},{9,10},{10,1... | collective-permute-start | bytes 786440 | tf_op jit(solution)/shard_map/ppermute | solution.py:400
  72.1 11.8 %collective-permute-start.16 = (f32[32,8,256]{2,1,0:T(8,128)S(1)}, f32[32,8,256]{2,1,0:T(8,128)S(1)}, u32[]{:S(2)}, u32[]{:S(2)}) collective-permute-start(f32[32,8,256]{2,1,0:T(8,128)S(1)} %fusion.9), channel_id=1, source_target_pairs={{0,1},{1,2},{2,3},{3,4},{4,5},{5,6},{6,7},{7,8},{8,9},{9,10},{10,1... | collective-permute-start | bytes 786440 | tf_op jit(solution)/shard_map/ppermute | solution.py:400
  72.2 12.5 %collective-permute-start.17 = (f32[32,8,256]{2,1,0:T(8,128)S(1)}, f32[32,8,256]{2,1,0:T(8,128)S(1)}, u32[]{:S(2)}, u32[]{:S(2)}) collective-permute-start(f32[32,8,256]{2,1,0:T(8,128)S(1)} %fusion.9), channel_id=1, source_target_pairs={{1,0},{2,1},{3,2},{4,3},{5,4},{6,5},{7,6},{8,7},{9,8},{10,9},{11,1... | collective-permute-start | bytes 786440 | tf_op jit(solution)/shard_map/ppermute | solution.py:405
  78.0 9.4 %collective-permute-start.6 = (f32[32,8,512]{2,1,0:T(8,128)S(1)}, f32[32,8,512]{2,1,0:T(8,128)S(1)}, u32[]{:S(2)}, u32[]{:S(2)}) collective-permute-start(f32[32,8,512]{2,1,0:T(8,128)S(1)} %get-tuple-element.30.refs_0_.refs_4_.f00), channel_id=1, source_target_pairs={{1,0},{2,1},{3,2},{4,3},{5,4},{6,5},{7,6},{8,7},{9,8},{10,9},{11,1... | collective-permute-start | bytes 1572872 | tf_op jit(solution)/shard_map/ppermute | solution.py:405
  81.0 13.7 %collective-permute-start.7 = (f32[32,8,512]{2,1,0:T(8,128)S(1)}, f32[32,8,512]{2,1,0:T(8,128)}, u32[]{:S(2)}, u32[]{:S(2)}) collective-permute-start(f32[32,8,512]{2,1,0:T(8,128)S(1)} %get-tuple-element.31.refs_1_.refs_5_.f01), channel_id=1, source_target_pairs={{1,0},{2,1},{3,2},{4,3},{5,4},{6,5},{7,6},{8,7},{9,8},{10,9},{11,1... | collective-permute-start | bytes 1572872 | tf_op jit(solution)/shard_map/ppermute | solution.py:405
  83.9 14.1 %collective-permute-start.8 = (f32[32,8,512]{2,1,0:T(8,128)S(1)}, f32[32,8,512]{2,1,0:T(8,128)}, u32[]{:S(2)}, u32[]{:S(2)}) collective-permute-start(f32[32,8,512]{2,1,0:T(8,128)S(1)} %get-tuple-element.32.refs_2_.refs_6_.f10), channel_id=1, source_target_pairs={{1,0},{2,1},{3,2},{4,3},{5,4},{6,5},{7,6},{8,7},{9,8},{10,9},{11,1... | collective-permute-start | bytes 1572872 | tf_op jit(solution)/shard_map/ppermute | solution.py:405
  84.7 18.9 %collective-permute-start.9 = (f32[32,8,512]{2,1,0:T(8,128)S(1)}, f32[32,8,512]{2,1,0:T(8,128)}, u32[]{:S(2)}, u32[]{:S(2)}) collective-permute-start(f32[32,8,512]{2,1,0:T(8,128)S(1)} %get-tuple-element.33.refs_3_.refs_7_.f11), channel_id=1, source_target_pairs={{1,0},{2,1},{3,2},{4,3},{5,4},{6,5},{7,6},{8,7},{9,8},{10,9},{11,1... | collective-permute-start | bytes 1572872 | tf_op jit(solution)/shard_map/ppermute | solution.py:405
  85.7 21.4 %collective-permute-start.18 = (f32[32,8,256]{2,1,0:T(8,128)}, f32[32,8,256]{2,1,0:T(8,128)}, u32[]{:S(2)}, u32[]{:S(2)}) collective-permute-start(f32[32,8,256]{2,1,0:T(8,128)} %fusion.14.c_own), channel_id=1, source_target_pairs={{0,1},{1,2},{2,3},{3,4},{4,5},{5,6},{6,7},{7,8},{8,9},{9,10},{10,1... | collective-permute-start | bytes 786440 | tf_op jit(solution)/shard_map/ppermute | solution.py:400
  88.2 18.9 %collective-permute-start.19 = (f32[32,8,256]{2,1,0:T(8,128)}, f32[32,8,256]{2,1,0:T(8,128)}, u32[]{:S(2)}, u32[]{:S(2)}) collective-permute-start(f32[32,8,256]{2,1,0:T(8,128)} %fusion.14.c_own), channel_id=1, source_target_pairs={{1,0},{2,1},{3,2},{4,3},{5,4},{6,5},{7,6},{8,7},{9,8},{10,9},{11,1... | collective-permute-start | bytes 786440 | tf_op jit(solution)/shard_map/ppermute | solution.py:405
  117.4 35.1 %collective-permute-start.20 = (f32[32,8,512]{2,1,0:T(8,128)S(1)}, f32[32,8,512]{2,1,0:T(8,128)S(1)}, u32[]{:S(2)}, u32[]{:S(2)}) collective-permute-start(f32[32,8,512]{2,1,0:T(8,128)S(1)} %get-tuple-element.37.refs_0_.refs_4_.v00), channel_id=1, source_target_pairs={{0,1},{1,2},{2,3},{3,4},{4,5},{5,6},{6,7},{7,8},{8,9},{9,10},{10,1... | collective-permute-start | bytes 1572872 | tf_op jit(solution)/shard_map/ppermute | solution.py:400
  117.4 35.2 %collective-permute-start.21 = (f32[32,8,512]{2,1,0:T(8,128)S(1)}, f32[32,8,512]{2,1,0:T(8,128)S(1)}, u32[]{:S(2)}, u32[]{:S(2)}) collective-permute-start(f32[32,8,512]{2,1,0:T(8,128)S(1)} %get-tuple-element.38.refs_1_.refs_5_.v01), channel_id=1, source_target_pairs={{0,1},{1,2},{2,3},{3,4},{4,5},{5,6},{6,7},{7,8},{8,9},{9,10},{10,1... | collective-permute-start | bytes 1572872 | tf_op jit(solution)/shard_map/ppermute | solution.py:400
  117.4 38.2 %collective-permute-start.22 = (f32[32,8,512]{2,1,0:T(8,128)S(1)}, f32[32,8,512]{2,1,0:T(8,128)S(1)}, u32[]{:S(2)}, u32[]{:S(2)}) collective-permute-start(f32[32,8,512]{2,1,0:T(8,128)S(1)} %get-tuple-element.39.refs_2_.refs_6_.v10), channel_id=1, source_target_pairs={{0,1},{1,2},{2,3},{3,4},{4,5},{5,6},{6,7},{7,8},{8,9},{9,10},{10,1... | collective-permute-start | bytes 1572872 | tf_op jit(solution)/shard_map/ppermute | solution.py:400
  119.6 18.0 %collective-permute-start.30 = (f32[32,8,256]{2,1,0:T(8,128)S(1)}, f32[32,8,256]{2,1,0:T(8,128)S(1)}, u32[]{:S(2)}, u32[]{:S(2)}) collective-permute-start(f32[32,8,256]{2,1,0:T(8,128)S(1)} %get-tuple-element.46), channel_id=1, source_target_pairs={{0,1},{1,2},{2,3},{3,4},{4,5},{5,6},{6,7},{7,8},{8,9},{9,10},{10,1... | collective-permute-start | bytes 786440 | tf_op jit(solution)/shard_map/ppermute | solution.py:400
  119.7 17.9 %collective-permute-start.31 = (f32[32,8,256]{2,1,0:T(8,128)S(1)}, f32[32,8,256]{2,1,0:T(8,128)S(1)}, u32[]{:S(2)}, u32[]{:S(2)}) collective-permute-start(f32[32,8,256]{2,1,0:T(8,128)S(1)} %get-tuple-element.46), channel_id=1, source_target_pairs={{1,0},{2,1},{3,2},{4,3},{5,4},{6,5},{7,6},{8,7},{9,8},{10,9},{11,1... | collective-permute-start | bytes 786440 | tf_op jit(solution)/shard_map/ppermute | solution.py:405
  138.0 8.0 %collective-permute-start.32 = (f32[32,8,256]{2,1,0:T(8,128)S(1)}, f32[32,8,256]{2,1,0:T(8,128)S(1)}, u32[]{:S(2)}, u32[]{:S(2)}) collective-permute-start(f32[32,8,256]{2,1,0:T(8,128)S(1)} %fusion.19), channel_id=1, source_target_pairs={{0,1},{1,2},{2,3},{3,4},{4,5},{5,6},{6,7},{7,8},{8,9},{9,10},{10,1... | collective-permute-start | bytes 786440 | tf_op jit(solution)/shard_map/ppermute | solution.py:400
  146.7 11.8 %collective-permute-start.34 = (f32[32,8,256]{2,1,0:T(8,128)S(1)}, f32[32,8,256]{2,1,0:T(8,128)S(1)}, u32[]{:S(2)}, u32[]{:S(2)}) collective-permute-start(f32[32,8,256]{2,1,0:T(8,128)S(1)} %fusion.24), channel_id=1, source_target_pairs={{0,1},{1,2},{2,3},{3,4},{4,5},{5,6},{6,7},{7,8},{8,9},{9,10},{10,1... | collective-permute-start | bytes 786440 | tf_op jit(solution)/shard_map/ppermute | solution.py:400
  146.8 12.6 %collective-permute-start.35 = (f32[32,8,256]{2,1,0:T(8,128)S(1)}, f32[32,8,256]{2,1,0:T(8,128)S(1)}, u32[]{:S(2)}, u32[]{:S(2)}) collective-permute-start(f32[32,8,256]{2,1,0:T(8,128)S(1)} %fusion.24), channel_id=1, source_target_pairs={{1,0},{2,1},{3,2},{4,3},{5,4},{6,5},{7,6},{8,7},{9,8},{10,9},{11,1... | collective-permute-start | bytes 786440 | tf_op jit(solution)/shard_map/ppermute | solution.py:405
  152.7 8.9 %collective-permute-start.24 = (f32[32,8,512]{2,1,0:T(8,128)S(1)}, f32[32,8,512]{2,1,0:T(8,128)S(1)}, u32[]{:S(2)}, u32[]{:S(2)}) collective-permute-start(f32[32,8,512]{2,1,0:T(8,128)S(1)} %get-tuple-element.37.refs_0_.refs_4_.v00), channel_id=1, source_target_pairs={{1,0},{2,1},{3,2},{4,3},{5,4},{6,5},{7,6},{8,7},{9,8},{10,9},{11,1... | collective-permute-start | bytes 1572872 | tf_op jit(solution)/shard_map/ppermute | solution.py:405
  155.7 11.6 %collective-permute-start.25 = (f32[32,8,512]{2,1,0:T(8,128)S(1)}, f32[32,8,512]{2,1,0:T(8,128)S(1)}, u32[]{:S(2)}, u32[]{:S(2)}) collective-permute-start(f32[32,8,512]{2,1,0:T(8,128)S(1)} %get-tuple-element.38.refs_1_.refs_5_.v01), channel_id=1, source_target_pairs={{1,0},{2,1},{3,2},{4,3},{5,4},{6,5},{7,6},{8,7},{9,8},{10,9},{11,1... | collective-permute-start | bytes 1572872 | tf_op jit(solution)/shard_map/ppermute | solution.py:405
  158.6 14.0 %collective-permute-start.26 = (f32[32,8,512]{2,1,0:T(8,128)S(1)}, f32[32,8,512]{2,1,0:T(8,128)S(1)}, u32[]{:S(2)}, u32[]{:S(2)}) collective-permute-start(f32[32,8,512]{2,1,0:T(8,128)S(1)} %get-tuple-element.39.refs_2_.refs_6_.v10), channel_id=1, source_target_pairs={{1,0},{2,1},{3,2},{4,3},{5,4},{6,5},{7,6},{8,7},{9,8},{10,9},{11,1... | collective-permute-start | bytes 1572872 | tf_op jit(solution)/shard_map/ppermute | solution.py:405
  159.4 18.7 %collective-permute-start.27 = (f32[32,8,512]{2,1,0:T(8,128)S(1)}, f32[32,8,512]{2,1,0:T(8,128)S(1)}, u32[]{:S(2)}, u32[]{:S(2)}) collective-permute-start(f32[32,8,512]{2,1,0:T(8,128)S(1)} %get-tuple-element.40.refs_3_.refs_7_.v11), channel_id=1, source_target_pairs={{1,0},{2,1},{3,2},{4,3},{5,4},{6,5},{7,6},{8,7},{9,8},{10,9},{11,1... | collective-permute-start | bytes 1572872 | tf_op jit(solution)/shard_map/ppermute | solution.py:405
  159.7 21.9 %collective-permute-start.36 = (f32[32,8,256]{2,1,0:T(8,128)S(1)}, f32[32,8,256]{2,1,0:T(8,128)S(1)}, u32[]{:S(2)}, u32[]{:S(2)}) collective-permute-start(f32[32,8,256]{2,1,0:T(8,128)S(1)} %fusion.29.c_own), channel_id=1, source_target_pairs={{0,1},{1,2},{2,3},{3,4},{4,5},{5,6},{6,7},{7,8},{8,9},{9,10},{10,1... | collective-permute-start | bytes 786440 | tf_op jit(solution)/shard_map/ppermute | solution.py:400
  161.6 20.0 %collective-permute-start.37 = (f32[32,8,256]{2,1,0:T(8,128)S(1)}, f32[32,8,256]{2,1,0:T(8,128)S(1)}, u32[]{:S(2)}, u32[]{:S(2)}) collective-permute-start(f32[32,8,256]{2,1,0:T(8,128)S(1)} %fusion.29.c_own), channel_id=1, source_target_pairs={{1,0},{2,1},{3,2},{4,3},{5,4},{6,5},{7,6},{8,7},{9,8},{10,9},{11,1... | collective-permute-start | bytes 786440 | tf_op jit(solution)/shard_map/ppermute | solution.py:405
  (14 other events, 123.4 us)

commit v5 on v4

--- a/solution.py
+++ b/solution.py
@@ -108,7 +108,7 @@
 
 
 def source_kernel(
-    X, D, curved, rest, left, right, table, f00, f01, f10, f11, s0, s1, total, XH, DH, G, T, acc
+    X, D, curved, rest, left, right, table, f00, f01, f10, f11, s0, s1, total, shift, XH, DH, G, T, acc
 ):
     nj = X.shape[1] - 2
     half = nj // 2
@@ -139,6 +139,7 @@
     folded = acc[...]
     width = folded.shape[1]
     total[...] = sum(folded[:, k : k + LANES] for k in range(0, width, LANES))
+    shift[...] = jnp.broadcast_to(fold_row(total[...]) * (1.0 / (2 * nj * acc.size)), shift.shape)
     pair_up(G, 0, table, s0)
     pair_up(G, 1, table, s1)
 
@@ -390,7 +391,7 @@
         in_specs=[VMEM] * len(args),
         out_specs=out_specs or [VMEM] * len(outs),
         scratch_shapes=[pltpu.VMEM(s, jnp.float32) for s in scratch],
-        compiler_params=pltpu.CompilerParams(vmem_limit_bytes=24 * 2**20),
+        compiler_params=pltpu.CompilerParams(vmem_limit_bytes=20 * 2**20),
         cost_estimate=pl.CostEstimate(flops=flops, bytes_accessed=moved, transcendentals=0),
     )(*args)
 
@@ -461,11 +462,10 @@
     prepared = call(
         prepare_kernel, (potential,), [(2, *tall), (2, *tall), (2, nj, 8, nz), (2, nj, 8, nz)], [tiles], 10**8
     )
-    *forcing, s0, s1, total = call(
-        source_kernel, (*prepared, left, right, pairs), [chunk] * 4 + [coarse] * 2 + [(8, LANES)],
+    *forcing, s0, s1, total, shift = call(
+        source_kernel, (*prepared, left, right, pairs), [chunk] * 4 + [coarse] * 2 + [(8, LANES), (8, nz)],
         [(2, *tall), (2, *tall), (2, nc, 8, nz), tiles, (8, nz)], 10**8,
     )
-    shift = jnp.broadcast_to(jnp.sum(total) / share, (8, nz))
     (local,) = call(
         rhs_first_kernel, (*forcing, pairs), [coarse], [(1, *tall), (1, nc, 8, nz)], 3 * 10**7
     )

time: 228 us -> 225 us (0.987)
  Pallas kernels: 34.1 us -> 30.6 us
  waiting for transfers between devices: 48.1 us -> 51.4 us
    pallas_call x10, Pallas kernels: 32.3 us -> 28.7 us  [call(): pl.pallas_call(kernel, out_shape=[jax.ShapeDtypeStruct(o, jnp.float32) fo...]
    ppermute x19, waiting for transfers between devices: 21.3 us -> 24.5 us  [from_right(): return lax.ppermute(x, 'gx', [((i + 1) % count, i) for i in range(count)])]
  transfers between devices with their start and end apart: 38 -> 38, of which waited for: 12 -> 15; matrix products, arithmetic and copies ran while one was open for 2% -> 1% of each run, Pallas kernels for 7% -> 6%
where the time goes in v5:
time: 225 us
  starting transfers between devices  98.4 us (44%)
  waiting for transfers between devices  51.4 us (23%)
  blocking collectives  39 us (17%)
  Pallas kernels  30.6 us (14%)
  local copies, waits for them, and re-layouts  3.09 us (1%)
    ppermute x19, starting transfers between devices, from_right(): return lax.ppermute(x, 'gx', [((i + 1) % count, i) for i in range(count)])  86 us
    all_to_all x1, blocking collectives, gathered(): return lax.all_to_all(rows, 'gx', 0, 0, tiled=True)  39 us
    pallas_call x10, Pallas kernels, call(): pl.pallas_call(kernel, out_shape=[jax.ShapeDtypeStruct(o, jnp.float32) fo...  28.7 us
    ppermute x19, waiting for transfers between devices, from_left(): return lax.ppermute(x, 'gx', [(i, (i + 1) % count) for i in range(count)])  26.9 us
    ppermute x19, waiting for transfers between devices, from_right(): return lax.ppermute(x, 'gx', [((i + 1) % count, i) for i in range(count)])  24.5 us
    ppermute x19, starting transfers between devices, from_left(): return lax.ppermute(x, 'gx', [(i, (i + 1) % count) for i in range(count)])  12.4 us
  transfers between devices with their start and end apart: 38, of which 15 were waited for; matrix products, arithmetic and copies ran while one was open for 1% of the time, Pallas kernels for 6%

profile of v5, /device:TPU:37, one launch (start us, length us, event | category | flops | bytes accessed | tf_op | source)
XLA Modules:
  0.0 225.1 jit_solution(6842150064551422126)
XLA Ops:
  2.1 3.2 %collective-permute-start = (f32[1,512,512]{2,1,0:T(8,128)S(1)}, f32[1,512,512]{2,1,0:T(8,128)S(1)}, u32[]{:S(2)}, u32[]{:S(2)}) collective-permute-start(f32[1,512,512]{2,1,0:T(8,128)S(1)} %slice.230), channel_id=1, source_target_pairs={{0,1},{1,2},{2,3},{3,4},{4,5},{5,6},{6,7},{7,8},{8,9},{9,10},{10,1... | collective-permute-start | bytes 3145736 | tf_op jit(solution)/shard_map/ppermute | solution.py:401
  5.4 17.7 %collective-permute-start.1 = (f32[1,512,512]{2,1,0:T(8,128)S(1)}, f32[1,512,512]{2,1,0:T(8,128)S(1)}, u32[]{:S(2)}, u32[]{:S(2)}) collective-permute-start(f32[1,512,512]{2,1,0:T(8,128)S(1)} %slice.231), channel_id=1, source_target_pairs={{1,0},{2,1},{3,2},{4,3},{5,4},{6,5},{7,6},{8,7},{9,8},{10,9},{11,1... | collective-permute-start | bytes 3145736 | tf_op jit(solution)/shard_map/ppermute | solution.py:406
  23.1 3.7 %shard_map.41 = (f32[2,66,8,512]{3,2,1,0:T(8,128)S(1)}, f32[2,66,8,512]{3,2,1,0:T(8,128)S(1)}, f32[2,64,8,512]{3,2,1,0:T(8,128)S(1)}, f32[2,64,8,512]{3,2,1,0:T(8,128)S(1)}) custom-call(f32[2,512,512]{2,1,0:T(8,128)S(1)} %copy-done), custom_call_target="tpu_custom_call" | custom-call | flops 100000000 | bytes 10616832 | tf_op jit(solution)/shard_map/pallas_call | solution.py:388
  26.8 3.7 %shard_map.42 = (f32[32,8,512]{2,1,0:T(8,128)S(1)}, f32[32,8,512]{2,1,0:T(8,128)S(1)}, f32[32,8,512]{2,1,0:T(8,128)S(1)}, f32[32,8,512]{2,1,0:T(8,128)S(1)}, f32...) custom-call(f32[2,66,8,512]{3,2,1,0:T(8,128)S(1)} %get-tuple-element.26.X, ...), custom_call_target="tpu_custom_call" | custom-call | flops 100000000 | bytes 13783040 | tf_op jit(solution)/shard_map/pallas_call | solution.py:388
  30.6 12.1 %collective-permute-start.11 = (f32[32,8,256]{2,1,0:T(8,128)S(1)}, f32[32,8,256]{2,1,0:T(8,128)S(1)}, u32[]{:S(2)}, u32[]{:S(2)}) collective-permute-start(f32[32,8,256]{2,1,0:T(8,128)S(1)} %get-tuple-element.36), channel_id=1, source_target_pairs={{1,0},{2,1},{3,2},{4,3},{5,4},{6,5},{7,6},{8,7},{9,8},{10,9},{11,1... | collective-permute-start | bytes 786440 | tf_op jit(solution)/shard_map/ppermute | solution.py:406
  44.4 5.8 %collective-permute-start.13 = (f32[32,8,256]{2,1,0:T(8,128)S(1)}, f32[32,8,256]{2,1,0:T(8,128)S(1)}, u32[]{:S(2)}, u32[]{:S(2)}) collective-permute-start(f32[32,8,256]{2,1,0:T(8,128)S(1)} %get-tuple-element.50), channel_id=1, source_target_pairs={{1,0},{2,1},{3,2},{4,3},{5,4},{6,5},{7,6},{8,7},{9,8},{10,9},{11,1... | collective-permute-start | bytes 786440 | tf_op jit(solution)/shard_map/ppermute | solution.py:406
  50.4 12.6 %collective-permute-done.12 = f32[32,8,256]{2,1,0:T(8,128)S(1)} collective-permute-done((f32[32,8,256]{2,1,0:T(8,128)S(1)}, f32[32,8,256]{2,1,0:T(8,128)S(1)}, u32[]{:S(2)}, u32[]{:S(2)}) %collective-permute-start.12) | collective-permute-done | bytes 262176 | tf_op jit(solution)/shard_map/ppermute | solution.py:401
  63.3 2.5 %collective-permute-start.14 = (f32[32,8,256]{2,1,0:T(8,128)S(1)}, f32[32,8,256]{2,1,0:T(8,128)S(1)}, u32[]{:S(2)}, u32[]{:S(2)}) collective-permute-start(f32[32,8,256]{2,1,0:T(8,128)S(1)} %fusion.4), channel_id=1, source_target_pairs={{0,1},{1,2},{2,3},{3,4},{4,5},{5,6},{6,7},{7,8},{8,9},{9,10},{10,1... | collective-permute-start | bytes 786440 | tf_op jit(solution)/shard_map/ppermute | solution.py:401
  65.8 4.4 %collective-permute-start.15 = (f32[32,8,256]{2,1,0:T(8,128)S(1)}, f32[32,8,256]{2,1,0:T(8,128)S(1)}, u32[]{:S(2)}, u32[]{:S(2)}) collective-permute-start(f32[32,8,256]{2,1,0:T(8,128)S(1)} %fusion.4), channel_id=1, source_target_pairs={{1,0},{2,1},{3,2},{4,3},{5,4},{6,5},{7,6},{8,7},{9,8},{10,9},{11,1... | collective-permute-start | bytes 786440 | tf_op jit(solution)/shard_map/ppermute | solution.py:406
  72.1 5.6 %collective-permute-start.17 = (f32[32,8,256]{2,1,0:T(8,128)S(1)}, f32[32,8,256]{2,1,0:T(8,128)S(1)}, u32[]{:S(2)}, u32[]{:S(2)}) collective-permute-start(f32[32,8,256]{2,1,0:T(8,128)S(1)} %fusion.9), channel_id=1, source_target_pairs={{1,0},{2,1},{3,2},{4,3},{5,4},{6,5},{7,6},{8,7},{9,8},{10,9},{11,1... | collective-permute-start | bytes 786440 | tf_op jit(solution)/shard_map/ppermute | solution.py:406
  77.9 3.0 %collective-permute-start.6 = (f32[32,8,512]{2,1,0:T(8,128)S(1)}, f32[32,8,512]{2,1,0:T(8,128)S(1)}, u32[]{:S(2)}, u32[]{:S(2)}) collective-permute-start(f32[32,8,512]{2,1,0:T(8,128)S(1)} %get-tuple-element.31.refs_0_.refs_4_.f00), channel_id=1, source_target_pairs={{1,0},{2,1},{3,2},{4,3},{5,4},{6,5},{7,6},{8,7},{9,8},{10,9},{11,1... | collective-permute-start | bytes 1572872 | tf_op jit(solution)/shard_map/ppermute | solution.py:406
  80.9 2.9 %collective-permute-start.7 = (f32[32,8,512]{2,1,0:T(8,128)S(1)}, f32[32,8,512]{2,1,0:T(8,128)S(1)}, u32[]{:S(2)}, u32[]{:S(2)}) collective-permute-start(f32[32,8,512]{2,1,0:T(8,128)S(1)} %get-tuple-element.32.refs_1_.refs_5_.f01), channel_id=1, source_target_pairs={{1,0},{2,1},{3,2},{4,3},{5,4},{6,5},{7,6},{8,7},{9,8},{10,9},{11,1... | collective-permute-start | bytes 1572872 | tf_op jit(solution)/shard_map/ppermute | solution.py:406
  86.9 3.8 %collective-permute-start.19 = (f32[32,8,256]{2,1,0:T(8,128)S(1)}, f32[32,8,256]{2,1,0:T(8,128)S(1)}, u32[]{:S(2)}, u32[]{:S(2)}) collective-permute-start(f32[32,8,256]{2,1,0:T(8,128)S(1)} %fusion.14.c_own), channel_id=1, source_target_pairs={{1,0},{2,1},{3,2},{4,3},{5,4},{6,5},{7,6},{8,7},{9,8},{10,9},{11,1... | collective-permute-start | bytes 786440 | tf_op jit(solution)/shard_map/ppermute | solution.py:406
  92.5 5.3 %collective-permute-done.8.refs_10_ = f32[32,8,512]{2,1,0:T(8,128)S(1)} collective-permute-done((f32[32,8,512]{2,1,0:T(8,128)S(1)}, f32[32,8,512]{2,1,0:T(8,128)S(1)}, u32[]{:S(2)}, u32[]{:S(2)}) %collective-permute-start.8) | collective-permute-done | bytes 524320 | tf_op jit(solution)/shard_map/ppermute | solution.py:406
  97.8 5.6 %collective-permute-done.9.refs_11_ = f32[32,8,512]{2,1,0:T(8,128)S(1)} collective-permute-done((f32[32,8,512]{2,1,0:T(8,128)S(1)}, f32[32,8,512]{2,1,0:T(8,128)S(1)}, u32[]{:S(2)}, u32[]{:S(2)}) %collective-permute-start.9) | collective-permute-done | bytes 524320 | tf_op jit(solution)/shard_map/ppermute | solution.py:406
  103.4 2.1 shard_map.44.part
  106.2 5.2 %shard_map.46 = (f32[32,8,512]{2,1,0:T(8,128)S(1)}, f32[32,8,512]{2,1,0:T(8,128)S(1)}, f32[32,8,512]{2,1,0:T(8,128)S(1)}, f32[32,8,512]{2,1,0:T(8,128)S(1)}, f32...) custom-call(f32[32,8,512]{2,1,0:T(8,128)S(1)} %get-tuple-element.31.refs_0_.refs_4_.f00, ...), custom_call_target="tpu_custom_call" | custom-call | flops 100000000 | bytes 10240512 | tf_op jit(solution)/shard_map/pallas_call | solution.py:388
  111.6 4.0 %collective-permute-start.29 = (f32[32,8,256]{2,1,0:T(8,128)S(1)}, f32[32,8,256]{2,1,0:T(8,128)S(1)}, u32[]{:S(2)}, u32[]{:S(2)}) collective-permute-start(f32[32,8,256]{2,1,0:T(8,128)S(1)} %get-tuple-element.43), channel_id=1, source_target_pairs={{1,0},{2,1},{3,2},{4,3},{5,4},{6,5},{7,6},{8,7},{9,8},{10,9},{11,1... | collective-permute-start | bytes 786440 | tf_op jit(solution)/shard_map/ppermute | solution.py:406
  117.7 5.3 %collective-permute-start.31 = (f32[32,8,256]{2,1,0:T(8,128)S(1)}, f32[32,8,256]{2,1,0:T(8,128)S(1)}, u32[]{:S(2)}, u32[]{:S(2)}) collective-permute-start(f32[32,8,256]{2,1,0:T(8,128)S(1)} %get-tuple-element.48), channel_id=1, source_target_pairs={{1,0},{2,1},{3,2},{4,3},{5,4},{6,5},{7,6},{8,7},{9,8},{10,9},{11,1... | collective-permute-start | bytes 786440 | tf_op jit(solution)/shard_map/ppermute | solution.py:406
  123.1 12.6 %collective-permute-done.30 = f32[32,8,256]{2,1,0:T(8,128)S(1)} collective-permute-done((f32[32,8,256]{2,1,0:T(8,128)S(1)}, f32[32,8,256]{2,1,0:T(8,128)S(1)}, u32[]{:S(2)}, u32[]{:S(2)}) %collective-permute-start.30) | collective-permute-done | bytes 262176 | tf_op jit(solution)/shard_map/ppermute | solution.py:401
  136.1 2.5 %collective-permute-start.32 = (f32[32,8,256]{2,1,0:T(8,128)S(1)}, f32[32,8,256]{2,1,0:T(8,128)S(1)}, u32[]{:S(2)}, u32[]{:S(2)}) collective-permute-start(f32[32,8,256]{2,1,0:T(8,128)S(1)} %fusion.19), channel_id=1, source_target_pairs={{0,1},{1,2},{2,3},{3,4},{4,5},{5,6},{6,7},{7,8},{8,9},{9,10},{10,1... | collective-permute-start | bytes 786440 | tf_op jit(solution)/shard_map/ppermute | solution.py:401
  138.6 4.4 %collective-permute-start.33 = (f32[32,8,256]{2,1,0:T(8,128)S(1)}, f32[32,8,256]{2,1,0:T(8,128)S(1)}, u32[]{:S(2)}, u32[]{:S(2)}) collective-permute-start(f32[32,8,256]{2,1,0:T(8,128)S(1)} %fusion.19), channel_id=1, source_target_pairs={{1,0},{2,1},{3,2},{4,3},{5,4},{6,5},{7,6},{8,7},{9,8},{10,9},{11,1... | collective-permute-start | bytes 786440 | tf_op jit(solution)/shard_map/ppermute | solution.py:406
  144.9 5.6 %collective-permute-start.35 = (f32[32,8,256]{2,1,0:T(8,128)S(1)}, f32[32,8,256]{2,1,0:T(8,128)S(1)}, u32[]{:S(2)}, u32[]{:S(2)}) collective-permute-start(f32[32,8,256]{2,1,0:T(8,128)S(1)} %fusion.24), channel_id=1, source_target_pairs={{1,0},{2,1},{3,2},{4,3},{5,4},{6,5},{7,6},{8,7},{9,8},{10,9},{11,1... | collective-permute-start | bytes 786440 | tf_op jit(solution)/shard_map/ppermute | solution.py:406
  150.7 3.0 %collective-permute-start.24 = (f32[32,8,512]{2,1,0:T(8,128)S(1)}, f32[32,8,512]{2,1,0:T(8,128)S(1)}, u32[]{:S(2)}, u32[]{:S(2)}) collective-permute-start(f32[32,8,512]{2,1,0:T(8,128)S(1)} %get-tuple-element.38.refs_0_.refs_4_.v00), channel_id=1, source_target_pairs={{1,0},{2,1},{3,2},{4,3},{5,4},{6,5},{7,6},{8,7},{9,8},{10,9},{11,1... | collective-permute-start | bytes 1572872 | tf_op jit(solution)/shard_map/ppermute | solution.py:406
  153.7 2.9 %collective-permute-start.25 = (f32[32,8,512]{2,1,0:T(8,128)S(1)}, f32[32,8,512]{2,1,0:T(8,128)S(1)}, u32[]{:S(2)}, u32[]{:S(2)}) collective-permute-start(f32[32,8,512]{2,1,0:T(8,128)S(1)} %get-tuple-element.39.refs_1_.refs_5_.v01), channel_id=1, source_target_pairs={{1,0},{2,1},{3,2},{4,3},{5,4},{6,5},{7,6},{8,7},{9,8},{10,9},{11,1... | collective-permute-start | bytes 1572872 | tf_op jit(solution)/shard_map/ppermute | solution.py:406
  159.6 3.8 %collective-permute-start.37 = (f32[32,8,256]{2,1,0:T(8,128)S(1)}, f32[32,8,256]{2,1,0:T(8,128)S(1)}, u32[]{:S(2)}, u32[]{:S(2)}) collective-permute-start(f32[32,8,256]{2,1,0:T(8,128)S(1)} %fusion.29.c_own), channel_id=1, source_target_pairs={{1,0},{2,1},{3,2},{4,3},{5,4},{6,5},{7,6},{8,7},{9,8},{10,9},{11,1... | collective-permute-start | bytes 786440 | tf_op jit(solution)/shard_map/ppermute | solution.py:406
  163.4 1.9 shard_map.47.refs_16_
  165.3 5.3 %collective-permute-done.26.refs_10_ = f32[32,8,512]{2,1,0:T(8,128)S(1)} collective-permute-done((f32[32,8,512]{2,1,0:T(8,128)S(1)}, f32[32,8,512]{2,1,0:T(8,128)S(1)}, u32[]{:S(2)}, u32[]{:S(2)}) %collective-permute-start.26) | collective-permute-done | bytes 524320 | tf_op jit(solution)/shard_map/ppermute | solution.py:406
  170.6 5.6 %collective-permute-done.27.refs_11_ = f32[32,8,512]{2,1,0:T(8,128)S(1)} collective-permute-done((f32[32,8,512]{2,1,0:T(8,128)S(1)}, f32[32,8,512]{2,1,0:T(8,128)S(1)}, u32[]{:S(2)}, u32[]{:S(2)}) %collective-permute-start.27) | collective-permute-done | bytes 524320 | tf_op jit(solution)/shard_map/ppermute | solution.py:406
  176.2 2.3 %shard_map.48.part = f32[4,64,8,512]{3,2,1,0:T(8,128)S(1)} custom-call(f32[32,8,512]{2,1,0:T(8,128)S(1)} %collective-permute-done.20.refs_0_, f32[32,8,512]{2,1,0:T(8,128)S(1)} %collective-permute-done.21.refs_1_, f32[32,8,512]{2,1,0:T(8,128)S(1)} %collective-permute-done.22.refs_2_, f32[32,8,512]{2,1,0:T(8,128)S(1)} %collective-permute-done.23.refs_3_, ...), custom_call_target="tpu_custom_call" | custom-call | flops 100000000 | bytes 14680064 | tf_op jit(solution)/shard_map/pallas_call | solution.py:388
  179.0 5.2 %shard_map.50 = (f32[2,4,512,128]{3,2,1,0:T(8,128)S(1)}, f32[64,1,128]{2,1,0:T(1,128)S(1)}) custom-call(f32[32,8,512]{2,1,0:T(8,128)S(1)} %get-tuple-element.31.refs_0_.refs_4_.f00, f32[32,8,512]{2,1,0:T(8,128)S(1)} %get-tuple-element.32.refs_1_.refs_5_.f01, f32[32,8,512]{2,1,0:T(8,128)S(1)} %get-tuple-element.33.refs_2_.refs_6_.f10, ...), custom_call_target="tpu_custom_call" | custom-call | flops 100000000 | bytes 9753088 | tf_op jit(solution)/shard_map/pallas_call | solution.py:388
  184.2 39.0 %all_to_all.5 = f32[64,1,128]{2,1,0:T(1,128)S(1)} all-to-all(f32[64,1,128]{2,1,0:T(1,128)S(1)} %get-tuple-element.46), channel_id=1, replica_groups=mesh['runs'=4,'gx'=64] {'gx'}, dimensions={0} | all-to-all | bytes 65536 | tf_op jit(solution)/shard_map/all_to_all | solution.py:410
  (100 shorter events, 21.3 us)
Async XLA Ops:
  2.1 24.7 %collective-permute-start = (f32[1,512,512]{2,1,0:T(8,128)S(1)}, f32[1,512,512]{2,1,0:T(8,128)S(1)}, u32[]{:S(2)}, u32[]{:S(2)}) collective-permute-start(f32[1,512,512]{2,1,0:T(8,128)S(1)} %slice.230), channel_id=1, source_target_pairs={{0,1},{1,2},{2,3},{3,4},{4,5},{5,6},{6,7},{7,8},{8,9},{9,10},{10,1... | collective-permute-start | bytes 3145736 | tf_op jit(solution)/shard_map/ppermute | solution.py:401
  5.4 21.4 %collective-permute-start.1 = (f32[1,512,512]{2,1,0:T(8,128)S(1)}, f32[1,512,512]{2,1,0:T(8,128)S(1)}, u32[]{:S(2)}, u32[]{:S(2)}) collective-permute-start(f32[1,512,512]{2,1,0:T(8,128)S(1)} %slice.231), channel_id=1, source_target_pairs={{1,0},{2,1},{3,2},{4,3},{5,4},{6,5},{7,6},{8,7},{9,8},{10,9},{11,1... | collective-permute-start | bytes 3145736 | tf_op jit(solution)/shard_map/ppermute | solution.py:406
  30.6 13.6 %collective-permute-start.10 = (f32[32,8,256]{2,1,0:T(8,128)S(1)}, f32[32,8,256]{2,1,0:T(8,128)S(1)}, u32[]{:S(2)}, u32[]{:S(2)}) collective-permute-start(f32[32,8,256]{2,1,0:T(8,128)S(1)} %get-tuple-element.35), channel_id=1, source_target_pairs={{0,1},{1,2},{2,3},{3,4},{4,5},{5,6},{6,7},{7,8},{8,9},{9,10},{10,1... | collective-permute-start | bytes 786440 | tf_op jit(solution)/shard_map/ppermute | solution.py:401
  30.6 13.5 %collective-permute-start.11 = (f32[32,8,256]{2,1,0:T(8,128)S(1)}, f32[32,8,256]{2,1,0:T(8,128)S(1)}, u32[]{:S(2)}, u32[]{:S(2)}) collective-permute-start(f32[32,8,256]{2,1,0:T(8,128)S(1)} %get-tuple-element.36), channel_id=1, source_target_pairs={{1,0},{2,1},{3,2},{4,3},{5,4},{6,5},{7,6},{8,7},{9,8},{10,9},{11,1... | collective-permute-start | bytes 786440 | tf_op jit(solution)/shard_map/ppermute | solution.py:406
  42.8 35.1 %collective-permute-start.2 = (f32[32,8,512]{2,1,0:T(8,128)S(1)}, f32[32,8,512]{2,1,0:T(8,128)S(1)}, u32[]{:S(2)}, u32[]{:S(2)}) collective-permute-start(f32[32,8,512]{2,1,0:T(8,128)S(1)} %get-tuple-element.31.refs_0_.refs_4_.f00), channel_id=1, source_target_pairs={{0,1},{1,2},{2,3},{3,4},{4,5},{5,6},{6,7},{7,8},{8,9},{9,10},{10,1... | collective-permute-start | bytes 1572872 | tf_op jit(solution)/shard_map/ppermute | solution.py:401
  42.8 35.2 %collective-permute-start.3 = (f32[32,8,512]{2,1,0:T(8,128)S(1)}, f32[32,8,512]{2,1,0:T(8,128)S(1)}, u32[]{:S(2)}, u32[]{:S(2)}) collective-permute-start(f32[32,8,512]{2,1,0:T(8,128)S(1)} %get-tuple-element.32.refs_1_.refs_5_.f01), channel_id=1, source_target_pairs={{0,1},{1,2},{2,3},{3,4},{4,5},{5,6},{6,7},{7,8},{8,9},{9,10},{10,1... | collective-permute-start | bytes 1572872 | tf_op jit(solution)/shard_map/ppermute | solution.py:401
  42.8 38.2 %collective-permute-start.4 = (f32[32,8,512]{2,1,0:T(8,128)S(1)}, f32[32,8,512]{2,1,0:T(8,128)S(1)}, u32[]{:S(2)}, u32[]{:S(2)}) collective-permute-start(f32[32,8,512]{2,1,0:T(8,128)S(1)} %get-tuple-element.33.refs_2_.refs_6_.f10), channel_id=1, source_target_pairs={{0,1},{1,2},{2,3},{3,4},{4,5},{5,6},{6,7},{7,8},{8,9},{9,10},{10,1... | collective-permute-start | bytes 1572872 | tf_op jit(solution)/shard_map/ppermute | solution.py:401
  44.4 18.6 %collective-permute-start.12 = (f32[32,8,256]{2,1,0:T(8,128)S(1)}, f32[32,8,256]{2,1,0:T(8,128)S(1)}, u32[]{:S(2)}, u32[]{:S(2)}) collective-permute-start(f32[32,8,256]{2,1,0:T(8,128)S(1)} %get-tuple-element.50), channel_id=1, source_target_pairs={{0,1},{1,2},{2,3},{3,4},{4,5},{5,6},{6,7},{7,8},{8,9},{9,10},{10,1... | collective-permute-start | bytes 786440 | tf_op jit(solution)/shard_map/ppermute | solution.py:401
  44.4 18.5 %collective-permute-start.13 = (f32[32,8,256]{2,1,0:T(8,128)S(1)}, f32[32,8,256]{2,1,0:T(8,128)S(1)}, u32[]{:S(2)}, u32[]{:S(2)}) collective-permute-start(f32[32,8,256]{2,1,0:T(8,128)S(1)} %get-tuple-element.50), channel_id=1, source_target_pairs={{1,0},{2,1},{3,2},{4,3},{5,4},{6,5},{7,6},{8,7},{9,8},{10,9},{11,1... | collective-permute-start | bytes 786440 | tf_op jit(solution)/shard_map/ppermute | solution.py:406
  63.3 7.9 %collective-permute-start.14 = (f32[32,8,256]{2,1,0:T(8,128)S(1)}, f32[32,8,256]{2,1,0:T(8,128)S(1)}, u32[]{:S(2)}, u32[]{:S(2)}) collective-permute-start(f32[32,8,256]{2,1,0:T(8,128)S(1)} %fusion.4), channel_id=1, source_target_pairs={{0,1},{1,2},{2,3},{3,4},{4,5},{5,6},{6,7},{7,8},{8,9},{9,10},{10,1... | collective-permute-start | bytes 786440 | tf_op jit(solution)/shard_map/ppermute | solution.py:401
  72.0 11.8 %collective-permute-start.16 = (f32[32,8,256]{2,1,0:T(8,128)S(1)}, f32[32,8,256]{2,1,0:T(8,128)S(1)}, u32[]{:S(2)}, u32[]{:S(2)}) collective-permute-start(f32[32,8,256]{2,1,0:T(8,128)S(1)} %fusion.9), channel_id=1, source_target_pairs={{0,1},{1,2},{2,3},{3,4},{4,5},{5,6},{6,7},{7,8},{8,9},{9,10},{10,1... | collective-permute-start | bytes 786440 | tf_op jit(solution)/shard_map/ppermute | solution.py:401
  72.1 12.6 %collective-permute-start.17 = (f32[32,8,256]{2,1,0:T(8,128)S(1)}, f32[32,8,256]{2,1,0:T(8,128)S(1)}, u32[]{:S(2)}, u32[]{:S(2)}) collective-permute-start(f32[32,8,256]{2,1,0:T(8,128)S(1)} %fusion.9), channel_id=1, source_target_pairs={{1,0},{2,1},{3,2},{4,3},{5,4},{6,5},{7,6},{8,7},{9,8},{10,9},{11,1... | collective-permute-start | bytes 786440 | tf_op jit(solution)/shard_map/ppermute | solution.py:406
  77.9 8.9 %collective-permute-start.6 = (f32[32,8,512]{2,1,0:T(8,128)S(1)}, f32[32,8,512]{2,1,0:T(8,128)S(1)}, u32[]{:S(2)}, u32[]{:S(2)}) collective-permute-start(f32[32,8,512]{2,1,0:T(8,128)S(1)} %get-tuple-element.31.refs_0_.refs_4_.f00), channel_id=1, source_target_pairs={{1,0},{2,1},{3,2},{4,3},{5,4},{6,5},{7,6},{8,7},{9,8},{10,9},{11,1... | collective-permute-start | bytes 1572872 | tf_op jit(solution)/shard_map/ppermute | solution.py:406
  80.9 11.6 %collective-permute-start.7 = (f32[32,8,512]{2,1,0:T(8,128)S(1)}, f32[32,8,512]{2,1,0:T(8,128)S(1)}, u32[]{:S(2)}, u32[]{:S(2)}) collective-permute-start(f32[32,8,512]{2,1,0:T(8,128)S(1)} %get-tuple-element.32.refs_1_.refs_5_.f01), channel_id=1, source_target_pairs={{1,0},{2,1},{3,2},{4,3},{5,4},{6,5},{7,6},{8,7},{9,8},{10,9},{11,1... | collective-permute-start | bytes 1572872 | tf_op jit(solution)/shard_map/ppermute | solution.py:406
  83.8 14.0 %collective-permute-start.8 = (f32[32,8,512]{2,1,0:T(8,128)S(1)}, f32[32,8,512]{2,1,0:T(8,128)S(1)}, u32[]{:S(2)}, u32[]{:S(2)}) collective-permute-start(f32[32,8,512]{2,1,0:T(8,128)S(1)} %get-tuple-element.33.refs_2_.refs_6_.f10), channel_id=1, source_target_pairs={{1,0},{2,1},{3,2},{4,3},{5,4},{6,5},{7,6},{8,7},{9,8},{10,9},{11,1... | collective-permute-start | bytes 1572872 | tf_op jit(solution)/shard_map/ppermute | solution.py:406
  84.7 18.7 %collective-permute-start.9 = (f32[32,8,512]{2,1,0:T(8,128)S(1)}, f32[32,8,512]{2,1,0:T(8,128)S(1)}, u32[]{:S(2)}, u32[]{:S(2)}) collective-permute-start(f32[32,8,512]{2,1,0:T(8,128)S(1)} %get-tuple-element.34.refs_3_.refs_7_.f11), channel_id=1, source_target_pairs={{1,0},{2,1},{3,2},{4,3},{5,4},{6,5},{7,6},{8,7},{9,8},{10,9},{11,1... | collective-permute-start | bytes 1572872 | tf_op jit(solution)/shard_map/ppermute | solution.py:406
  84.9 20.6 %collective-permute-start.18 = (f32[32,8,256]{2,1,0:T(8,128)S(1)}, f32[32,8,256]{2,1,0:T(8,128)S(1)}, u32[]{:S(2)}, u32[]{:S(2)}) collective-permute-start(f32[32,8,256]{2,1,0:T(8,128)S(1)} %fusion.14.c_own), channel_id=1, source_target_pairs={{0,1},{1,2},{2,3},{3,4},{4,5},{5,6},{6,7},{7,8},{8,9},{9,10},{10,1... | collective-permute-start | bytes 786440 | tf_op jit(solution)/shard_map/ppermute | solution.py:401
  86.9 19.4 %collective-permute-start.19 = (f32[32,8,256]{2,1,0:T(8,128)S(1)}, f32[32,8,256]{2,1,0:T(8,128)S(1)}, u32[]{:S(2)}, u32[]{:S(2)}) collective-permute-start(f32[32,8,256]{2,1,0:T(8,128)S(1)} %fusion.14.c_own), channel_id=1, source_target_pairs={{1,0},{2,1},{3,2},{4,3},{5,4},{6,5},{7,6},{8,7},{9,8},{10,9},{11,1... | collective-permute-start | bytes 786440 | tf_op jit(solution)/shard_map/ppermute | solution.py:406
  115.5 35.0 %collective-permute-start.20 = (f32[32,8,512]{2,1,0:T(8,128)S(1)}, f32[32,8,512]{2,1,0:T(8,128)S(1)}, u32[]{:S(2)}, u32[]{:S(2)}) collective-permute-start(f32[32,8,512]{2,1,0:T(8,128)S(1)} %get-tuple-element.38.refs_0_.refs_4_.v00), channel_id=1, source_target_pairs={{0,1},{1,2},{2,3},{3,4},{4,5},{5,6},{6,7},{7,8},{8,9},{9,10},{10,1... | collective-permute-start | bytes 1572872 | tf_op jit(solution)/shard_map/ppermute | solution.py:401
  115.5 35.1 %collective-permute-start.21 = (f32[32,8,512]{2,1,0:T(8,128)S(1)}, f32[32,8,512]{2,1,0:T(8,128)S(1)}, u32[]{:S(2)}, u32[]{:S(2)}) collective-permute-start(f32[32,8,512]{2,1,0:T(8,128)S(1)} %get-tuple-element.39.refs_1_.refs_5_.v01), channel_id=1, source_target_pairs={{0,1},{1,2},{2,3},{3,4},{4,5},{5,6},{6,7},{7,8},{8,9},{9,10},{10,1... | collective-permute-start | bytes 1572872 | tf_op jit(solution)/shard_map/ppermute | solution.py:401
  115.5 38.1 %collective-permute-start.22 = (f32[32,8,512]{2,1,0:T(8,128)S(1)}, f32[32,8,512]{2,1,0:T(8,128)S(1)}, u32[]{:S(2)}, u32[]{:S(2)}) collective-permute-start(f32[32,8,512]{2,1,0:T(8,128)S(1)} %get-tuple-element.40.refs_2_.refs_6_.v10), channel_id=1, source_target_pairs={{0,1},{1,2},{2,3},{3,4},{4,5},{5,6},{6,7},{7,8},{8,9},{9,10},{10,1... | collective-permute-start | bytes 1572872 | tf_op jit(solution)/shard_map/ppermute | solution.py:401
  117.6 18.1 %collective-permute-start.30 = (f32[32,8,256]{2,1,0:T(8,128)S(1)}, f32[32,8,256]{2,1,0:T(8,128)S(1)}, u32[]{:S(2)}, u32[]{:S(2)}) collective-permute-start(f32[32,8,256]{2,1,0:T(8,128)S(1)} %get-tuple-element.48), channel_id=1, source_target_pairs={{0,1},{1,2},{2,3},{3,4},{4,5},{5,6},{6,7},{7,8},{8,9},{9,10},{10,1... | collective-permute-start | bytes 786440 | tf_op jit(solution)/shard_map/ppermute | solution.py:401
  117.7 18.0 %collective-permute-start.31 = (f32[32,8,256]{2,1,0:T(8,128)S(1)}, f32[32,8,256]{2,1,0:T(8,128)S(1)}, u32[]{:S(2)}, u32[]{:S(2)}) collective-permute-start(f32[32,8,256]{2,1,0:T(8,128)S(1)} %get-tuple-element.48), channel_id=1, source_target_pairs={{1,0},{2,1},{3,2},{4,3},{5,4},{6,5},{7,6},{8,7},{9,8},{10,9},{11,1... | collective-permute-start | bytes 786440 | tf_op jit(solution)/shard_map/ppermute | solution.py:406
  136.1 7.9 %collective-permute-start.32 = (f32[32,8,256]{2,1,0:T(8,128)S(1)}, f32[32,8,256]{2,1,0:T(8,128)S(1)}, u32[]{:S(2)}, u32[]{:S(2)}) collective-permute-start(f32[32,8,256]{2,1,0:T(8,128)S(1)} %fusion.19), channel_id=1, source_target_pairs={{0,1},{1,2},{2,3},{3,4},{4,5},{5,6},{6,7},{7,8},{8,9},{9,10},{10,1... | collective-permute-start | bytes 786440 | tf_op jit(solution)/shard_map/ppermute | solution.py:401
  144.8 11.7 %collective-permute-start.34 = (f32[32,8,256]{2,1,0:T(8,128)S(1)}, f32[32,8,256]{2,1,0:T(8,128)S(1)}, u32[]{:S(2)}, u32[]{:S(2)}) collective-permute-start(f32[32,8,256]{2,1,0:T(8,128)S(1)} %fusion.24), channel_id=1, source_target_pairs={{0,1},{1,2},{2,3},{3,4},{4,5},{5,6},{6,7},{7,8},{8,9},{9,10},{10,1... | collective-permute-start | bytes 786440 | tf_op jit(solution)/shard_map/ppermute | solution.py:401
  144.9 12.5 %collective-permute-start.35 = (f32[32,8,256]{2,1,0:T(8,128)S(1)}, f32[32,8,256]{2,1,0:T(8,128)S(1)}, u32[]{:S(2)}, u32[]{:S(2)}) collective-permute-start(f32[32,8,256]{2,1,0:T(8,128)S(1)} %fusion.24), channel_id=1, source_target_pairs={{1,0},{2,1},{3,2},{4,3},{5,4},{6,5},{7,6},{8,7},{9,8},{10,9},{11,1... | collective-permute-start | bytes 786440 | tf_op jit(solution)/shard_map/ppermute | solution.py:406
  150.7 8.9 %collective-permute-start.24 = (f32[32,8,512]{2,1,0:T(8,128)S(1)}, f32[32,8,512]{2,1,0:T(8,128)S(1)}, u32[]{:S(2)}, u32[]{:S(2)}) collective-permute-start(f32[32,8,512]{2,1,0:T(8,128)S(1)} %get-tuple-element.38.refs_0_.refs_4_.v00), channel_id=1, source_target_pairs={{1,0},{2,1},{3,2},{4,3},{5,4},{6,5},{7,6},{8,7},{9,8},{10,9},{11,1... | collective-permute-start | bytes 1572872 | tf_op jit(solution)/shard_map/ppermute | solution.py:406
  153.7 11.6 %collective-permute-start.25 = (f32[32,8,512]{2,1,0:T(8,128)S(1)}, f32[32,8,512]{2,1,0:T(8,128)S(1)}, u32[]{:S(2)}, u32[]{:S(2)}) collective-permute-start(f32[32,8,512]{2,1,0:T(8,128)S(1)} %get-tuple-element.39.refs_1_.refs_5_.v01), channel_id=1, source_target_pairs={{1,0},{2,1},{3,2},{4,3},{5,4},{6,5},{7,6},{8,7},{9,8},{10,9},{11,1... | collective-permute-start | bytes 1572872 | tf_op jit(solution)/shard_map/ppermute | solution.py:406
  156.6 14.0 %collective-permute-start.26 = (f32[32,8,512]{2,1,0:T(8,128)S(1)}, f32[32,8,512]{2,1,0:T(8,128)S(1)}, u32[]{:S(2)}, u32[]{:S(2)}) collective-permute-start(f32[32,8,512]{2,1,0:T(8,128)S(1)} %get-tuple-element.40.refs_2_.refs_6_.v10), channel_id=1, source_target_pairs={{1,0},{2,1},{3,2},{4,3},{5,4},{6,5},{7,6},{8,7},{9,8},{10,9},{11,1... | collective-permute-start | bytes 1572872 | tf_op jit(solution)/shard_map/ppermute | solution.py:406
  157.4 18.7 %collective-permute-start.27 = (f32[32,8,512]{2,1,0:T(8,128)S(1)}, f32[32,8,512]{2,1,0:T(8,128)S(1)}, u32[]{:S(2)}, u32[]{:S(2)}) collective-permute-start(f32[32,8,512]{2,1,0:T(8,128)S(1)} %get-tuple-element.41.refs_3_.refs_7_.v11), channel_id=1, source_target_pairs={{1,0},{2,1},{3,2},{4,3},{5,4},{6,5},{7,6},{8,7},{9,8},{10,9},{11,1... | collective-permute-start | bytes 1572872 | tf_op jit(solution)/shard_map/ppermute | solution.py:406
  157.7 20.8 %collective-permute-start.36 = (f32[32,8,256]{2,1,0:T(8,128)S(1)}, f32[32,8,256]{2,1,0:T(8,128)S(1)}, u32[]{:S(2)}, u32[]{:S(2)}) collective-permute-start(f32[32,8,256]{2,1,0:T(8,128)S(1)} %fusion.29.c_own), channel_id=1, source_target_pairs={{0,1},{1,2},{2,3},{3,4},{4,5},{5,6},{6,7},{7,8},{8,9},{9,10},{10,1... | collective-permute-start | bytes 786440 | tf_op jit(solution)/shard_map/ppermute | solution.py:401
  159.6 19.4 %collective-permute-start.37 = (f32[32,8,256]{2,1,0:T(8,128)S(1)}, f32[32,8,256]{2,1,0:T(8,128)S(1)}, u32[]{:S(2)}, u32[]{:S(2)}) collective-permute-start(f32[32,8,256]{2,1,0:T(8,128)S(1)} %fusion.29.c_own), channel_id=1, source_target_pairs={{1,0},{2,1},{3,2},{4,3},{5,4},{6,5},{7,6},{8,7},{9,8},{10,9},{11,1... | collective-permute-start | bytes 786440 | tf_op jit(solution)/shard_map/ppermute | solution.py:406
  (8 other events, 66.5 us)
